TPU v7x, 512 devices: a whole 4x4x16 slice. The times are simulated.
512 devices in a mesh: rep: 4 (over x_hi, core), row: 32 (over x_lo, z), col: 4 (over y).
Axes of the slice: x: 4 (x_hi: 2, x_lo: 2; x = x_hi * 2 + x_lo), y: 4, z: 16, core: 2. Of those that a mesh axis runs over, the one named last changes fastest.
Arguments:
- spin_init: bfloat16 [256, 8192], P('rep', 'row'), may hold values from -1 to 1, as said below
- couplings: bfloat16 [32, 4, 64, 8192], P(None, 'col', None, 'row'), may hold values from -1 to 1, as said below
- flip_noise: float32 [10, 256, 8192], P(None, 'rep', 'row'), may hold values from 0 to 17, as said below
- colors: int32 [8192], P('row'), may hold values 0 or 1
- beta_steps: int32 [256], replicated, may hold values from 96 to 1024
- partners: int32 [256], replicated, may hold values from 0 to 255, as said below
- swap_noise: float32 [256], replicated, may hold values from 0 to 17, as said below
Outputs:
- spins_out: bfloat16 [256, 8192], P('rep', 'row')
- energies: float32 [256], P('rep')
Inputs may be any that keep to these rules, and one draw needn't show every extreme that they name: `spin_init`: every entry is -1 or +1. `couplings`: the 8192 x 8192 matrix is symmetric, zero on its diagonal, and every other entry is -1 or +1. `flip_noise`: independent exponential variates of mean one. `swap_noise`: independent exponential variates of mean one. Pairs slots: partners[partners[r]] = r and partners[r] != r for every slot.
All inputs are finite; a program needn't handle non-finite values. No bound on the sum of `colors` on one device may be relied on, other than what follows from the above.
Results may differ from a plain program's by a relative error of at most 0.001.
Values may be sent and summed in bfloat16 or wider, within the bound.
No kernel may reach another device: no remote copies, remote signals or barrier semaphores. Data moves between devices by JAX's collectives and lax.ppermute only.
A program may use at most 64 MiB of HBM per device.

v0:
```python
import math

import jax
import jax.numpy as jnp
from jax import lax
from jax.sharding import PartitionSpec as P

N = 8192
SWEEPS = 10


def joined_along(blocks, dim):
    blocks = jnp.moveaxis(blocks, 0, dim)
    dims = blocks.shape
    return blocks.reshape(*dims[:dim], dims[dim] * dims[dim + 1], *dims[dim + 2 :])


def copy_for_each(value, axis):
    length = lax.axis_size(axis)
    return lax.all_to_all(
        jnp.broadcast_to(value[None], (length, *value.shape)), axis, 0, 0, tiled=True
    )


def gathered_copies(value, axis, dim):
    return joined_along(copy_for_each(value, axis), dim)


def split_up(value, dim, length):
    dims = value.shape
    blocks = value.reshape(*dims[:dim], length, dims[dim] // length, *dims[dim + 1 :])
    return jnp.moveaxis(blocks, dim, 0)


def sent_and_summed(value, axis, dim):
    blocks = split_up(value, dim, lax.axis_size(axis))
    arrived = lax.all_to_all(blocks, axis, split_axis=0, concat_axis=0, tiled=True)
    return arrived.sum(axis=0)


def over_copies(value, axis):
    everything = copy_for_each(value, axis)
    return jnp.sum(everything, axis=0)


def metropolis(spin_state, fields, parity, color_part, noise_part, beta_col):
    values = spin_state.astype(jnp.float32)
    energy_cost = beta_col * (values * fields) * (1.0 / 16384.0)
    flipped = (color_part == parity)[None, :] & (energy_cost < noise_part)
    return jnp.where(flipped, -values, values).astype(jnp.bfloat16)


def partial_fields(strided, coupling_block):
    return jnp.dot(strided, coupling_block, preferred_element_type=jnp.float32)


def per_device(spin_init, couplings, flip_noise, colors, beta_steps, partners, swap_noise):
    rep_dev, row_width = spin_init.shape
    col_count = lax.axis_size("col")
    col_index = lax.axis_index("col")
    rep_index = lax.axis_index("rep")
    piece_size = row_width // col_count
    coupling_block = couplings.reshape(-1, row_width)
    beta_col = lax.dynamic_slice_in_dim(beta_steps, rep_index * rep_dev, rep_dev).astype(
        jnp.float32
    )[:, None]
    color_part = lax.dynamic_slice_in_dim(colors, col_index * piece_size, piece_size)
    noise_part = lax.dynamic_slice_in_dim(flip_noise, col_index * piece_size, piece_size, 2)

    def strided_of(spin_state):
        return gathered_copies(spin_state, "row", 1)

    def one_sweep(step_index, spin_state):
        terms = partial_fields(strided_of(spin_state), coupling_block)
        fields = sent_and_summed(terms, "col", 1)
        return metropolis(
            spin_state, fields, step_index % 2, color_part, noise_part[step_index], beta_col
        )

    start_pieces = lax.dynamic_slice_in_dim(spin_init, col_index * piece_size, piece_size, 1)
    final_pieces = lax.fori_loop(0, SWEEPS, one_sweep, start_pieces)
    strided = strided_of(final_pieces)
    final_rows = gathered_copies(final_pieces, "col", 1)
    every_spins = gathered_copies(final_rows, "rep", 0)
    final_partial = partial_fields(strided, coupling_block)
    row_values = final_rows.astype(jnp.float32)
    final_local = over_copies(final_partial, "col")
    total_sum = over_copies(jnp.sum(row_values * final_local, axis=1), "row")
    energy = -0.5 * total_sum
    every_energy = gathered_copies(energy, "rep", 0)
    slot_ids = rep_index * rep_dev + jnp.arange(rep_dev, dtype=jnp.int32)
    mate_ids = lax.dynamic_slice_in_dim(partners, rep_index * rep_dev, rep_dev)
    all_betas = beta_steps.astype(jnp.float32)
    mate_energy = every_energy[mate_ids]
    swap_gain = (
        (beta_col[:, 0] - all_betas[mate_ids])
        * (energy - mate_energy)
        * (1.0 / (64.0 * N * math.sqrt(N)))
    )
    accept = swap_gain + swap_noise[jnp.minimum(slot_ids, mate_ids)] > 0.0
    spins_out = jnp.where(accept[:, None], every_spins[mate_ids], final_rows)
    energies = jnp.where(accept, mate_energy, energy) * (1.0 / (N * math.sqrt(N)))
    return (spins_out, energies)


def solution(mesh):
    in_specs = (
        P("rep", "row"),
        P(None, "col", None, "row"),
        P(None, "rep", "row"),
        P("row"),
        P(),
        P(),
        P(),
    )
    out_specs = (P("rep", "row"), P("rep"))
    return jax.shard_map(
        per_device, mesh=mesh, in_specs=in_specs, out_specs=out_specs, check_vma=False
    )
```

profile of v0, /device:TPU:1, one launch (start us, length us, event | category | flops | bytes accessed | tf_op | source)
XLA Modules:
  0.0 473.6 jit_solution(16910285389802976583)
XLA Ops:
  3.2 1.5 copy.24
  5.5 362.3 %while.15 = (s32[]{:T(128)}, bf16[64,64]{1,0:T(8,128)(2,1)S(1)}, s32[64]{0:T(128)S(1)}, f32[64,1]{0,1:T(1,128)S(1)}, bf16[2048,256]{0,1:T(8,128)(2,1)S(1)}, /*in...) while((s32[]{:T(128)}, bf16[64,64]{1,0:T(8,128)(2,1)S(1)}, ...), condition=%wide.region_2.3_spmd, body=%wide.region_0.2_spmd.sunk | while | flops 67158080 | bytes 5251975 | solution.py:81
  5.6 1.1 reshape.128
  6.7 16.9 %all-to-all-start = ((bf16[32,2,2048]{2,1,0:T(2,128)(2,1)}), bf16[32,2,2048]{2,1,0:T(2,128)(2,1)S(1)}, u32[]{:S(2)}, u32[]{:S(2)}) async-start(bf16[32,2,2048]{2,1,0:T(2,128)(2,1)} %reshape.128), calls=%async_computation | async-start | bytes 524288 | tf_op jit(solution)/shard_map/while/body/eval_jaxpr/all_to_all | solution.py:20
  23.6 20.0 %all-to-all-done = bf16[32,2,2048]{2,1,0:T(2,128)(2,1)S(1)} async-done(((bf16[32,2,2048]{2,1,0:T(2,128)(2,1)}), bf16[32,2,2048]{2,1,0:T(2,128)(2,1)S(1)}, u32[]{:S(2)}, u32[]{:S(2)}) %all-to-all-start) | async-done | bytes 262176 | tf_op jit(solution)/shard_map/while/body/eval_jaxpr/all_to_all | solution.py:20
  46.2 4.2 all-to-all-start.1
  50.4 4.5 all-to-all-done.1
  56.6 1.1 reshape.128
  57.7 5.0 %all-to-all-start = ((bf16[32,2,2048]{2,1,0:T(2,128)(2,1)}), bf16[32,2,2048]{2,1,0:T(2,128)(2,1)S(1)}, u32[]{:S(2)}, u32[]{:S(2)}) async-start(bf16[32,2,2048]{2,1,0:T(2,128)(2,1)} %reshape.128), calls=%async_computation | async-start | bytes 524288 | tf_op jit(solution)/shard_map/while/body/eval_jaxpr/all_to_all | solution.py:20
  62.7 17.5 %all-to-all-done = bf16[32,2,2048]{2,1,0:T(2,128)(2,1)S(1)} async-done(((bf16[32,2,2048]{2,1,0:T(2,128)(2,1)}), bf16[32,2,2048]{2,1,0:T(2,128)(2,1)S(1)}, u32[]{:S(2)}, u32[]{:S(2)}) %all-to-all-start) | async-done | bytes 262176 | tf_op jit(solution)/shard_map/while/body/eval_jaxpr/all_to_all | solution.py:20
  82.7 3.3 all-to-all-start.1
  86.0 4.4 all-to-all-done.1
  92.2 1.1 reshape.128
  93.3 5.7 %all-to-all-start = ((bf16[32,2,2048]{2,1,0:T(2,128)(2,1)}), bf16[32,2,2048]{2,1,0:T(2,128)(2,1)S(1)}, u32[]{:S(2)}, u32[]{:S(2)}) async-start(bf16[32,2,2048]{2,1,0:T(2,128)(2,1)} %reshape.128), calls=%async_computation | async-start | bytes 524288 | tf_op jit(solution)/shard_map/while/body/eval_jaxpr/all_to_all | solution.py:20
  98.9 17.1 %all-to-all-done = bf16[32,2,2048]{2,1,0:T(2,128)(2,1)S(1)} async-done(((bf16[32,2,2048]{2,1,0:T(2,128)(2,1)}), bf16[32,2,2048]{2,1,0:T(2,128)(2,1)S(1)}, u32[]{:S(2)}, u32[]{:S(2)}) %all-to-all-start) | async-done | bytes 262176 | tf_op jit(solution)/shard_map/while/body/eval_jaxpr/all_to_all | solution.py:20
  118.6 3.3 all-to-all-start.1
  122.0 4.4 all-to-all-done.1
  128.1 1.1 reshape.128
  129.2 3.9 all-to-all-start
  133.0 17.1 %all-to-all-done = bf16[32,2,2048]{2,1,0:T(2,128)(2,1)S(1)} async-done(((bf16[32,2,2048]{2,1,0:T(2,128)(2,1)}), bf16[32,2,2048]{2,1,0:T(2,128)(2,1)S(1)}, u32[]{:S(2)}, u32[]{:S(2)}) %all-to-all-start) | async-done | bytes 262176 | tf_op jit(solution)/shard_map/while/body/eval_jaxpr/all_to_all | solution.py:20
  152.7 3.3 all-to-all-start.1
  156.0 4.4 all-to-all-done.1
  162.1 1.1 reshape.128
  163.2 3.9 all-to-all-start
  167.1 17.1 %all-to-all-done = bf16[32,2,2048]{2,1,0:T(2,128)(2,1)S(1)} async-done(((bf16[32,2,2048]{2,1,0:T(2,128)(2,1)}), bf16[32,2,2048]{2,1,0:T(2,128)(2,1)S(1)}, u32[]{:S(2)}, u32[]{:S(2)}) %all-to-all-start) | async-done | bytes 262176 | tf_op jit(solution)/shard_map/while/body/eval_jaxpr/all_to_all | solution.py:20
  186.8 3.3 all-to-all-start.1
  190.1 4.5 all-to-all-done.1
  196.2 1.1 reshape.128
  197.3 3.9 all-to-all-start
  201.2 17.2 %all-to-all-done = bf16[32,2,2048]{2,1,0:T(2,128)(2,1)S(1)} async-done(((bf16[32,2,2048]{2,1,0:T(2,128)(2,1)}), bf16[32,2,2048]{2,1,0:T(2,128)(2,1)S(1)}, u32[]{:S(2)}, u32[]{:S(2)}) %all-to-all-start) | async-done | bytes 262176 | tf_op jit(solution)/shard_map/while/body/eval_jaxpr/all_to_all | solution.py:20
  221.0 3.3 all-to-all-start.1
  224.3 4.7 all-to-all-done.1
  230.7 1.1 reshape.128
  231.8 3.9 all-to-all-start
  235.7 17.1 %all-to-all-done = bf16[32,2,2048]{2,1,0:T(2,128)(2,1)S(1)} async-done(((bf16[32,2,2048]{2,1,0:T(2,128)(2,1)}), bf16[32,2,2048]{2,1,0:T(2,128)(2,1)S(1)}, u32[]{:S(2)}, u32[]{:S(2)}) %all-to-all-start) | async-done | bytes 262176 | tf_op jit(solution)/shard_map/while/body/eval_jaxpr/all_to_all | solution.py:20
  255.4 3.3 all-to-all-start.1
  258.7 4.4 all-to-all-done.1
  264.8 1.1 reshape.128
  265.9 3.9 all-to-all-start
  269.8 17.1 %all-to-all-done = bf16[32,2,2048]{2,1,0:T(2,128)(2,1)S(1)} async-done(((bf16[32,2,2048]{2,1,0:T(2,128)(2,1)}), bf16[32,2,2048]{2,1,0:T(2,128)(2,1)S(1)}, u32[]{:S(2)}, u32[]{:S(2)}) %all-to-all-start) | async-done | bytes 262176 | tf_op jit(solution)/shard_map/while/body/eval_jaxpr/all_to_all | solution.py:20
  289.4 3.3 all-to-all-start.1
  292.7 4.7 all-to-all-done.1
  299.2 1.1 reshape.128
  300.3 3.9 all-to-all-start
  304.1 17.1 %all-to-all-done = bf16[32,2,2048]{2,1,0:T(2,128)(2,1)S(1)} async-done(((bf16[32,2,2048]{2,1,0:T(2,128)(2,1)}), bf16[32,2,2048]{2,1,0:T(2,128)(2,1)S(1)}, u32[]{:S(2)}, u32[]{:S(2)}) %all-to-all-start) | async-done | bytes 262176 | tf_op jit(solution)/shard_map/while/body/eval_jaxpr/all_to_all | solution.py:20
  323.8 3.3 all-to-all-start.1
  327.1 4.7 all-to-all-done.1
  334.6 3.9 all-to-all-start
  338.5 17.1 %all-to-all-done = bf16[32,2,2048]{2,1,0:T(2,128)(2,1)S(1)} async-done(((bf16[32,2,2048]{2,1,0:T(2,128)(2,1)}), bf16[32,2,2048]{2,1,0:T(2,128)(2,1)S(1)}, u32[]{:S(2)}, u32[]{:S(2)}) %all-to-all-start) | async-done | bytes 262176 | tf_op jit(solution)/shard_map/while/body/eval_jaxpr/all_to_all | solution.py:20
  358.2 3.3 all-to-all-start.1
  361.5 4.7 all-to-all-done.1
  367.9 1.1 reshape.121
  369.0 3.9 all-to-all-start.3
  373.6 16.4 %all-to-all-done.3 = bf16[32,2,2048]{2,1,0:T(2,128)(2,1)S(1)} async-done(((bf16[32,2,2048]{2,1,0:T(2,128)(2,1)}), bf16[32,2,2048]{2,1,0:T(2,128)(2,1)S(1)}, u32[]{:S(2)}, u32[]{:S(2)}) %all-to-all-start.3) | async-done | bytes 262176 | tf_op jit(solution)/shard_map/all_to_all | solution.py:20
  390.0 3.3 all-to-all-start.2
  395.1 2.4 all-to-all-done.2
  398.2 3.5 all-to-all-start.4
  402.0 5.4 %all-to-all-done.4 = f32[4,64,256]{2,1,0:T(8,128)S(1)} async-done(((f32[4,64,256]{2,1,0:T(8,128)}), f32[4,64,256]{2,1,0:T(8,128)S(1)}, u32[]{:S(2)}, u32[]{:S(2)}) %all-to-all-start.4) | async-done | bytes 262176 | tf_op jit(solution)/shard_map/all_to_all | solution.py:20
  408.7 3.8 all-to-all-start.5
  412.7 12.0 %all-to-all-done.5 = f32[32,1,64]{2,1,0:T(1,128)S(1)} async-done(((f32[32,1,64]{2,1,0:T(1,128)}), f32[32,1,64]{2,1,0:T(1,128)S(1)}, u32[]{:S(2)}, u32[]{:S(2)}) %all-to-all-start.5) | async-done | bytes 8224 | tf_op jit(solution)/shard_map/all_to_all | solution.py:20
  425.3 30.6 %all-to-all-start.7 = ((bf16[4,64,256]{2,1,0:T(8,128)(2,1)}), bf16[4,64,256]{2,1,0:T(8,128)(2,1)S(1)}, u32[]{:S(2)}, u32[]{:S(2)}) async-start(bf16[4,64,256]{2,1,0:T(8,128)(2,1)} %broadcast_in_dim.89), calls=%async_computation.7 | async-start | bytes 262144 | tf_op jit(solution)/shard_map/all_to_all | solution.py:20
  455.9 5.0 %all-to-all-done.7 = bf16[4,64,256]{2,1,0:T(8,128)(2,1)S(1)} async-done(((bf16[4,64,256]{2,1,0:T(8,128)(2,1)}), bf16[4,64,256]{2,1,0:T(8,128)(2,1)S(1)}, u32[]{:S(2)}, u32[]{:S(2)}) %all-to-all-start.7) | async-done | bytes 131104 | tf_op jit(solution)/shard_map/all_to_all | solution.py:20
  461.5 4.2 all-to-all-start.6
  468.0 2.2 all-to-all-done.6
  (171 shorter events, 58.6 us)
Async XLA Ops:
  0.6 1.1 copy-start
  1.7 0.8 copy-start.3
  2.5 0.7 copy-start.6
  4.7 0.7 copy-start.4
  6.7 36.9 %all-to-all-start = ((bf16[32,2,2048]{2,1,0:T(2,128)(2,1)}), bf16[32,2,2048]{2,1,0:T(2,128)(2,1)S(1)}, u32[]{:S(2)}, u32[]{:S(2)}) async-start(bf16[32,2,2048]{2,1,0:T(2,128)(2,1)} %reshape.128), calls=%async_computation | async-start | bytes 524288 | tf_op jit(solution)/shard_map/while/body/eval_jaxpr/all_to_all | solution.py:20
  46.2 8.7 %all-to-all-start.1 = ((f32[4,1,4096]{2,1,0:T(1,128)}), f32[4,1,4096]{2,1,0:T(1,128)S(1)}, u32[]{:S(2)}, u32[]{:S(2)}) async-start(f32[4,1,4096]{2,1,0:T(1,128)} %reshape.131), calls=%async_computation.1 | async-start | bytes 131072 | tf_op jit(solution)/shard_map/while/body/eval_jaxpr/all_to_all | solution.py:37
  57.7 22.5 %all-to-all-start = ((bf16[32,2,2048]{2,1,0:T(2,128)(2,1)}), bf16[32,2,2048]{2,1,0:T(2,128)(2,1)S(1)}, u32[]{:S(2)}, u32[]{:S(2)}) async-start(bf16[32,2,2048]{2,1,0:T(2,128)(2,1)} %reshape.128), calls=%async_computation | async-start | bytes 524288 | tf_op jit(solution)/shard_map/while/body/eval_jaxpr/all_to_all | solution.py:20
  82.7 7.7 %all-to-all-start.1 = ((f32[4,1,4096]{2,1,0:T(1,128)}), f32[4,1,4096]{2,1,0:T(1,128)S(1)}, u32[]{:S(2)}, u32[]{:S(2)}) async-start(f32[4,1,4096]{2,1,0:T(1,128)} %reshape.131), calls=%async_computation.1 | async-start | bytes 131072 | tf_op jit(solution)/shard_map/while/body/eval_jaxpr/all_to_all | solution.py:37
  93.3 22.8 %all-to-all-start = ((bf16[32,2,2048]{2,1,0:T(2,128)(2,1)}), bf16[32,2,2048]{2,1,0:T(2,128)(2,1)S(1)}, u32[]{:S(2)}, u32[]{:S(2)}) async-start(bf16[32,2,2048]{2,1,0:T(2,128)(2,1)} %reshape.128), calls=%async_computation | async-start | bytes 524288 | tf_op jit(solution)/shard_map/while/body/eval_jaxpr/all_to_all | solution.py:20
  118.6 7.7 %all-to-all-start.1 = ((f32[4,1,4096]{2,1,0:T(1,128)}), f32[4,1,4096]{2,1,0:T(1,128)S(1)}, u32[]{:S(2)}, u32[]{:S(2)}) async-start(f32[4,1,4096]{2,1,0:T(1,128)} %reshape.131), calls=%async_computation.1 | async-start | bytes 131072 | tf_op jit(solution)/shard_map/while/body/eval_jaxpr/all_to_all | solution.py:37
  129.2 21.0 %all-to-all-start = ((bf16[32,2,2048]{2,1,0:T(2,128)(2,1)}), bf16[32,2,2048]{2,1,0:T(2,128)(2,1)S(1)}, u32[]{:S(2)}, u32[]{:S(2)}) async-start(bf16[32,2,2048]{2,1,0:T(2,128)(2,1)} %reshape.128), calls=%async_computation | async-start | bytes 524288 | tf_op jit(solution)/shard_map/while/body/eval_jaxpr/all_to_all | solution.py:20
  152.7 7.7 %all-to-all-start.1 = ((f32[4,1,4096]{2,1,0:T(1,128)}), f32[4,1,4096]{2,1,0:T(1,128)S(1)}, u32[]{:S(2)}, u32[]{:S(2)}) async-start(f32[4,1,4096]{2,1,0:T(1,128)} %reshape.131), calls=%async_computation.1 | async-start | bytes 131072 | tf_op jit(solution)/shard_map/while/body/eval_jaxpr/all_to_all | solution.py:37
  163.2 21.0 %all-to-all-start = ((bf16[32,2,2048]{2,1,0:T(2,128)(2,1)}), bf16[32,2,2048]{2,1,0:T(2,128)(2,1)S(1)}, u32[]{:S(2)}, u32[]{:S(2)}) async-start(bf16[32,2,2048]{2,1,0:T(2,128)(2,1)} %reshape.128), calls=%async_computation | async-start | bytes 524288 | tf_op jit(solution)/shard_map/while/body/eval_jaxpr/all_to_all | solution.py:20
  186.8 7.8 %all-to-all-start.1 = ((f32[4,1,4096]{2,1,0:T(1,128)}), f32[4,1,4096]{2,1,0:T(1,128)S(1)}, u32[]{:S(2)}, u32[]{:S(2)}) async-start(f32[4,1,4096]{2,1,0:T(1,128)} %reshape.131), calls=%async_computation.1 | async-start | bytes 131072 | tf_op jit(solution)/shard_map/while/body/eval_jaxpr/all_to_all | solution.py:37
  197.3 21.1 %all-to-all-start = ((bf16[32,2,2048]{2,1,0:T(2,128)(2,1)}), bf16[32,2,2048]{2,1,0:T(2,128)(2,1)S(1)}, u32[]{:S(2)}, u32[]{:S(2)}) async-start(bf16[32,2,2048]{2,1,0:T(2,128)(2,1)} %reshape.128), calls=%async_computation | async-start | bytes 524288 | tf_op jit(solution)/shard_map/while/body/eval_jaxpr/all_to_all | solution.py:20
  221.0 8.0 %all-to-all-start.1 = ((f32[4,1,4096]{2,1,0:T(1,128)}), f32[4,1,4096]{2,1,0:T(1,128)S(1)}, u32[]{:S(2)}, u32[]{:S(2)}) async-start(f32[4,1,4096]{2,1,0:T(1,128)} %reshape.131), calls=%async_computation.1 | async-start | bytes 131072 | tf_op jit(solution)/shard_map/while/body/eval_jaxpr/all_to_all | solution.py:37
  231.8 21.0 %all-to-all-start = ((bf16[32,2,2048]{2,1,0:T(2,128)(2,1)}), bf16[32,2,2048]{2,1,0:T(2,128)(2,1)S(1)}, u32[]{:S(2)}, u32[]{:S(2)}) async-start(bf16[32,2,2048]{2,1,0:T(2,128)(2,1)} %reshape.128), calls=%async_computation | async-start | bytes 524288 | tf_op jit(solution)/shard_map/while/body/eval_jaxpr/all_to_all | solution.py:20
  255.4 7.7 %all-to-all-start.1 = ((f32[4,1,4096]{2,1,0:T(1,128)}), f32[4,1,4096]{2,1,0:T(1,128)S(1)}, u32[]{:S(2)}, u32[]{:S(2)}) async-start(f32[4,1,4096]{2,1,0:T(1,128)} %reshape.131), calls=%async_computation.1 | async-start | bytes 131072 | tf_op jit(solution)/shard_map/while/body/eval_jaxpr/all_to_all | solution.py:37
  265.9 21.0 %all-to-all-start = ((bf16[32,2,2048]{2,1,0:T(2,128)(2,1)}), bf16[32,2,2048]{2,1,0:T(2,128)(2,1)S(1)}, u32[]{:S(2)}, u32[]{:S(2)}) async-start(bf16[32,2,2048]{2,1,0:T(2,128)(2,1)} %reshape.128), calls=%async_computation | async-start | bytes 524288 | tf_op jit(solution)/shard_map/while/body/eval_jaxpr/all_to_all | solution.py:20
  289.4 8.0 %all-to-all-start.1 = ((f32[4,1,4096]{2,1,0:T(1,128)}), f32[4,1,4096]{2,1,0:T(1,128)S(1)}, u32[]{:S(2)}, u32[]{:S(2)}) async-start(f32[4,1,4096]{2,1,0:T(1,128)} %reshape.131), calls=%async_computation.1 | async-start | bytes 131072 | tf_op jit(solution)/shard_map/while/body/eval_jaxpr/all_to_all | solution.py:37
  300.3 21.0 %all-to-all-start = ((bf16[32,2,2048]{2,1,0:T(2,128)(2,1)}), bf16[32,2,2048]{2,1,0:T(2,128)(2,1)S(1)}, u32[]{:S(2)}, u32[]{:S(2)}) async-start(bf16[32,2,2048]{2,1,0:T(2,128)(2,1)} %reshape.128), calls=%async_computation | async-start | bytes 524288 | tf_op jit(solution)/shard_map/while/body/eval_jaxpr/all_to_all | solution.py:20
  323.8 8.0 %all-to-all-start.1 = ((f32[4,1,4096]{2,1,0:T(1,128)}), f32[4,1,4096]{2,1,0:T(1,128)S(1)}, u32[]{:S(2)}, u32[]{:S(2)}) async-start(f32[4,1,4096]{2,1,0:T(1,128)} %reshape.131), calls=%async_computation.1 | async-start | bytes 131072 | tf_op jit(solution)/shard_map/while/body/eval_jaxpr/all_to_all | solution.py:37
  334.6 21.0 %all-to-all-start = ((bf16[32,2,2048]{2,1,0:T(2,128)(2,1)}), bf16[32,2,2048]{2,1,0:T(2,128)(2,1)S(1)}, u32[]{:S(2)}, u32[]{:S(2)}) async-start(bf16[32,2,2048]{2,1,0:T(2,128)(2,1)} %reshape.128), calls=%async_computation | async-start | bytes 524288 | tf_op jit(solution)/shard_map/while/body/eval_jaxpr/all_to_all | solution.py:20
  358.2 8.0 %all-to-all-start.1 = ((f32[4,1,4096]{2,1,0:T(1,128)}), f32[4,1,4096]{2,1,0:T(1,128)S(1)}, u32[]{:S(2)}, u32[]{:S(2)}) async-start(f32[4,1,4096]{2,1,0:T(1,128)} %reshape.131), calls=%async_computation.1 | async-start | bytes 131072 | tf_op jit(solution)/shard_map/while/body/eval_jaxpr/all_to_all | solution.py:37
  369.0 21.0 %all-to-all-start.3 = ((bf16[32,2,2048]{2,1,0:T(2,128)(2,1)}), bf16[32,2,2048]{2,1,0:T(2,128)(2,1)S(1)}, u32[]{:S(2)}, u32[]{:S(2)}) async-start(bf16[32,2,2048]{2,1,0:T(2,128)(2,1)} %reshape.121), calls=%async_computation.3 | async-start | bytes 524288 | tf_op jit(solution)/shard_map/all_to_all | solution.py:20
  390.0 7.5 %all-to-all-start.2 = ((bf16[4,2,2048]{2,1,0:T(2,128)(2,1)}), bf16[4,2,2048]{2,1,0:T(2,128)(2,1)S(1)}, u32[]{:S(2)}, u32[]{:S(2)}) async-start(bf16[4,2,2048]{2,1,0:T(2,128)(2,1)} %reshape.119), calls=%async_computation.2 | async-start | bytes 65536 | tf_op jit(solution)/shard_map/all_to_all | solution.py:20
  393.6 1.2 copy-start.2
  398.2 3.5 copy-start.5
  398.2 9.1 %all-to-all-start.4 = ((f32[4,64,256]{2,1,0:T(8,128)}), f32[4,64,256]{2,1,0:T(8,128)S(1)}, u32[]{:S(2)}, u32[]{:S(2)}) async-start(f32[4,64,256]{2,1,0:T(8,128)} %broadcast_in_dim.83), calls=%async_computation.4 | async-start | bytes 524288 | tf_op jit(solution)/shard_map/all_to_all | solution.py:20
  408.7 16.0 %all-to-all-start.5 = ((f32[32,1,64]{2,1,0:T(1,128)}), f32[32,1,64]{2,1,0:T(1,128)S(1)}, u32[]{:S(2)}, u32[]{:S(2)}) async-start(f32[32,1,64]{2,1,0:T(1,128)} %broadcast_in_dim.84), calls=%async_computation.5 | async-start | bytes 32768 | tf_op jit(solution)/shard_map/all_to_all | solution.py:20
  425.3 35.6 %all-to-all-start.7 = ((bf16[4,64,256]{2,1,0:T(8,128)(2,1)}), bf16[4,64,256]{2,1,0:T(8,128)(2,1)S(1)}, u32[]{:S(2)}, u32[]{:S(2)}) async-start(bf16[4,64,256]{2,1,0:T(8,128)(2,1)} %broadcast_in_dim.89), calls=%async_computation.7 | async-start | bytes 262144 | tf_op jit(solution)/shard_map/all_to_all | solution.py:20
  461.5 8.8 %all-to-all-start.6 = ((f32[4,1,64]{2,1,0:T(1,128)}), f32[4,1,64]{2,1,0:T(1,128)S(1)}, u32[]{:S(2)}, u32[]{:S(2)}) async-start(f32[4,1,64]{2,1,0:T(1,128)} %broadcast_in_dim.85), calls=%async_computation.6 | async-start | bytes 4096 | tf_op jit(solution)/shard_map/all_to_all | solution.py:20
  465.7 0.8 copy-start.1
where the time goes:
time: 476 us; the launch traced here: 474 us
  waiting for transfers between devices  263 us (55%)
  starting transfers between devices  138 us (29%)
  local copies, waits for them, and re-layouts  52.5 us (11%)
  other arithmetic  12 us (3%)
  matrix products  6.57 us (1%)
    all_to_all x16, waiting for transfers between devices, copy_for_each(): lax.all_to_all(jnp.broadcast_to(value[None], (length, *value.shape)), axi...  218 us
    all_to_all x16, starting transfers between devices, copy_for_each(): lax.all_to_all(jnp.broadcast_to(value[None], (length, *value.shape)), axi...  104 us
    all_to_all x10, waiting for transfers between devices, sent_and_summed(): lax.all_to_all(blocks, axis, split_axis=0, concat_axis=0, tiled=True)  45.5 us
    all_to_all x10, starting transfers between devices, sent_and_summed(): lax.all_to_all(blocks, axis, split_axis=0, concat_axis=0, tiled=True)  33.7 us
    while x40, local copies, waits for them, and re-layouts  23.4 us
  transfers between devices with their start and end apart: 26, of which 26 were waited for; matrix products, arithmetic and copies ran while one was open for 1% of the time, Pallas kernels for 0%

commit v1 on v0

v1 whole, which is shorter than its diff:
```python
import math

import jax
import jax.numpy as jnp
from jax import lax
from jax.sharding import Mesh, PartitionSpec as P

N = 8192
SWEEPS = 10
NEVER = -3.0e38

GROUP = ("xh", "core")
PLANE = ("xl", "y")
LAYER = ("xh", "core", "xl", "y")


def sent_to_all(value, axes):
    length = lax.axis_size(axes)
    return lax.all_to_all(
        jnp.broadcast_to(value[None], (length, *value.shape)), axes, 0, 0, tiled=True
    )


def per_device(spin_init, couplings, flip_noise, colors, beta_steps, partners, swap_noise):
    rep_dev, row_width = spin_init.shape
    n_xl = lax.axis_size("xl")
    n_y = lax.axis_size("y")
    n_z = lax.axis_size("z")
    n_core = lax.axis_size("core")
    y_index = lax.axis_index("y")
    core_index = lax.axis_index("core")
    rep_index = lax.axis_index(GROUP)
    share = rep_dev // (n_xl * n_y)
    piece = row_width // n_y
    width = n_xl * row_width
    own_block = couplings.reshape(-1, row_width)

    core_part = lax.dynamic_slice_in_dim(
        couplings.reshape(n_core, -1, row_width), core_index, 1, 0
    )[0]
    gathered = lax.all_gather(core_part, ("core", *PLANE))
    layer_block = (
        gathered.reshape(n_core, n_xl, n_y, n_z, piece, row_width)
        .transpose(3, 0, 2, 4, 1, 5)
        .reshape(N, width)
    )

    start_piece = lax.dynamic_slice_in_dim(spin_init, y_index * piece, piece, 1)
    start_rows = sent_to_all(start_piece, ("xl", "z"))
    start_rows = start_rows.transpose(1, 0, 2).reshape(rep_dev, -1)
    partial = jnp.dot(start_rows, own_block, preferred_element_type=jnp.float32)
    partial = lax.all_to_all(
        partial.reshape(n_xl * n_y, share, row_width), PLANE, 0, 0, tiled=True
    )
    fields = partial.reshape(n_xl, n_y, share, row_width).sum(axis=1)
    fields = fields.transpose(1, 0, 2).reshape(share, width)

    steps = jnp.arange(SWEEPS, dtype=jnp.int32)[:, None, None]
    limits = jnp.where(colors[None, None, :] == steps % 2, flip_noise, NEVER)
    both = jnp.concatenate([spin_init.astype(jnp.float32)[None], limits], axis=0)
    both = both.reshape(SWEEPS + 1, n_xl, n_y, share, row_width)
    both = lax.dynamic_index_in_dim(both, y_index, 2, keepdims=False)
    both = lax.all_to_all(both.transpose(1, 0, 2, 3), "xl", 0, 0, tiled=True)
    both = both.transpose(1, 2, 0, 3).reshape(SWEEPS + 1, share, width)
    spins = both[0]
    limits = both[1:]
    first_slot = rep_index * rep_dev + lax.axis_index(PLANE) * share
    beta_col = lax.dynamic_slice_in_dim(beta_steps, first_slot, share).astype(jnp.float32)
    beta_col = beta_col[:, None] * (1.0 / 16384.0)

    def metropolis(spins, fields, limit):
        energy_cost = beta_col * (spins * fields)
        return jnp.where(energy_cost < limit, -spins, spins)

    def layer_fields(spins):
        rows = sent_to_all(spins.astype(jnp.bfloat16), "z")
        rows = rows.transpose(1, 0, 2).reshape(share, N)
        return jnp.dot(rows, layer_block, preferred_element_type=jnp.float32)

    spins = metropolis(spins, fields, limits[0])
    for step in range(1, SWEEPS):
        spins = metropolis(spins, layer_fields(spins), limits[step])

    blocks = spins.astype(jnp.bfloat16).reshape(share, n_xl, row_width).transpose(1, 0, 2)
    blocks = jnp.broadcast_to(
        blocks[None, :, None], (lax.axis_size(GROUP), n_xl, n_y, share, row_width)
    ).reshape(-1, share, row_width)
    every_spins = lax.all_to_all(blocks, LAYER, 0, 0, tiled=True).reshape(-1, row_width)

    layer_sum = jnp.sum(spins * layer_fields(spins), axis=1)
    layer_sum = jnp.pad(layer_sum[None], ((0, 0), (0, 128 - share)))
    energy = -0.5 * sent_to_all(layer_sum, "z").sum(axis=0)
    every_energy = sent_to_all(energy, LAYER)[:, 0, :share].reshape(-1)

    slot_ids = rep_index * rep_dev + jnp.arange(rep_dev, dtype=jnp.int32)
    mate_ids = lax.dynamic_slice_in_dim(partners, rep_index * rep_dev, rep_dev)
    all_ids = jnp.arange(every_energy.shape[0], dtype=jnp.int32)[None, :]

    def picked(table, ids):
        return jnp.sum(jnp.where(ids[:, None] == all_ids, table[None, :], 0.0), axis=1)

    all_betas = beta_steps.astype(jnp.float32)
    own_energy = picked(every_energy, slot_ids)
    mate_energy = picked(every_energy, mate_ids)
    swap_gain = (
        (picked(all_betas, slot_ids) - picked(all_betas, mate_ids))
        * (own_energy - mate_energy)
        * (1.0 / (64.0 * N * math.sqrt(N)))
    )
    accept = swap_gain + picked(swap_noise, jnp.minimum(slot_ids, mate_ids)) > 0.0
    source = jnp.where(accept, mate_ids, slot_ids)
    chosen = (source[:, None] == all_ids).astype(jnp.bfloat16)
    spins_out = jnp.dot(chosen, every_spins, preferred_element_type=jnp.float32)
    energies = jnp.where(accept, mate_energy, own_energy) * (1.0 / (N * math.sqrt(N)))
    return (spins_out.astype(jnp.bfloat16), energies)


def solution(mesh):
    fine = Mesh(mesh.devices.reshape(2, 2, 2, 16, 4), ("xh", "core", "xl", "z", "y"))
    rep, row, col = ("xh", "core"), ("xl", "z"), "y"
    in_specs = (
        P(rep, row),
        P(None, col, None, row),
        P(None, rep, row),
        P(row),
        P(),
        P(),
        P(),
    )
    out_specs = (P(rep, row), P(rep))
    return jax.shard_map(
        per_device, mesh=fine, in_specs=in_specs, out_specs=out_specs, check_vma=False
    )
```

time: 476 us -> 342 us (0.72)
  waiting for transfers between devices: 263 us -> 69 us
  blocking collectives: 0 us -> 141 us
  starting transfers between devices: 138 us -> 57.2 us
  local copies, waits for them, and re-layouts: 52.5 us -> 33.4 us
  matrix products: 6.57 us -> 20.3 us
  between operations: 0.82 us -> 14.3 us
  other arithmetic: 12 us -> 5.25 us
    all_to_all x26 -> x8, waiting for transfers between devices: 263 us -> 62.1 us  [the longest x5 45.7 us: sent_to_all(): lax.all_to_all(jnp.broadcast_to(value[None], (length, *value.shape)), axe...]
    all_to_all x0 -> x8, blocking collectives: none -> 141 us  [sent_to_all(): lax.all_to_all(jnp.broadcast_to(value[None], (length, *value.shape)), axe...]
    all_to_all x26 -> x8, starting transfers between devices: 138 us -> 57.1 us  [the longest x5 45.5 us: sent_to_all(): lax.all_to_all(jnp.broadcast_to(value[None], (length, *value.shape)), axe...]
    while x41 -> x0, local copies, waits for them, and re-layouts: 24.9 us -> none
    dot_general x11 -> x12, matrix products: 6.57 us -> 20.3 us  [the longest x10 18.6 us: layer_fields(): return jnp.dot(rows, layer_block, preferred_element_type=jnp.float32)]
    transpose x11 -> x2, local copies, waits for them, and re-layouts: 3.79 us -> 16.7 us  [the longest x1 16.4 us: per_device(): layer_block = gathered.reshape(n_core, n_xl, n_y, n_z, piece, row_width)....]
    all_to_all x11 -> x0, other arithmetic: 8.78 us -> none  [the longest x10 8.12 us: sent_and_summed(): lax.all_to_all(blocks, axis, split_axis=0, concat_axis=0, tiled=True)]
    all_gather x0 -> x1, waiting for transfers between devices: none -> 6.97 us  [per_device(): gathered = lax.all_gather(core_part, ('core', *PLANE))]
  transfers between devices with their start and end apart: 26 -> 9, of which waited for: 26 -> 8; matrix products, arithmetic and copies ran while one was open for 1% -> 10% of each run, Pallas kernels for 0% -> 0%
where the time goes in v1:
time: 342 us; the launch traced here: 341 us
  blocking collectives  141 us (41%)
  waiting for transfers between devices  69 us (20%)
  starting transfers between devices  57.2 us (17%)
  local copies, waits for them, and re-layouts  33.4 us (10%)
  matrix products  20.3 us (6%)
  between operations  14.3 us (4%)
  other arithmetic  5.25 us (2%)
    all_to_all x8, blocking collectives, sent_to_all(): lax.all_to_all(jnp.broadcast_to(value[None], (length, *value.shape)), axe...  141 us
    all_to_all x5, waiting for transfers between devices, sent_to_all(): lax.all_to_all(jnp.broadcast_to(value[None], (length, *value.shape)), axe...  45.7 us
    all_to_all x5, starting transfers between devices, sent_to_all(): lax.all_to_all(jnp.broadcast_to(value[None], (length, *value.shape)), axe...  45.5 us
    dot_general x10, matrix products, layer_fields(): return jnp.dot(rows, layer_block, preferred_element_type=jnp.float32)  18.6 us
    transpose x1, local copies, waits for them, and re-layouts, per_device(): layer_block = gathered.reshape(n_core, n_xl, n_y, n_z, piece, row_width)....  16.4 us
    unnamed x15, local copies, waits for them, and re-layouts  10.7 us
    all_gather x1, waiting for transfers between devices, per_device(): gathered = lax.all_gather(core_part, ('core', *PLANE))  6.97 us
  transfers between devices with their start and end apart: 9, of which 8 were waited for; matrix products, arithmetic and copies ran while one was open for 10% of the time, Pallas kernels for 0%

profile of v1, /device:TPU:1, one launch (start us, length us, event | category | flops | bytes accessed | tf_op | source)
XLA Modules:
  0.0 340.9 jit_solution(9335404819582479330)
XLA Ops:
  7.2 1.2 copy-done
  8.4 0.9 constant_dynamic-slice_fusion
  9.3 0.8 constant_dynamic-slice_fusion.1
  10.1 0.1 broadcast_in_dim.82
  10.2 1.1 reshape.234
  11.3 16.9 %all-to-all-start.1 = ((bf16[32,2,2048]{2,1,0:T(2,128)(2,1)}), bf16[32,2,2048]{2,1,0:T(2,128)(2,1)S(1)}, u32[]{:S(2)}, u32[]{:S(2)}) async-start(bf16[32,2,2048]{2,1,0:T(2,128)(2,1)} %reshape.234), calls=%async_computation.1 | async-start | bytes 524288 | tf_op jit(solution)/shard_map/all_to_all | solution.py:19
  28.3 0.8 convert.1
  29.1 0.8 convert_multiply_fusion
  29.8 0.8 broadcast_compare_fusion
  30.6 1.2 broadcast_select_fusion
  31.7 0.7 copy_bitcast_fusion
  32.4 15.8 %all-to-all-done.1 = bf16[32,2,2048]{2,1,0:T(2,128)(2,1)S(1)} async-done(((bf16[32,2,2048]{2,1,0:T(2,128)(2,1)}), bf16[32,2,2048]{2,1,0:T(2,128)(2,1)S(1)}, u32[]{:S(2)}, u32[]{:S(2)}) %all-to-all-start.1) | async-done | bytes 262176 | tf_op jit(solution)/shard_map/all_to_all | solution.py:19
  48.3 3.4 %all-to-all-start = ((f32[2,11,8,256]{3,2,1,0:T(8,128)}), f32[2,11,8,256]{3,2,1,0:T(8,128)S(1)}, u32[]{:S(2)}, u32[]{:S(2)}) async-start(f32[2,11,8,256]{3,2,1,0:T(8,128)} %copy_bitcast_fusion), calls=%async_computation | async-start | bytes 360448 | tf_op jit(solution)/shard_map/all_to_all | solution.py:63
  51.7 0.4 reshape.235
  52.1 0.3 copy.20
  52.4 0.5 dot_general.38
  52.9 0.9 fusion.44
  53.8 3.9 %all-to-all-done = f32[2,11,8,256]{3,2,1,0:T(8,128)S(1)} async-done(((f32[2,11,8,256]{3,2,1,0:T(8,128)}), f32[2,11,8,256]{3,2,1,0:T(8,128)S(1)}, u32[]{:S(2)}, u32[]{:S(2)}) %all-to-all-start) | async-done | bytes 180256 | tf_op jit(solution)/shard_map/all_to_all | solution.py:63
  57.7 4.0 %all-to-all-start.2 = ((f32[8,8,256]{2,1,0:T(8,128)}), f32[8,8,256]{2,1,0:T(8,128)S(1)}, u32[]{:S(2)}, u32[]{:S(2)}) async-start(f32[8,8,256]{2,1,0:T(8,128)} %fusion.44), calls=%async_computation.2 | async-start | bytes 131072 | tf_op jit(solution)/shard_map/all_to_all | solution.py:52
  61.8 5.6 %all-to-all-done.2 = f32[8,8,256]{2,1,0:T(8,128)S(1)} async-done(((f32[8,8,256]{2,1,0:T(8,128)}), f32[8,8,256]{2,1,0:T(8,128)S(1)}, u32[]{:S(2)}, u32[]{:S(2)}) %all-to-all-start.2) | async-done | bytes 65568 | tf_op jit(solution)/shard_map/all_to_all | solution.py:52
  67.4 0.1 fusion.33
  67.5 0.7 broadcast_in_dim.83
  68.1 5.3 %all-to-all-start.3 = ((bf16[16,8,512]{2,1,0:T(8,128)(2,1)}), bf16[16,8,512]{2,1,0:T(8,128)(2,1)S(1)}, u32[]{:S(2)}, u32[]{:S(2)}) async-start(bf16[16,8,512]{2,1,0:T(8,128)(2,1)} %broadcast_in_dim.83), calls=%async_computation.3 | async-start | bytes 262144 | tf_op jit(solution)/shard_map/all_to_all | solution.py:19
  73.5 7.0 %all-gather.2.cloned.1.call-done = bf16[16,1024,256]{2,1,0:T(8,128)(2,1)} async-done(((bf16[1,1024,256]{2,1,0:T(8,128)(2,1)}), bf16[16,1024,256]{2,1,0:T(8,128)(2,1)}) %all-gather.2.cloned.1.call-update) | async-done | bytes 8388624 | tf_op jit(solution)/shard_map/all_gather | solution.py:41
  80.5 16.4 %copy.21 = bf16[16,2,4,64,2,256]{5,4,3,2,1,0:T(2,128)(2,1)} copy(bf16[16,2,4,64,2,256]{5,3,0,2,4,1:T(8,128)(2,1)} %bitcast.113) | data formatting | bytes 16777216 | tf_op jit(solution)/shard_map/transpose | solution.py:44
  96.9 8.0 %copy.25 = bf16[1024,8,2,256]{3,1,2,0:T(8,128)(2,1)} copy(bf16[1024,8,2,256]{3,2,1,0:T(2,128)(2,1)} %bitcast.112) | data formatting | bytes 16777216
  104.9 4.7 %fusion.35 = (bf16[8,512]{1,0:T(8,128)(2,1)S(1)}, f32[8,512]{1,0:T(8,128)S(1)}) fusion(f32[8,512]{1,0:T(8,128)S(1)} %bitcast.143, bf16[8,8192]{1,0:T(8,128)(2,1)S(1)} %bitcast.116, bf16[8192,512]{1,0:T(8,128)(2,1)} %bitcast.100, f32[8,512]{1,0:T(8,128)S(1)} %bitcast.130, f32[8,512]{1,0:T(8,128)S(1)} %bitcast.128, f32[8,512]{1,0:T(8,128)S(1)} %bitcast.132, ...), kind=kOutput, calls=%fused_computation.74 | convolution fusion | flops 67153920 | bytes 8609824 | tf_op jit(solution)/shard_map/dot_general | solution.py:78
  109.6 23.3 %all_to_all.80 = bf16[16,8,512]{2,1,0:T(8,128)(2,1)S(1)} all-to-all(bf16[16,8,512]{2,1,0:T(8,128)(2,1)S(1)} %broadcast_in_dim.84), channel_id=1, replica_groups=mesh['xh'=2,'core'=2,'xl'=2,'z'=16,'y'=4] {'z'}, dimensions={0} | all-to-all | bytes 262144 | tf_op jit(solution)/shard_map/all_to_all | solution.py:19
  133.0 1.2 fusion.36
  134.1 0.1 broadcast_in_dim.85
  134.2 18.3 %all_to_all.81 = bf16[16,8,512]{2,1,0:T(8,128)(2,1)S(1)} all-to-all(bf16[16,8,512]{2,1,0:T(8,128)(2,1)S(1)} %broadcast_in_dim.85), channel_id=1, replica_groups=mesh['xh'=2,'core'=2,'xl'=2,'z'=16,'y'=4] {'z'}, dimensions={0} | all-to-all | bytes 262144 | tf_op jit(solution)/shard_map/all_to_all | solution.py:19
  152.5 1.2 fusion.37
  153.7 17.8 %all_to_all.82 = bf16[16,8,512]{2,1,0:T(8,128)(2,1)S(1)} all-to-all(bf16[16,8,512]{2,1,0:T(8,128)(2,1)S(1)} %broadcast_in_dim.86), channel_id=1, replica_groups=mesh['xh'=2,'core'=2,'xl'=2,'z'=16,'y'=4] {'z'}, dimensions={0} | all-to-all | bytes 262144 | tf_op jit(solution)/shard_map/all_to_all | solution.py:19
  171.4 1.2 fusion.38
  172.6 0.1 broadcast_in_dim.158
  172.7 17.2 %all_to_all.83 = bf16[16,8,512]{2,1,0:T(8,128)(2,1)S(1)} all-to-all(bf16[16,8,512]{2,1,0:T(8,128)(2,1)S(1)} %broadcast_in_dim.158), channel_id=1, replica_groups=mesh['xh'=2,'core'=2,'xl'=2,'z'=16,'y'=4] {'z'}, dimensions={0} | all-to-all | bytes 262144 | tf_op jit(solution)/shard_map/all_to_all | solution.py:19
  189.9 1.2 fusion.39
  191.1 17.0 %all_to_all.84 = bf16[16,8,512]{2,1,0:T(8,128)(2,1)S(1)} all-to-all(bf16[16,8,512]{2,1,0:T(8,128)(2,1)S(1)} %broadcast_in_dim.159), channel_id=1, replica_groups=mesh['xh'=2,'core'=2,'xl'=2,'z'=16,'y'=4] {'z'}, dimensions={0} | all-to-all | bytes 262144 | tf_op jit(solution)/shard_map/all_to_all | solution.py:19
  208.0 1.2 fusion.40
  209.2 16.1 %all_to_all.85 = bf16[16,8,512]{2,1,0:T(8,128)(2,1)S(1)} all-to-all(bf16[16,8,512]{2,1,0:T(8,128)(2,1)S(1)} %broadcast_in_dim.160), channel_id=1, replica_groups=mesh['xh'=2,'core'=2,'xl'=2,'z'=16,'y'=4] {'z'}, dimensions={0} | all-to-all | bytes 262144 | tf_op jit(solution)/shard_map/all_to_all | solution.py:19
  225.4 1.2 fusion.41
  226.6 15.8 %all_to_all.86 = bf16[16,8,512]{2,1,0:T(8,128)(2,1)S(1)} all-to-all(bf16[16,8,512]{2,1,0:T(8,128)(2,1)S(1)} %broadcast_in_dim.161), channel_id=1, replica_groups=mesh['xh'=2,'core'=2,'xl'=2,'z'=16,'y'=4] {'z'}, dimensions={0} | all-to-all | bytes 262144 | tf_op jit(solution)/shard_map/all_to_all | solution.py:19
  242.4 1.2 fusion.42
  243.6 15.9 %all_to_all.87 = bf16[16,8,512]{2,1,0:T(8,128)(2,1)S(1)} all-to-all(bf16[16,8,512]{2,1,0:T(8,128)(2,1)S(1)} %broadcast_in_dim.162), channel_id=1, replica_groups=mesh['xh'=2,'core'=2,'xl'=2,'z'=16,'y'=4] {'z'}, dimensions={0} | all-to-all | bytes 262144 | tf_op jit(solution)/shard_map/all_to_all | solution.py:19
  259.5 1.2 fusion.43
  260.7 0.7 broadcast_in_dim.163
  261.3 4.0 %all-to-all-start.12 = ((bf16[16,8,512]{2,1,0:T(8,128)(2,1)}), bf16[16,8,512]{2,1,0:T(8,128)(2,1)S(1)}, u32[]{:S(2)}, u32[]{:S(2)}) async-start(bf16[16,8,512]{2,1,0:T(8,128)(2,1)} %broadcast_in_dim.163), calls=%async_computation.12 | async-start | bytes 262144 | tf_op jit(solution)/shard_map/all_to_all | solution.py:19
  265.3 12.0 %all-to-all-done.12 = bf16[16,8,512]{2,1,0:T(8,128)(2,1)S(1)} async-done(((bf16[16,8,512]{2,1,0:T(8,128)(2,1)}), bf16[16,8,512]{2,1,0:T(8,128)(2,1)S(1)}, u32[]{:S(2)}, u32[]{:S(2)}) %all-to-all-start.12) | async-done | bytes 131104 | tf_op jit(solution)/shard_map/all_to_all | solution.py:19
  277.4 4.7 %fusion.27 = f32[8]{0:T(128)S(1)} fusion(f32[8,512]{1,0:T(8,128)S(1)} %get-tuple-element.40, bf16[8,8192]{1,0:T(8,128)(2,1)S(1)} %bitcast.126, bf16[8192,512]{1,0:T(8,128)(2,1)} %bitcast.101), kind=kOutput, calls=%fused_computation.38 | convolution fusion | flops 67117048 | bytes 8536096 | tf_op jit(solution)/shard_map/dot_general | solution.py:78
  282.1 0.6 broadcast_in_dim.166
  282.7 4.0 %all-to-all-start.13 = ((f32[16,1,128]{2,1,0:T(1,128)}), f32[16,1,128]{2,1,0:T(1,128)S(1)}, u32[]{:S(2)}, u32[]{:S(2)}) async-start(f32[16,1,128]{2,1,0:T(1,128)} %broadcast_in_dim.166), calls=%async_computation.13 | async-start | bytes 16384 | tf_op jit(solution)/shard_map/all_to_all | solution.py:19
  286.7 0.1 fusion.32
  286.7 11.2 %all-to-all-done.13 = f32[16,1,128]{2,1,0:T(1,128)S(1)} async-done(((f32[16,1,128]{2,1,0:T(1,128)}), f32[16,1,128]{2,1,0:T(1,128)S(1)}, u32[]{:S(2)}, u32[]{:S(2)}) %all-to-all-start.13) | async-done | bytes 8224 | tf_op jit(solution)/shard_map/all_to_all | solution.py:19
  297.9 0.6 broadcast_in_dim.167
  298.6 15.2 %all-to-all-start.14 = ((f32[32,1,128]{2,1,0:T(1,128)}), f32[32,1,128]{2,1,0:T(1,128)S(1)}, u32[]{:S(2)}, u32[]{:S(2)}) async-start(f32[32,1,128]{2,1,0:T(1,128)} %broadcast_in_dim.167), calls=%async_computation.14 | async-start | bytes 32768 | tf_op jit(solution)/shard_map/all_to_all | solution.py:19
  313.8 0.2 select_reduce_fusion
  314.0 6.6 %all-to-all-done.14 = f32[32,1,128]{2,1,0:T(1,128)S(1)} async-done(((f32[32,1,128]{2,1,0:T(1,128)}), f32[32,1,128]{2,1,0:T(1,128)S(1)}, u32[]{:S(2)}, u32[]{:S(2)}) %all-to-all-start.14) | async-done | bytes 16416 | tf_op jit(solution)/shard_map/all_to_all | solution.py:19
  320.6 0.7 broadcast_in_dim.171
  321.3 4.2 %all-to-all-start.15 = ((bf16[32,8,256]{2,1,0:T(8,128)(2,1)}), bf16[32,8,256]{2,1,0:T(8,128)(2,1)S(1)}, u32[]{:S(2)}, u32[]{:S(2)}) async-start(bf16[32,8,256]{2,1,0:T(8,128)(2,1)} %bitcast.50), calls=%async_computation.15 | async-start | bytes 262144 | tf_op jit(solution)/shard_map/all_to_all | solution.py:88
  325.6 0.1 broadcast_in_dim.168
  325.7 0.2 select_reduce_fusion.1
  325.9 0.5 fusion.31
  326.4 6.8 %all-to-all-done.15 = bf16[32,8,256]{2,1,0:T(8,128)(2,1)S(1)} async-done(((bf16[32,8,256]{2,1,0:T(8,128)(2,1)}), bf16[32,8,256]{2,1,0:T(8,128)(2,1)S(1)}, u32[]{:S(2)}, u32[]{:S(2)}) %all-to-all-start.15) | async-done | bytes 131104 | tf_op jit(solution)/shard_map/all_to_all | solution.py:88
  333.2 0.8 convolution_convert_fusion
  (30 shorter events, 0.5 us)
Async XLA Ops:
  7.2 1.2 copy-start
  7.2 73.3 %all-gather.2.cloned.1.call-start = ((), (), s32[]{:S(2)}) async-start(), calls=%async_computation.16 | async-start | bytes 8912896 | tf_op jit(solution)/shard_map/all_gather | solution.py:41
  11.3 36.9 %all-to-all-start.1 = ((bf16[32,2,2048]{2,1,0:T(2,128)(2,1)}), bf16[32,2,2048]{2,1,0:T(2,128)(2,1)S(1)}, u32[]{:S(2)}, u32[]{:S(2)}) async-start(bf16[32,2,2048]{2,1,0:T(2,128)(2,1)} %reshape.234), calls=%async_computation.1 | async-start | bytes 524288 | tf_op jit(solution)/shard_map/all_to_all | solution.py:19
  48.3 9.5 %all-to-all-start = ((f32[2,11,8,256]{3,2,1,0:T(8,128)}), f32[2,11,8,256]{3,2,1,0:T(8,128)S(1)}, u32[]{:S(2)}, u32[]{:S(2)}) async-start(f32[2,11,8,256]{3,2,1,0:T(8,128)} %copy_bitcast_fusion), calls=%async_computation | async-start | bytes 360448 | tf_op jit(solution)/shard_map/all_to_all | solution.py:63
  57.7 9.7 %all-to-all-start.2 = ((f32[8,8,256]{2,1,0:T(8,128)}), f32[8,8,256]{2,1,0:T(8,128)S(1)}, u32[]{:S(2)}, u32[]{:S(2)}) async-start(f32[8,8,256]{2,1,0:T(8,128)} %fusion.44), calls=%async_computation.2 | async-start | bytes 131072 | tf_op jit(solution)/shard_map/all_to_all | solution.py:52
  68.1 36.7 %all-to-all-start.3 = ((bf16[16,8,512]{2,1,0:T(8,128)(2,1)}), bf16[16,8,512]{2,1,0:T(8,128)(2,1)S(1)}, u32[]{:S(2)}, u32[]{:S(2)}) async-start(bf16[16,8,512]{2,1,0:T(8,128)(2,1)} %broadcast_in_dim.83), calls=%async_computation.3 | async-start | bytes 262144 | tf_op jit(solution)/shard_map/all_to_all | solution.py:19
  104.9 28.1 %slice-start = ((s8[8388608]{0:T(1024)(128)(4,1)}), s8[4194304]{0:T(1024)(128)(4,1)S(1)}, s32[]{:S(2)}) async-start(s8[8388608]{0:T(1024)(128)(4,1)} %bitcast.102), calls=%async_computation.17 | async-start | bytes 8388608
  104.9 28.1 %slice-start.1 = ((s8[8388608]{0:T(1024)(128)(4,1)}), s8[4194304]{0:T(1024)(128)(4,1)S(1)}, s32[]{:S(2)}) async-start(s8[8388608]{0:T(1024)(128)(4,1)} %bitcast.102), calls=%async_computation.18 | async-start | bytes 8388608
  260.6 26.0 %copy-start.3 = (s32[256]{0:T(256)S(1)}, s32[256]{0:T(256)}, u32[]{:S(2)}) copy-start(s32[256]{0:T(256)} %param.12) | copy-start | bytes 3076
  260.6 53.2 %copy-start.1 = (f32[256]{0:T(256)S(1)}, f32[256]{0:T(256)}, u32[]{:S(2)}) copy-start(f32[256]{0:T(256)} %param.13) | copy-start | bytes 3076
  260.7 53.3 %copy-start.2 = (s32[256]{0:T(256)S(1)}, s32[256]{0:T(256)}, u32[]{:S(2)}) copy-start(s32[256]{0:T(256)} %param.11) | copy-start | bytes 3076
  261.3 16.1 %all-to-all-start.12 = ((bf16[16,8,512]{2,1,0:T(8,128)(2,1)}), bf16[16,8,512]{2,1,0:T(8,128)(2,1)S(1)}, u32[]{:S(2)}, u32[]{:S(2)}) async-start(bf16[16,8,512]{2,1,0:T(8,128)(2,1)} %broadcast_in_dim.163), calls=%async_computation.12 | async-start | bytes 262144 | tf_op jit(solution)/shard_map/all_to_all | solution.py:19
  282.7 15.2 %all-to-all-start.13 = ((f32[16,1,128]{2,1,0:T(1,128)}), f32[16,1,128]{2,1,0:T(1,128)S(1)}, u32[]{:S(2)}, u32[]{:S(2)}) async-start(f32[16,1,128]{2,1,0:T(1,128)} %broadcast_in_dim.166), calls=%async_computation.13 | async-start | bytes 16384 | tf_op jit(solution)/shard_map/all_to_all | solution.py:19
  298.6 22.1 %all-to-all-start.14 = ((f32[32,1,128]{2,1,0:T(1,128)}), f32[32,1,128]{2,1,0:T(1,128)S(1)}, u32[]{:S(2)}, u32[]{:S(2)}) async-start(f32[32,1,128]{2,1,0:T(1,128)} %broadcast_in_dim.167), calls=%async_computation.14 | async-start | bytes 32768 | tf_op jit(solution)/shard_map/all_to_all | solution.py:19
  321.3 11.9 %all-to-all-start.15 = ((bf16[32,8,256]{2,1,0:T(8,128)(2,1)}), bf16[32,8,256]{2,1,0:T(8,128)(2,1)S(1)}, u32[]{:S(2)}, u32[]{:S(2)}) async-start(bf16[32,8,256]{2,1,0:T(8,128)(2,1)} %bitcast.50), calls=%async_computation.15 | async-start | bytes 262144 | tf_op jit(solution)/shard_map/all_to_all | solution.py:88
Sparse Core Ops, SparseCore 0:
  10.1 70.2 all-gather.1

commit v2 on v1

v2 whole, which is shorter than its diff:
```python
import math

import jax
import jax.numpy as jnp
from jax import lax
from jax.experimental import pallas as pl
from jax.experimental.pallas import tpu as pltpu
from jax.sharding import Mesh, PartitionSpec as P

N = 8192
SWEEPS = 10
NEVER = -3.0e38

GROUP = ("xh", "core")
PLANE = ("xl", "y")
LAYER = ("xh", "core", "xl", "y")


def sent_to_all(value, axes):
    length = lax.axis_size(axes)
    return lax.all_to_all(
        jnp.broadcast_to(value[None], (length, *value.shape)), axes, 0, 0, tiled=True
    )


def in_spin_order(gathered):
    n_core, n_xl, n_y, n_z, piece, width = gathered.shape
    shape = (n_z, n_core * n_y, piece, width)

    def body(source, *rest):
        halves, sems = rest[:n_xl], rest[n_xl]
        copies = [
            pltpu.make_async_copy(
                source.at[core, xl, y],
                halves[xl].at[:, core * n_y + y],
                sems.at[core, xl, y],
            )
            for xl in range(n_xl)
            for core in range(n_core)
            for y in range(n_y)
        ]
        for copy in copies:
            copy.start()
        for copy in copies:
            copy.wait()

    halves = pl.pallas_call(
        body,
        in_specs=[pl.BlockSpec(memory_space=pltpu.HBM)],
        out_specs=[pl.BlockSpec(memory_space=pl.ANY)] * n_xl,
        out_shape=[jax.ShapeDtypeStruct(shape, gathered.dtype)] * n_xl,
        scratch_shapes=[pltpu.SemaphoreType.DMA((n_core, n_xl, n_y))],
        compiler_params=pltpu.CompilerParams(vmem_limit_bytes=2 * 1024 * 1024),
        name="in_spin_order",
    )(pltpu.with_memory_space_constraint(gathered, pltpu.HBM))
    return [half.reshape(-1, width) for half in halves]


def per_device(spin_init, couplings, flip_noise, colors, beta_steps, partners, swap_noise):
    rep_dev, row_width = spin_init.shape
    n_xl = lax.axis_size("xl")
    n_y = lax.axis_size("y")
    n_z = lax.axis_size("z")
    n_core = lax.axis_size("core")
    y_index = lax.axis_index("y")
    xl_index = lax.axis_index("xl")
    core_index = lax.axis_index("core")
    rep_index = lax.axis_index(GROUP)
    share = rep_dev // (n_xl * n_y)
    piece = row_width // n_y
    width = n_xl * row_width
    own_block = couplings.reshape(-1, row_width)

    core_part = lax.dynamic_slice_in_dim(
        couplings.reshape(n_core, -1, row_width), core_index, 1, 0
    )[0]
    gathered = lax.all_gather(core_part, ("core", *PLANE))

    start_piece = lax.dynamic_slice_in_dim(spin_init, y_index * piece, piece, 1)
    start_rows = sent_to_all(start_piece, ("xl", "z"))

    slot_ids = rep_index * rep_dev + jnp.arange(rep_dev, dtype=jnp.int32)
    mate_ids = lax.dynamic_slice_in_dim(partners, rep_index * rep_dev, rep_dev)
    all_ids = jnp.arange(partners.shape[0], dtype=jnp.int32)[None, :]

    def picked(values, ids):
        return jnp.sum(jnp.where(ids[:, None] == all_ids, values[None, :], 0.0), axis=1)

    all_betas = beta_steps.astype(jnp.float32)
    beta_gap = picked(all_betas, slot_ids) - picked(all_betas, mate_ids)
    noise = picked(swap_noise, jnp.minimum(slot_ids, mate_ids))
    mate_rows_of = (mate_ids[:, None] == all_ids).astype(jnp.bfloat16)
    start_rows, beta_gap, noise, mate_rows_of = lax.optimization_barrier(
        (start_rows, beta_gap, noise, mate_rows_of)
    )
    start_rows = start_rows.transpose(1, 0, 2).reshape(rep_dev, -1)
    partial = jnp.dot(start_rows, own_block, preferred_element_type=jnp.float32)
    partial = lax.all_to_all(
        partial.reshape(n_xl * n_y, share, row_width), PLANE, 0, 0, tiled=True
    )
    fields = partial.reshape(n_xl, n_y, share, row_width).sum(axis=1)
    fields = fields.transpose(1, 0, 2).reshape(share, width)

    steps = jnp.arange(SWEEPS, dtype=jnp.int32)[:, None, None]

    def start_of(xl):
        first = (xl * n_y + y_index) * share
        noise = lax.dynamic_slice_in_dim(flip_noise, first, share, 1)
        limits = jnp.where(colors[None, None, :] == steps % 2, noise, NEVER)
        spins = lax.dynamic_slice_in_dim(spin_init, first, share, 0)
        return jnp.concatenate([spins.astype(jnp.float32)[None], limits], axis=0)

    kept = start_of(xl_index)
    other = lax.ppermute(start_of(1 - xl_index), "xl", [(0, 1), (1, 0)])
    is_left = xl_index == 0
    both = jnp.concatenate(
        [jnp.where(is_left, kept, other), jnp.where(is_left, other, kept)], axis=2
    )
    spins = both[0]
    limits = both[1:]
    first_slot = rep_index * rep_dev + lax.axis_index(PLANE) * share
    beta_col = lax.dynamic_slice_in_dim(beta_steps, first_slot, share).astype(jnp.float32)
    beta_col = beta_col[:, None] * (1.0 / 16384.0)

    def metropolis(spins, fields, limit):
        energy_cost = beta_col * (spins * fields)
        return jnp.where(energy_cost < limit, -spins, spins)

    def layer_rows(spins):
        return sent_to_all(spins.astype(jnp.bfloat16), "z")

    def layer_fields(rows, layer_block):
        rows = rows.transpose(1, 0, 2).reshape(share, N)
        halves = [jnp.dot(rows, half, preferred_element_type=jnp.float32) for half in layer_block]
        return jnp.concatenate(halves, axis=1)

    spins = metropolis(spins, fields, limits[0])
    rows, gathered = lax.optimization_barrier((layer_rows(spins), gathered))
    layer_block = in_spin_order(
        gathered.reshape(n_core, n_xl, n_y, n_z, piece, row_width)
    )
    for step in range(1, SWEEPS):
        spins = metropolis(spins, layer_fields(rows, layer_block), limits[step])
        rows = layer_rows(spins)

    layer_sum = jnp.sum(spins * layer_fields(rows, layer_block), axis=1, keepdims=True)
    layer_sum = jnp.broadcast_to(layer_sum, (share, 128))
    energy = -0.5 * sent_to_all(layer_sum, "z").sum(axis=0)

    high = lax.reduce_precision(energy, 8, 7)
    middle = lax.reduce_precision(energy - high, 8, 7)
    low = (energy - high) - middle
    terms = jnp.concatenate(
        [high[:, :1], middle[:, :1], low[:, :1], jnp.zeros((share, 125), jnp.float32)], axis=1
    )
    blocks = spins.astype(jnp.bfloat16).reshape(share, n_xl, row_width).transpose(1, 0, 2)
    terms = jnp.broadcast_to(terms.astype(jnp.bfloat16)[None], (n_xl, share, 128))
    blocks = jnp.concatenate([blocks, terms], axis=2)
    blocks = jnp.broadcast_to(
        blocks[None, :, None], (lax.axis_size(GROUP), n_xl, n_y, *blocks.shape[1:])
    ).reshape(-1, *blocks.shape[1:])
    table = lax.all_to_all(blocks, LAYER, 0, 0, tiled=True).reshape(-1, row_width + 128)

    own_rows = lax.dynamic_slice_in_dim(table, rep_index * rep_dev, rep_dev, 0)
    own_rows = own_rows.astype(jnp.float32)
    mate_rows = jnp.dot(mate_rows_of, table, preferred_element_type=jnp.float32)

    def energy_of(rows):
        return rows[:, row_width] + (rows[:, row_width + 1] + rows[:, row_width + 2])

    own_energy = energy_of(own_rows)
    mate_energy = energy_of(mate_rows)
    swap_gain = beta_gap * (own_energy - mate_energy) * (1.0 / (64.0 * N * math.sqrt(N)))
    accept = swap_gain + noise > 0.0
    spins_out = jnp.where(
        accept[:, None], mate_rows[:, :row_width], own_rows[:, :row_width]
    )
    energies = jnp.where(accept, mate_energy, own_energy) * (1.0 / (N * math.sqrt(N)))
    return (spins_out.astype(jnp.bfloat16), energies)


def solution(mesh):
    fine = Mesh(mesh.devices.reshape(2, 2, 2, 16, 4), ("xh", "core", "xl", "z", "y"))
    rep, row, col = ("xh", "core"), ("xl", "z"), "y"
    in_specs = (
        P(rep, row),
        P(None, col, None, row),
        P(None, rep, row),
        P(row),
        P(),
        P(),
        P(),
    )
    out_specs = (P(rep, row), P(rep))
    return jax.shard_map(
        per_device, mesh=fine, in_specs=in_specs, out_specs=out_specs, check_vma=False
    )
```

time: 342 us -> 305 us (0.89)
  blocking collectives: 141 us -> 197 us
  waiting for transfers between devices: 69 us -> 31.6 us
  starting transfers between devices: 57.2 us -> 28.4 us
  local copies, waits for them, and re-layouts: 33.4 us -> 6.16 us
  matrix products: 20.3 us -> 14.1 us
  Pallas kernels: 0 us -> 3.51 us
    all_to_all x8 -> x10, blocking collectives: 141 us -> 174 us  [sent_to_all(): lax.all_to_all(jnp.broadcast_to(value[None], (length, *value.shape)), axe...]
    all_to_all x5 -> x2, starting transfers between devices: 45.5 us -> 20.9 us  [sent_to_all(): lax.all_to_all(jnp.broadcast_to(value[None], (length, *value.shape)), axe...]
    all_to_all x0 -> x1, blocking collectives: none -> 23.4 us  [per_device(): lax.all_to_all(blocks, LAYER, 0, 0, tiled=True).reshape(-1, row_width + 128)]
    all_to_all x5 -> x2, waiting for transfers between devices: 45.7 us -> 22.4 us  [sent_to_all(): lax.all_to_all(jnp.broadcast_to(value[None], (length, *value.shape)), axe...]
    transpose x1 -> x0, local copies, waits for them, and re-layouts: 16.4 us -> none  [per_device(): layer_block = gathered.reshape(n_core, n_xl, n_y, n_z, piece, row_width)....]
    all_to_all x2 -> x0, waiting for transfers between devices: 10.8 us -> none  [the longest x1 6.81 us: per_device(): lax.all_to_all(blocks, LAYER, 0, 0, tiled=True).reshape(-1, row_width)]
    unnamed x15 -> x3, local copies, waits for them, and re-layouts: 10.7 us -> 2.3 us
    all_to_all x2 -> x0, starting transfers between devices: 7.66 us -> none  [the longest x1 4.23 us: per_device(): lax.all_to_all(blocks, LAYER, 0, 0, tiled=True).reshape(-1, row_width)]
  transfers between devices with their start and end apart: 9 -> 5, of which waited for: 8 -> 4; matrix products, arithmetic and copies ran while one was open for 10% -> 3% of each run, Pallas kernels for 0% -> 0%
where the time goes in v2:
time: 305 us; the launch traced here: 304 us
  blocking collectives  197 us (65%)
  waiting for transfers between devices  31.6 us (10%)
  starting transfers between devices  28.4 us (9%)
  between operations  14.3 us (5%)
  matrix products  14.1 us (5%)
  other arithmetic  8.57 us (3%)
  local copies, waits for them, and re-layouts  6.16 us (2%)
  Pallas kernels  3.51 us (1%)
    all_to_all x10, blocking collectives, sent_to_all(): lax.all_to_all(jnp.broadcast_to(value[None], (length, *value.shape)), axe...  174 us
    all_to_all x1, blocking collectives, per_device(): lax.all_to_all(blocks, LAYER, 0, 0, tiled=True).reshape(-1, row_width + 128)  23.4 us
    all_to_all x2, waiting for transfers between devices, sent_to_all(): lax.all_to_all(jnp.broadcast_to(value[None], (length, *value.shape)), axe...  22.4 us
    all_to_all x2, starting transfers between devices, sent_to_all(): lax.all_to_all(jnp.broadcast_to(value[None], (length, *value.shape)), axe...  20.9 us
    dot_general x20, matrix products, layer_fields(): jnp.dot(rows, half, preferred_element_type=jnp.float32)  13 us
  transfers between devices with their start and end apart: 5, of which 4 were waited for; matrix products, arithmetic and copies ran while one was open for 3% of the time, Pallas kernels for 0%

profile of v2, /device:TPU:1, one launch (start us, length us, event | category | flops | bytes accessed | tf_op | source)
XLA Modules:
  0.0 303.6 jit_solution(5303286113855294729)
XLA Ops:
  7.2 1.2 copy-done
  8.4 0.9 constant_dynamic-slice_fusion
  9.3 0.8 constant_dynamic-slice_fusion.1
  10.1 0.1 broadcast_in_dim.173
  10.2 1.1 reshape.570
  11.3 16.9 %all-to-all-start = ((bf16[32,2,2048]{2,1,0:T(2,128)(2,1)}), bf16[32,2,2048]{2,1,0:T(2,128)(2,1)S(1)}, u32[]{:S(2)}, u32[]{:S(2)}) async-start(bf16[32,2,2048]{2,1,0:T(2,128)(2,1)} %reshape.570), calls=%async_computation | async-start | bytes 524288 | tf_op jit(solution)/shard_map/all_to_all | solution.py:21
  28.3 0.7 bitcast_convert_fusion.1
  29.0 0.8 broadcast_compare_fusion
  29.8 1.0 dynamic-slice_select_fusion.1
  30.8 3.1 %collective-permute-start = (f32[11,8,256]{2,1,0:T(8,128)S(1)}, f32[11,8,256]{2,1,0:T(8,128)S(1)}, u32[]{:S(2)}, u32[]{:S(2)}) collective-permute-start(f32[11,8,256]{2,1,0:T(8,128)S(1)} %pad_maximum_fusion.1), channel_id=1, source_target_pairs={{0,64},{64,0},{1,65},{65,1},{2,66},{66,2},{3,67},{67,3},{4,68},{68... | collective-permute-start | bytes 270344 | tf_op jit(solution)/shard_map/ppermute | solution.py:114
  33.9 0.7 convert_element_type.66
  34.6 0.8 fusion.84
  35.4 0.2 select_reduce_fusion.1
  35.6 0.8 convert_multiply_fusion
  36.3 0.9 select_reduce_fusion
  37.3 11.0 %all-to-all-done = bf16[32,2,2048]{2,1,0:T(2,128)(2,1)S(1)} async-done(((bf16[32,2,2048]{2,1,0:T(2,128)(2,1)}), bf16[32,2,2048]{2,1,0:T(2,128)(2,1)S(1)}, u32[]{:S(2)}, u32[]{:S(2)}) %all-to-all-start) | async-done | bytes 262176 | tf_op jit(solution)/shard_map/all_to_all | solution.py:21
  48.3 0.4 reshape.571
  48.6 0.3 copy.10
  49.0 0.5 dot_general.68
  49.5 0.9 fusion.95
  50.4 4.3 %all-to-all-start.1 = ((f32[8,8,256]{2,1,0:T(8,128)}), f32[8,8,256]{2,1,0:T(8,128)S(1)}, u32[]{:S(2)}, u32[]{:S(2)}) async-start(f32[8,8,256]{2,1,0:T(8,128)} %fusion.95), calls=%async_computation.1 | async-start | bytes 131072 | tf_op jit(solution)/shard_map/all_to_all | solution.py:98
  54.7 5.6 %all-to-all-done.1 = f32[8,8,256]{2,1,0:T(8,128)S(1)} async-done(((f32[8,8,256]{2,1,0:T(8,128)}), f32[8,8,256]{2,1,0:T(8,128)S(1)}, u32[]{:S(2)}, u32[]{:S(2)}) %all-to-all-start.1) | async-done | bytes 65568 | tf_op jit(solution)/shard_map/all_to_all | solution.py:98
  60.4 16.5 %all_to_all.70 = bf16[16,8,512]{2,1,0:T(8,128)(2,1)S(1)} all-to-all(bf16[16,8,512]{2,1,0:T(8,128)(2,1)S(1)} %broadcast_in_dim.184), channel_id=1, replica_groups=mesh['xh'=2,'core'=2,'xl'=2,'z'=16,'y'=4] {'z'}, dimensions={0} | all-to-all | bytes 262144 | tf_op jit(solution)/shard_map/all_to_all | solution.py:21
  76.9 3.6 %all-gather.2.cloned.1.call-done = bf16[16,1024,256]{2,1,0:T(8,128)(2,1)} async-done(((bf16[1,1024,256]{2,1,0:T(8,128)(2,1)}), bf16[16,1024,256]{2,1,0:T(8,128)(2,1)}) %all-gather.2.cloned.1.call-update) | async-done | bytes 8388624 | tf_op jit(solution)/shard_map/all_gather | solution.py:77
  80.5 3.5 %in_spin_order.1 = (bf16[16,8,64,256]{3,2,1,0:T(8,128)(2,1)S(1)}, bf16[16,8,64,256]{3,2,1,0:T(8,128)(2,1)S(1)}) custom-call(bf16[2,2,4,16,64,256]{5,4,3,2,1,0:T(8,128)(2,1)} %bitcast.236), custom_call_target="tpu_custom_call" | custom-call | tf_op jit(solution)/shard_map/in_spin_order/pallas_call | solution.py:47
  84.0 0.6 fusion.97
  84.6 0.7 fusion.96
  85.4 23.2 %all_to_all.71 = bf16[16,8,512]{2,1,0:T(8,128)(2,1)S(1)} all-to-all(bf16[16,8,512]{2,1,0:T(8,128)(2,1)S(1)} %broadcast_in_dim.186), channel_id=1, replica_groups=mesh['xh'=2,'core'=2,'xl'=2,'z'=16,'y'=4] {'z'}, dimensions={0} | all-to-all | bytes 262144 | tf_op jit(solution)/shard_map/all_to_all | solution.py:21
  108.6 0.6 fusion.99
  109.3 0.7 fusion.98
  110.0 18.3 %all_to_all.72 = bf16[16,8,512]{2,1,0:T(8,128)(2,1)S(1)} all-to-all(bf16[16,8,512]{2,1,0:T(8,128)(2,1)S(1)} %broadcast_in_dim.188), channel_id=1, replica_groups=mesh['xh'=2,'core'=2,'xl'=2,'z'=16,'y'=4] {'z'}, dimensions={0} | all-to-all | bytes 262144 | tf_op jit(solution)/shard_map/all_to_all | solution.py:21
  128.3 0.6 fusion.101
  128.9 0.7 fusion.100
  129.7 17.8 %all_to_all.73 = bf16[16,8,512]{2,1,0:T(8,128)(2,1)S(1)} all-to-all(bf16[16,8,512]{2,1,0:T(8,128)(2,1)S(1)} %broadcast_in_dim.190), channel_id=1, replica_groups=mesh['xh'=2,'core'=2,'xl'=2,'z'=16,'y'=4] {'z'}, dimensions={0} | all-to-all | bytes 262144 | tf_op jit(solution)/shard_map/all_to_all | solution.py:21
  147.5 0.6 fusion.103
  148.1 0.7 fusion.102
  148.9 17.2 %all_to_all.74 = bf16[16,8,512]{2,1,0:T(8,128)(2,1)S(1)} all-to-all(bf16[16,8,512]{2,1,0:T(8,128)(2,1)S(1)} %broadcast_in_dim.192), channel_id=1, replica_groups=mesh['xh'=2,'core'=2,'xl'=2,'z'=16,'y'=4] {'z'}, dimensions={0} | all-to-all | bytes 262144 | tf_op jit(solution)/shard_map/all_to_all | solution.py:21
  166.1 0.6 fusion.105
  166.7 0.7 fusion.104
  167.5 17.0 %all_to_all.75 = bf16[16,8,512]{2,1,0:T(8,128)(2,1)S(1)} all-to-all(bf16[16,8,512]{2,1,0:T(8,128)(2,1)S(1)} %broadcast_in_dim.194), channel_id=1, replica_groups=mesh['xh'=2,'core'=2,'xl'=2,'z'=16,'y'=4] {'z'}, dimensions={0} | all-to-all | bytes 262144 | tf_op jit(solution)/shard_map/all_to_all | solution.py:21
  184.4 0.6 fusion.107
  185.1 0.7 fusion.106
  185.8 16.1 %all_to_all.76 = bf16[16,8,512]{2,1,0:T(8,128)(2,1)S(1)} all-to-all(bf16[16,8,512]{2,1,0:T(8,128)(2,1)S(1)} %broadcast_in_dim.196), channel_id=1, replica_groups=mesh['xh'=2,'core'=2,'xl'=2,'z'=16,'y'=4] {'z'}, dimensions={0} | all-to-all | bytes 262144 | tf_op jit(solution)/shard_map/all_to_all | solution.py:21
  202.0 0.6 fusion.109
  202.6 0.7 fusion.108
  203.4 15.8 %all_to_all.77 = bf16[16,8,512]{2,1,0:T(8,128)(2,1)S(1)} all-to-all(bf16[16,8,512]{2,1,0:T(8,128)(2,1)S(1)} %broadcast_in_dim.198), channel_id=1, replica_groups=mesh['xh'=2,'core'=2,'xl'=2,'z'=16,'y'=4] {'z'}, dimensions={0} | all-to-all | bytes 262144 | tf_op jit(solution)/shard_map/all_to_all | solution.py:21
  219.2 0.6 fusion.111
  219.8 0.7 fusion.110
  220.6 15.9 %all_to_all.78 = bf16[16,8,512]{2,1,0:T(8,128)(2,1)S(1)} all-to-all(bf16[16,8,512]{2,1,0:T(8,128)(2,1)S(1)} %broadcast_in_dim.200), channel_id=1, replica_groups=mesh['xh'=2,'core'=2,'xl'=2,'z'=16,'y'=4] {'z'}, dimensions={0} | all-to-all | bytes 262144 | tf_op jit(solution)/shard_map/all_to_all | solution.py:21
  236.4 0.6 fusion.113
  237.1 0.7 fusion.112
  237.8 15.8 %all_to_all.79 = bf16[16,8,512]{2,1,0:T(8,128)(2,1)S(1)} all-to-all(bf16[16,8,512]{2,1,0:T(8,128)(2,1)S(1)} %broadcast_in_dim.202), channel_id=1, replica_groups=mesh['xh'=2,'core'=2,'xl'=2,'z'=16,'y'=4] {'z'}, dimensions={0} | all-to-all | bytes 262144 | tf_op jit(solution)/shard_map/all_to_all | solution.py:21
  253.7 0.6 fusion.115
  254.3 0.7 fusion.114
  255.0 0.2 fusion.10
  255.2 0.7 broadcast_in_dim_broadcast_in_dim_broadcast_in_dim.2
  255.9 4.0 %all-to-all-start.12 = ((f32[16,8,128]{2,1,0:T(8,128)}), f32[16,8,128]{2,1,0:T(8,128)S(1)}, u32[]{:S(2)}, u32[]{:S(2)}) async-start(f32[16,8,128]{2,1,0:T(8,128)} %broadcast_in_dim_broadcast_in_dim_broadcast_in_dim.2), calls=%async_computation.12 | async-start | bytes 131072 | tf_op jit(solution)/shard_map/all_to_all | solution.py:21
  260.1 11.4 %all-to-all-done.12 = f32[16,8,128]{2,1,0:T(8,128)S(1)} async-done(((f32[16,8,128]{2,1,0:T(8,128)}), f32[16,8,128]{2,1,0:T(8,128)S(1)}, u32[]{:S(2)}, u32[]{:S(2)}) %all-to-all-start.12) | async-done | bytes 65568 | tf_op jit(solution)/shard_map/all_to_all | solution.py:21
  271.6 23.4 %all_to_all.80 = bf16[32,8,384]{2,1,0:T(8,128)(2,1)S(1)} all-to-all(bf16[32,8,384]{2,1,0:T(8,128)(2,1)S(1)} %bitcast.259), channel_id=1, replica_groups=mesh['xh'=2,'core'=2,'xl'=2,'z'=16,'y'=4] {'xh','core','xl','y'}, dimensions={0} | all-to-all | bytes 393216 | tf_op jit(solution)/shard_map/all_to_all | solution.py:162
  295.0 0.2 fusion.82
  295.2 0.2 fusion.5
  295.4 0.2 fusion.7
  295.5 0.5 select_multiply_fusion
  296.1 0.7 fusion.2
  (40 shorter events, 1.4 us)
Async XLA Ops:
  7.2 1.2 copy-start
  7.2 73.3 %all-gather.2.cloned.1.call-start = ((), (), s32[]{:S(2)}) async-start(), calls=%async_computation.14 | async-start | bytes 8912896 | tf_op jit(solution)/shard_map/all_gather | solution.py:77
  11.3 37.0 %all-to-all-start = ((bf16[32,2,2048]{2,1,0:T(2,128)(2,1)}), bf16[32,2,2048]{2,1,0:T(2,128)(2,1)S(1)}, u32[]{:S(2)}, u32[]{:S(2)}) async-start(bf16[32,2,2048]{2,1,0:T(2,128)(2,1)} %reshape.570), calls=%async_computation | async-start | bytes 524288 | tf_op jit(solution)/shard_map/all_to_all | solution.py:21
  30.8 23.9 %collective-permute-start = (f32[11,8,256]{2,1,0:T(8,128)S(1)}, f32[11,8,256]{2,1,0:T(8,128)S(1)}, u32[]{:S(2)}, u32[]{:S(2)}) collective-permute-start(f32[11,8,256]{2,1,0:T(8,128)S(1)} %pad_maximum_fusion.1), channel_id=1, source_target_pairs={{0,64},{64,0},{1,65},{65,1},{2,66},{66,2},{3,67},{67,3},{4,68},{68... | collective-permute-start | bytes 270344 | tf_op jit(solution)/shard_map/ppermute | solution.py:114
  50.4 9.9 %all-to-all-start.1 = ((f32[8,8,256]{2,1,0:T(8,128)}), f32[8,8,256]{2,1,0:T(8,128)S(1)}, u32[]{:S(2)}, u32[]{:S(2)}) async-start(f32[8,8,256]{2,1,0:T(8,128)} %fusion.95), calls=%async_computation.1 | async-start | bytes 131072 | tf_op jit(solution)/shard_map/all_to_all | solution.py:98
  255.9 15.5 %all-to-all-start.12 = ((f32[16,8,128]{2,1,0:T(8,128)}), f32[16,8,128]{2,1,0:T(8,128)S(1)}, u32[]{:S(2)}, u32[]{:S(2)}) async-start(f32[16,8,128]{2,1,0:T(8,128)} %broadcast_in_dim_broadcast_in_dim_broadcast_in_dim.2), calls=%async_computation.12 | async-start | bytes 131072 | tf_op jit(solution)/shard_map/all_to_all | solution.py:21
Sparse Core Ops, SparseCore 0:
  10.1 70.2 all-gather.1

commit v3 on v2

--- a/solution.py
+++ b/solution.py
@@ -76,55 +76,71 @@
     )[0]
     gathered = lax.all_gather(core_part, ("core", *PLANE))
 
-    start_piece = lax.dynamic_slice_in_dim(spin_init, y_index * piece, piece, 1)
-    start_rows = sent_to_all(start_piece, ("xl", "z"))
-
-    slot_ids = rep_index * rep_dev + jnp.arange(rep_dev, dtype=jnp.int32)
-    mate_ids = lax.dynamic_slice_in_dim(partners, rep_index * rep_dev, rep_dev)
+    first_slot = rep_index * rep_dev
+    all_betas = beta_steps.astype(jnp.float32)
+    all_scales = all_betas * (1.0 / 16384.0)
+
+    def metropolis(spins, fields, limit, first):
+        scale = lax.dynamic_slice_in_dim(all_scales, first, spins.shape[0])[:, None]
+        energy_cost = scale * (spins * fields)
+        return jnp.where(energy_cost < limit, -spins, spins)
+
+    terms = lax.dot_general(
+        spin_init, own_block, (((1,), (1,)), ((), ())), preferred_element_type=jnp.float32
+    )
+    terms = terms.astype(jnp.bfloat16).reshape(rep_dev, -1, piece).transpose(1, 0, 2)
+    terms = lax.all_to_all(terms, ("xl", "z"), 0, 0, tiled=True)
+
+    slot_ids = first_slot + jnp.arange(rep_dev, dtype=jnp.int32)
+    mate_ids = lax.dynamic_slice_in_dim(partners, first_slot, rep_dev)
     all_ids = jnp.arange(partners.shape[0], dtype=jnp.int32)[None, :]
 
     def picked(values, ids):
         return jnp.sum(jnp.where(ids[:, None] == all_ids, values[None, :], 0.0), axis=1)
 
-    all_betas = beta_steps.astype(jnp.float32)
     beta_gap = picked(all_betas, slot_ids) - picked(all_betas, mate_ids)
     noise = picked(swap_noise, jnp.minimum(slot_ids, mate_ids))
     mate_rows_of = (mate_ids[:, None] == all_ids).astype(jnp.bfloat16)
-    start_rows, beta_gap, noise, mate_rows_of = lax.optimization_barrier(
-        (start_rows, beta_gap, noise, mate_rows_of)
-    )
-    start_rows = start_rows.transpose(1, 0, 2).reshape(rep_dev, -1)
-    partial = jnp.dot(start_rows, own_block, preferred_element_type=jnp.float32)
+    terms, beta_gap, noise, mate_rows_of = lax.optimization_barrier(
+        (terms, beta_gap, noise, mate_rows_of)
+    )
+
+    def own_piece(value):
+        return lax.dynamic_slice_in_dim(value, y_index * piece, piece, value.ndim - 1)
+
+    limit = jnp.where(own_piece(colors)[None, :] == 0, own_piece(flip_noise[0]), NEVER)
+    fields = terms.astype(jnp.float32).sum(axis=0)
+    own_spins = own_piece(spin_init).astype(jnp.float32)
+    own_spins = metropolis(own_spins, fields, limit, first_slot)
+
+    rows = sent_to_all(own_spins.astype(jnp.bfloat16), ("xl", "z"))
+    rows = rows.transpose(1, 0, 2).reshape(rep_dev, -1)
+    partial = jnp.dot(rows, own_block, preferred_element_type=jnp.float32)
+    partial = jnp.concatenate(
+        [partial, own_spins, jnp.zeros((rep_dev, 128 - piece), jnp.float32)], axis=1
+    )
     partial = lax.all_to_all(
-        partial.reshape(n_xl * n_y, share, row_width), PLANE, 0, 0, tiled=True
-    )
-    fields = partial.reshape(n_xl, n_y, share, row_width).sum(axis=1)
+        partial.reshape(n_xl * n_y, share, row_width + 128), PLANE, 0, 0, tiled=True
+    )
+    fields = partial[:, :, :row_width].reshape(n_xl, n_y, share, row_width).sum(axis=1)
     fields = fields.transpose(1, 0, 2).reshape(share, width)
-
-    steps = jnp.arange(SWEEPS, dtype=jnp.int32)[:, None, None]
-
-    def start_of(xl):
+    spins = partial[:, :, row_width : row_width + piece]
+    spins = spins.transpose(1, 0, 2).reshape(share, width)
+
+    steps = jnp.arange(1, SWEEPS, dtype=jnp.int32)[:, None, None]
+
+    def limits_of(xl):
         first = (xl * n_y + y_index) * share
-        noise = lax.dynamic_slice_in_dim(flip_noise, first, share, 1)
-        limits = jnp.where(colors[None, None, :] == steps % 2, noise, NEVER)
-        spins = lax.dynamic_slice_in_dim(spin_init, first, share, 0)
-        return jnp.concatenate([spins.astype(jnp.float32)[None], limits], axis=0)
-
-    kept = start_of(xl_index)
-    other = lax.ppermute(start_of(1 - xl_index), "xl", [(0, 1), (1, 0)])
+        noise = lax.dynamic_slice_in_dim(flip_noise, first, share, 1)[1:]
+        return jnp.where(colors[None, None, :] == steps % 2, noise, NEVER)
+
+    kept = limits_of(xl_index)
+    other = lax.ppermute(limits_of(1 - xl_index), "xl", [(0, 1), (1, 0)])
     is_left = xl_index == 0
-    both = jnp.concatenate(
+    limits = jnp.concatenate(
         [jnp.where(is_left, kept, other), jnp.where(is_left, other, kept)], axis=2
     )
-    spins = both[0]
-    limits = both[1:]
-    first_slot = rep_index * rep_dev + lax.axis_index(PLANE) * share
-    beta_col = lax.dynamic_slice_in_dim(beta_steps, first_slot, share).astype(jnp.float32)
-    beta_col = beta_col[:, None] * (1.0 / 16384.0)
-
-    def metropolis(spins, fields, limit):
-        energy_cost = beta_col * (spins * fields)
-        return jnp.where(energy_cost < limit, -spins, spins)
+    own_slot = first_slot + lax.axis_index(PLANE) * share
 
     def layer_rows(spins):
         return sent_to_all(spins.astype(jnp.bfloat16), "z")
@@ -134,13 +150,14 @@
         halves = [jnp.dot(rows, half, preferred_element_type=jnp.float32) for half in layer_block]
         return jnp.concatenate(halves, axis=1)
 
-    spins = metropolis(spins, fields, limits[0])
+    spins = metropolis(spins, fields, limits[0], own_slot)
     rows, gathered = lax.optimization_barrier((layer_rows(spins), gathered))
     layer_block = in_spin_order(
         gathered.reshape(n_core, n_xl, n_y, n_z, piece, row_width)
     )
-    for step in range(1, SWEEPS):
-        spins = metropolis(spins, layer_fields(rows, layer_block), limits[step])
+    for limit in limits[1:]:
+        spins = metropolis(spins, layer_fields(rows, layer_block), limit, own_slot)
+        spins = lax.optimization_barrier(spins)
         rows = layer_rows(spins)
 
     layer_sum = jnp.sum(spins * layer_fields(rows, layer_block), axis=1, keepdims=True)
@@ -161,7 +178,7 @@
     ).reshape(-1, *blocks.shape[1:])
     table = lax.all_to_all(blocks, LAYER, 0, 0, tiled=True).reshape(-1, row_width + 128)
 
-    own_rows = lax.dynamic_slice_in_dim(table, rep_index * rep_dev, rep_dev, 0)
+    own_rows = lax.dynamic_slice_in_dim(table, first_slot, rep_dev, 0)
     own_rows = own_rows.astype(jnp.float32)
     mate_rows = jnp.dot(mate_rows_of, table, preferred_element_type=jnp.float32)
 

time: 305 us -> 302 us (level)
  blocking collectives: 197 us -> 154 us
  waiting for transfers between devices: 31.6 us -> 62.7 us
  starting transfers between devices: 28.4 us -> 39.8 us
  other arithmetic: 8.57 us -> 4.16 us
    all_to_all x10 -> x8, blocking collectives: 174 us -> 126 us  [sent_to_all(): lax.all_to_all(jnp.broadcast_to(value[None], (length, *value.shape)), axe...]
    all_to_all x1 -> x2, waiting for transfers between devices: 5.61 us -> 24.5 us  [the longest x1 19.2 us: per_device(): terms = lax.all_to_all(terms, ('xl', 'z'), 0, 0, tiled=True)]
    all_to_all x1 -> x2, starting transfers between devices: 4.28 us -> 21.3 us  [the longest x1 16.9 us: per_device(): terms = lax.all_to_all(terms, ('xl', 'z'), 0, 0, tiled=True)]
    all_to_all x2 -> x3, waiting for transfers between devices: 22.4 us -> 38.2 us  [sent_to_all(): lax.all_to_all(jnp.broadcast_to(value[None], (length, *value.shape)), axe...]
    all_to_all x2 -> x3, starting transfers between devices: 20.9 us -> 15.3 us  [sent_to_all(): lax.all_to_all(jnp.broadcast_to(value[None], (length, *value.shape)), axe...]
    all_to_all x1, blocking collectives: 23.4 us -> 28.7 us  [per_device(): lax.all_to_all(blocks, LAYER, 0, 0, tiled=True).reshape(-1, row_width + 128)]
    all_gather x1, waiting for transfers between devices: 3.61 us -> 0.01 us  [per_device(): gathered = lax.all_gather(core_part, ('core', *PLANE))]
    dot_general x20 -> x18, matrix products: 13 us -> 11.7 us  [layer_fields(): jnp.dot(rows, half, preferred_element_type=jnp.float32)]
  transfers between devices with their start and end apart: 5 -> 7, of which waited for: 4 -> 5; matrix products, arithmetic and copies ran while one was open for 3% -> 3% of each run, Pallas kernels for 0% -> 0%
where the time goes in v3:
time: 302 us; the launch traced here: 301 us
  blocking collectives  154 us (51%)
  waiting for transfers between devices  62.7 us (21%)
  starting transfers between devices  39.8 us (13%)
  between operations  14.5 us (5%)
  matrix products  13.4 us (4%)
  local copies, waits for them, and re-layouts  8.62 us (3%)
  other arithmetic  4.16 us (1%)
  Pallas kernels  3.51 us (1%)
    all_to_all x8, blocking collectives, sent_to_all(): lax.all_to_all(jnp.broadcast_to(value[None], (length, *value.shape)), axe...  126 us
    all_to_all x3, waiting for transfers between devices, sent_to_all(): lax.all_to_all(jnp.broadcast_to(value[None], (length, *value.shape)), axe...  38.2 us
    all_to_all x1, blocking collectives, per_device(): lax.all_to_all(blocks, LAYER, 0, 0, tiled=True).reshape(-1, row_width + 128)  28.7 us
    all_to_all x1, waiting for transfers between devices, per_device(): terms = lax.all_to_all(terms, ('xl', 'z'), 0, 0, tiled=True)  19.2 us
    all_to_all x1, starting transfers between devices, per_device(): terms = lax.all_to_all(terms, ('xl', 'z'), 0, 0, tiled=True)  16.9 us
    all_to_all x3, starting transfers between devices, sent_to_all(): lax.all_to_all(jnp.broadcast_to(value[None], (length, *value.shape)), axe...  15.3 us
    dot_general x18, matrix products, layer_fields(): jnp.dot(rows, half, preferred_element_type=jnp.float32)  11.7 us
  transfers between devices with their start and end apart: 7, of which 5 were waited for; matrix products, arithmetic and copies ran while one was open for 3% of the time, Pallas kernels for 0%

profile of v3, /device:TPU:1, one launch (start us, length us, event | category | flops | bytes accessed | tf_op | source)
XLA Modules:
  0.0 301.0 jit_solution(1986392725668662955)
XLA Ops:
  7.3 1.2 copy-done
  8.5 0.9 constant_dynamic-slice_fusion
  9.4 1.3 convolution_convert_fusion
  10.6 0.5 reshape.227
  11.1 0.2 copy.22
  11.3 1.1 reshape.253
  12.5 16.9 %all-to-all-start = ((bf16[32,2,2048]{2,1,0:T(2,128)(2,1)}), bf16[32,2,2048]{2,1,0:T(2,128)(2,1)S(1)}, u32[]{:S(2)}, u32[]{:S(2)}) async-start(bf16[32,2,2048]{2,1,0:T(2,128)(2,1)} %reshape.253), calls=%async_computation | async-start | bytes 524288 | tf_op jit(solution)/shard_map/all_to_all | solution.py:92
  29.6 0.2 select_reduce_fusion.1
  29.9 0.2 select_reduce_fusion
  30.2 19.2 %all-to-all-done = bf16[32,2,2048]{2,1,0:T(2,128)(2,1)S(1)} async-done(((bf16[32,2,2048]{2,1,0:T(2,128)(2,1)}), bf16[32,2,2048]{2,1,0:T(2,128)(2,1)S(1)}, u32[]{:S(2)}, u32[]{:S(2)}) %all-to-all-start) | async-done | bytes 262176 | tf_op jit(solution)/shard_map/all_to_all | solution.py:92
  49.4 0.4 reshape.254
  49.8 0.1 convert_reduce_fusion
  50.0 0.1 broadcast_in_dim.90
  50.1 1.1 reshape.255
  51.3 5.0 %all-to-all-start.1 = ((bf16[32,2,2048]{2,1,0:T(2,128)(2,1)}), bf16[32,2,2048]{2,1,0:T(2,128)(2,1)S(1)}, u32[]{:S(2)}, u32[]{:S(2)}) async-start(bf16[32,2,2048]{2,1,0:T(2,128)(2,1)} %reshape.255), calls=%async_computation.1 | async-start | bytes 524288 | tf_op jit(solution)/shard_map/all_to_all | solution.py:21
  56.4 3.1 %collective-permute-start = (f32[9,8,256]{2,1,0:T(8,128)S(1)}, f32[9,8,256]{2,1,0:T(8,128)S(1)}, u32[]{:S(2)}, u32[]{:S(2)}) collective-permute-start(f32[9,8,256]{2,1,0:T(8,128)S(1)} %dynamic-slice_select_fusion), channel_id=1, source_target_pairs={{0,64},{64,0},{1,65},{65,1},{2,66},{66,2},{3,67},{67,3},{4,68},{68... | collective-permute-start | bytes 221192 | tf_op jit(solution)/shard_map/ppermute | solution.py:138
  59.8 15.0 %all-to-all-done.1 = bf16[32,2,2048]{2,1,0:T(2,128)(2,1)S(1)} async-done(((bf16[32,2,2048]{2,1,0:T(2,128)(2,1)}), bf16[32,2,2048]{2,1,0:T(2,128)(2,1)S(1)}, u32[]{:S(2)}, u32[]{:S(2)}) %all-to-all-start.1) | async-done | bytes 262176 | tf_op jit(solution)/shard_map/all_to_all | solution.py:21
  74.8 0.4 reshape.256
  75.1 0.3 copy.18
  75.5 0.5 reshape.228
  75.9 0.3 fusion.51
  76.2 0.6 maximum_bitcast_fusion
  76.9 4.4 %all-to-all-start.2 = ((f32[8,8,384]{2,1,0:T(8,128)}), f32[8,8,384]{2,1,0:T(8,128)S(1)}, u32[]{:S(2)}, u32[]{:S(2)}) async-start(f32[8,8,384]{2,1,0:T(8,128)} %maximum_bitcast_fusion), calls=%async_computation.2 | async-start | bytes 196608 | tf_op jit(solution)/shard_map/all_to_all | solution.py:122
  81.3 5.2 %all-to-all-done.2 = f32[8,8,384]{2,1,0:T(8,128)S(1)} async-done(((f32[8,8,384]{2,1,0:T(8,128)}), f32[8,8,384]{2,1,0:T(8,128)S(1)}, u32[]{:S(2)}, u32[]{:S(2)}) %all-to-all-start.2) | async-done | bytes 98336 | tf_op jit(solution)/shard_map/all_to_all | solution.py:122
  86.8 0.7 broadcast_in_dim.95
  87.4 6.6 %all-to-all-start.3 = ((bf16[16,8,512]{2,1,0:T(8,128)(2,1)}), bf16[16,8,512]{2,1,0:T(8,128)(2,1)S(1)}, u32[]{:S(2)}, u32[]{:S(2)}) async-start(bf16[16,8,512]{2,1,0:T(8,128)(2,1)} %broadcast_in_dim.95), calls=%async_computation.3 | async-start | bytes 262144 | tf_op jit(solution)/shard_map/all_to_all | solution.py:21
  94.1 11.9 %all-to-all-done.3 = bf16[16,8,512]{2,1,0:T(8,128)(2,1)S(1)} async-done(((bf16[16,8,512]{2,1,0:T(8,128)(2,1)}), bf16[16,8,512]{2,1,0:T(8,128)(2,1)S(1)}, u32[]{:S(2)}, u32[]{:S(2)}) %all-to-all-start.3) | async-done | bytes 131104 | tf_op jit(solution)/shard_map/all_to_all | solution.py:21
  106.0 3.5 %in_spin_order.1 = (bf16[16,8,64,256]{3,2,1,0:T(8,128)(2,1)S(1)}, bf16[16,8,64,256]{3,2,1,0:T(8,128)(2,1)S(1)}) custom-call(bf16[2,2,4,16,64,256]{5,4,3,2,1,0:T(8,128)(2,1)} %bitcast.178), custom_call_target="tpu_custom_call" | custom-call | tf_op jit(solution)/shard_map/in_spin_order/pallas_call | solution.py:47
  109.5 0.6 fusion.53
  110.1 0.7 fusion.52
  110.9 15.8 %all_to_all.70 = bf16[16,8,512]{2,1,0:T(8,128)(2,1)S(1)} all-to-all(bf16[16,8,512]{2,1,0:T(8,128)(2,1)S(1)} %broadcast_in_dim.96), channel_id=1, replica_groups=mesh['xh'=2,'core'=2,'xl'=2,'z'=16,'y'=4] {'z'}, dimensions={0} | all-to-all | bytes 262144 | tf_op jit(solution)/shard_map/all_to_all | solution.py:21
  126.7 0.6 fusion.55
  127.3 0.7 fusion.54
  128.1 15.9 %all_to_all.71 = bf16[16,8,512]{2,1,0:T(8,128)(2,1)S(1)} all-to-all(bf16[16,8,512]{2,1,0:T(8,128)(2,1)S(1)} %broadcast_in_dim.97), channel_id=1, replica_groups=mesh['xh'=2,'core'=2,'xl'=2,'z'=16,'y'=4] {'z'}, dimensions={0} | all-to-all | bytes 262144 | tf_op jit(solution)/shard_map/all_to_all | solution.py:21
  144.0 0.6 fusion.57
  144.6 0.7 fusion.56
  145.4 15.8 %all_to_all.72 = bf16[16,8,512]{2,1,0:T(8,128)(2,1)S(1)} all-to-all(bf16[16,8,512]{2,1,0:T(8,128)(2,1)S(1)} %broadcast_in_dim.98), channel_id=1, replica_groups=mesh['xh'=2,'core'=2,'xl'=2,'z'=16,'y'=4] {'z'}, dimensions={0} | all-to-all | bytes 262144 | tf_op jit(solution)/shard_map/all_to_all | solution.py:21
  161.2 0.6 fusion.59
  161.9 0.7 fusion.58
  162.6 15.8 %all_to_all.73 = bf16[16,8,512]{2,1,0:T(8,128)(2,1)S(1)} all-to-all(bf16[16,8,512]{2,1,0:T(8,128)(2,1)S(1)} %broadcast_in_dim.99), channel_id=1, replica_groups=mesh['xh'=2,'core'=2,'xl'=2,'z'=16,'y'=4] {'z'}, dimensions={0} | all-to-all | bytes 262144 | tf_op jit(solution)/shard_map/all_to_all | solution.py:21
  178.4 0.6 fusion.61
  179.1 0.7 fusion.60
  179.8 15.7 %all_to_all.74 = bf16[16,8,512]{2,1,0:T(8,128)(2,1)S(1)} all-to-all(bf16[16,8,512]{2,1,0:T(8,128)(2,1)S(1)} %broadcast_in_dim.100), channel_id=1, replica_groups=mesh['xh'=2,'core'=2,'xl'=2,'z'=16,'y'=4] {'z'}, dimensions={0} | all-to-all | bytes 262144 | tf_op jit(solution)/shard_map/all_to_all | solution.py:21
  195.5 0.6 fusion.63
  196.2 0.7 fusion.62
  196.9 15.6 %all_to_all.75 = bf16[16,8,512]{2,1,0:T(8,128)(2,1)S(1)} all-to-all(bf16[16,8,512]{2,1,0:T(8,128)(2,1)S(1)} %broadcast_in_dim.178), channel_id=1, replica_groups=mesh['xh'=2,'core'=2,'xl'=2,'z'=16,'y'=4] {'z'}, dimensions={0} | all-to-all | bytes 262144 | tf_op jit(solution)/shard_map/all_to_all | solution.py:21
  212.6 0.6 fusion.65
  213.2 0.7 fusion.64
  214.0 15.4 %all_to_all.76 = bf16[16,8,512]{2,1,0:T(8,128)(2,1)S(1)} all-to-all(bf16[16,8,512]{2,1,0:T(8,128)(2,1)S(1)} %broadcast_in_dim.179), channel_id=1, replica_groups=mesh['xh'=2,'core'=2,'xl'=2,'z'=16,'y'=4] {'z'}, dimensions={0} | all-to-all | bytes 262144 | tf_op jit(solution)/shard_map/all_to_all | solution.py:21
  229.4 0.6 fusion.67
  230.0 0.7 fusion.66
  230.8 15.6 %all_to_all.77 = bf16[16,8,512]{2,1,0:T(8,128)(2,1)S(1)} all-to-all(bf16[16,8,512]{2,1,0:T(8,128)(2,1)S(1)} %broadcast_in_dim.180), channel_id=1, replica_groups=mesh['xh'=2,'core'=2,'xl'=2,'z'=16,'y'=4] {'z'}, dimensions={0} | all-to-all | bytes 262144 | tf_op jit(solution)/shard_map/all_to_all | solution.py:21
  246.4 0.6 fusion.69
  247.0 0.7 fusion.68
  247.7 0.1 fusion.43
  247.8 0.7 broadcast_in_dim_broadcast_in_dim_broadcast_in_dim.2
  248.5 3.7 %all-to-all-start.12 = ((f32[16,8,128]{2,1,0:T(8,128)}), f32[16,8,128]{2,1,0:T(8,128)S(1)}, u32[]{:S(2)}, u32[]{:S(2)}) async-start(f32[16,8,128]{2,1,0:T(8,128)} %broadcast_in_dim_broadcast_in_dim_broadcast_in_dim.2), calls=%async_computation.12 | async-start | bytes 131072 | tf_op jit(solution)/shard_map/all_to_all | solution.py:21
  252.3 11.3 %all-to-all-done.12 = f32[16,8,128]{2,1,0:T(8,128)S(1)} async-done(((f32[16,8,128]{2,1,0:T(8,128)}), f32[16,8,128]{2,1,0:T(8,128)S(1)}, u32[]{:S(2)}, u32[]{:S(2)}) %all-to-all-start.12) | async-done | bytes 65568 | tf_op jit(solution)/shard_map/all_to_all | solution.py:21
  263.7 28.7 %all_to_all.78 = bf16[32,8,384]{2,1,0:T(8,128)(2,1)S(1)} all-to-all(bf16[32,8,384]{2,1,0:T(8,128)(2,1)S(1)} %bitcast.200), channel_id=1, replica_groups=mesh['xh'=2,'core'=2,'xl'=2,'z'=16,'y'=4] {'xh','core','xl','y'}, dimensions={0} | all-to-all | bytes 393216 | tf_op jit(solution)/shard_map/all_to_all | solution.py:179
  292.4 0.2 fusion.47
  292.5 0.2 fusion.7
  292.7 0.2 fusion.9
  292.9 0.5 select_multiply_fusion
  293.4 0.7 fusion
  (73 shorter events, 2.0 us)
Async XLA Ops:
  7.2 1.3 copy-start
  7.2 42.7 %copy-start.2 = (bf16[64,256]{1,0:T(8,128)(2,1)S(1)}, bf16[64,256]{1,0:T(8,128)(2,1)}, u32[]{:S(2)}) copy-start(bf16[64,256]{1,0:T(8,128)(2,1)} %param.7) | copy-start | bytes 98308
  7.2 42.7 %slice-start = ((f32[10,64,256]{2,1,0:T(8,128)}), f32[1,64,256]{2,1,0:T(8,128)S(1)}, s32[]{:S(2)}) async-start(f32[10,64,256]{2,1,0:T(8,128)} %param.9), calls=%async_computation.15 | async-start | bytes 131072 | tf_op jit(solution)/shard_map/slice | solution.py:111
  7.2 22.2 %copy-start.3 = (s32[256]{0:T(256)S(1)}, s32[256]{0:T(256)}, u32[]{:S(2)}) copy-start(s32[256]{0:T(256)} %param.11) | copy-start | bytes 3076
  7.2 22.3 %copy-start.6 = (s32[256]{0:T(256)S(1)}, s32[256]{0:T(256)}, u32[]{:S(2)}) copy-start(s32[256]{0:T(256)} %param.12) | copy-start | bytes 3076
  7.2 22.6 %copy-start.5 = (s32[256]{0:T(256)S(1)}, s32[256]{0:T(256)}, u32[]{:S(2)}) copy-start(s32[256]{0:T(256)} %param.10) | copy-start | bytes 3076
  7.2 22.7 %copy-start.4 = (f32[256]{0:T(256)S(1)}, f32[256]{0:T(256)}, u32[]{:S(2)}) copy-start(f32[256]{0:T(256)} %param.13) | copy-start | bytes 3076
  7.2 98.7 %all-gather.2.cloned.1.call-start = ((), (), s32[]{:S(2)}) async-start(), calls=%async_computation.14 | async-start | bytes 8912896 | tf_op jit(solution)/shard_map/all_gather | solution.py:77
  9.3 47.1 %copy-start.1 = (f32[10,64,256]{2,1,0:T(8,128)S(1)}, f32[10,64,256]{2,1,0:T(8,128)}, u32[]{:S(2)}) copy-start(f32[10,64,256]{2,1,0:T(8,128)} %param.9) | copy-start | bytes 1966084
  12.5 36.9 %all-to-all-start = ((bf16[32,2,2048]{2,1,0:T(2,128)(2,1)}), bf16[32,2,2048]{2,1,0:T(2,128)(2,1)S(1)}, u32[]{:S(2)}, u32[]{:S(2)}) async-start(bf16[32,2,2048]{2,1,0:T(2,128)(2,1)} %reshape.253), calls=%async_computation | async-start | bytes 524288 | tf_op jit(solution)/shard_map/all_to_all | solution.py:92
  51.3 23.5 %all-to-all-start.1 = ((bf16[32,2,2048]{2,1,0:T(2,128)(2,1)}), bf16[32,2,2048]{2,1,0:T(2,128)(2,1)S(1)}, u32[]{:S(2)}, u32[]{:S(2)}) async-start(bf16[32,2,2048]{2,1,0:T(2,128)(2,1)} %reshape.255), calls=%async_computation.1 | async-start | bytes 524288 | tf_op jit(solution)/shard_map/all_to_all | solution.py:21
  56.4 24.9 %collective-permute-start = (f32[9,8,256]{2,1,0:T(8,128)S(1)}, f32[9,8,256]{2,1,0:T(8,128)S(1)}, u32[]{:S(2)}, u32[]{:S(2)}) collective-permute-start(f32[9,8,256]{2,1,0:T(8,128)S(1)} %dynamic-slice_select_fusion), channel_id=1, source_target_pairs={{0,64},{64,0},{1,65},{65,1},{2,66},{66,2},{3,67},{67,3},{4,68},{68... | collective-permute-start | bytes 221192 | tf_op jit(solution)/shard_map/ppermute | solution.py:138
  76.9 9.7 %all-to-all-start.2 = ((f32[8,8,384]{2,1,0:T(8,128)}), f32[8,8,384]{2,1,0:T(8,128)S(1)}, u32[]{:S(2)}, u32[]{:S(2)}) async-start(f32[8,8,384]{2,1,0:T(8,128)} %maximum_bitcast_fusion), calls=%async_computation.2 | async-start | bytes 196608 | tf_op jit(solution)/shard_map/all_to_all | solution.py:122
  87.4 18.5 %all-to-all-start.3 = ((bf16[16,8,512]{2,1,0:T(8,128)(2,1)}), bf16[16,8,512]{2,1,0:T(8,128)(2,1)S(1)}, u32[]{:S(2)}, u32[]{:S(2)}) async-start(bf16[16,8,512]{2,1,0:T(8,128)(2,1)} %broadcast_in_dim.95), calls=%async_computation.3 | async-start | bytes 262144 | tf_op jit(solution)/shard_map/all_to_all | solution.py:21
  248.5 15.0 %all-to-all-start.12 = ((f32[16,8,128]{2,1,0:T(8,128)}), f32[16,8,128]{2,1,0:T(8,128)S(1)}, u32[]{:S(2)}, u32[]{:S(2)}) async-start(f32[16,8,128]{2,1,0:T(8,128)} %broadcast_in_dim_broadcast_in_dim_broadcast_in_dim.2), calls=%async_computation.12 | async-start | bytes 131072 | tf_op jit(solution)/shard_map/all_to_all | solution.py:21
Sparse Core Ops, SparseCore 0:
  10.2 72.1 all-gather.1

commit v4 on v3

--- a/solution.py
+++ b/solution.py
@@ -23,37 +23,28 @@
     )
 
 
-def in_spin_order(gathered):
-    n_core, n_xl, n_y, n_z, piece, width = gathered.shape
-    shape = (n_z, n_core * n_y, piece, width)
-
-    def body(source, *rest):
-        halves, sems = rest[:n_xl], rest[n_xl]
+def placed(name, places, pieces, outs):
+    def body(scalars, *refs):
+        sources, targets, sems = refs[: len(pieces)], refs[len(pieces) : -1], refs[-1]
         copies = [
-            pltpu.make_async_copy(
-                source.at[core, xl, y],
-                halves[xl].at[:, core * n_y + y],
-                sems.at[core, xl, y],
-            )
-            for xl in range(n_xl)
-            for core in range(n_core)
-            for y in range(n_y)
+            pltpu.make_async_copy(sources[i].at[src], targets[o].at[index], sems.at[n])
+            for n, (i, src, o, index) in enumerate(places["of"](scalars))
         ]
         for copy in copies:
             copy.start()
         for copy in copies:
             copy.wait()
 
-    halves = pl.pallas_call(
+    return pl.pallas_call(
         body,
-        in_specs=[pl.BlockSpec(memory_space=pltpu.HBM)],
-        out_specs=[pl.BlockSpec(memory_space=pl.ANY)] * n_xl,
-        out_shape=[jax.ShapeDtypeStruct(shape, gathered.dtype)] * n_xl,
-        scratch_shapes=[pltpu.SemaphoreType.DMA((n_core, n_xl, n_y))],
+        in_specs=[pl.BlockSpec(memory_space=pltpu.SMEM)]
+        + [pl.BlockSpec(memory_space=pl.ANY)] * len(pieces),
+        out_specs=[pl.BlockSpec(memory_space=pl.ANY)] * len(outs),
+        out_shape=[jax.ShapeDtypeStruct(shape, jnp.bfloat16) for shape in outs],
+        scratch_shapes=[pltpu.SemaphoreType.DMA((places["count"],))],
         compiler_params=pltpu.CompilerParams(vmem_limit_bytes=2 * 1024 * 1024),
-        name="in_spin_order",
-    )(pltpu.with_memory_space_constraint(gathered, pltpu.HBM))
-    return [half.reshape(-1, width) for half in halves]
+        name=name,
+    )(places["scalars"], *pieces)
 
 
 def per_device(spin_init, couplings, flip_noise, colors, beta_steps, partners, swap_noise):
@@ -71,11 +62,6 @@
     width = n_xl * row_width
     own_block = couplings.reshape(-1, row_width)
 
-    core_part = lax.dynamic_slice_in_dim(
-        couplings.reshape(n_core, -1, row_width), core_index, 1, 0
-    )[0]
-    gathered = lax.all_gather(core_part, ("core", *PLANE))
-
     first_slot = rep_index * rep_dev
     all_betas = beta_steps.astype(jnp.float32)
     all_scales = all_betas * (1.0 / 16384.0)
@@ -91,6 +77,21 @@
     terms = terms.astype(jnp.bfloat16).reshape(rep_dev, -1, piece).transpose(1, 0, 2)
     terms = lax.all_to_all(terms, ("xl", "z"), 0, 0, tiled=True)
 
+    def ring(value, shift):
+        return lax.ppermute(value, "y", [(i, (i + shift) % n_y) for i in range(n_y)])
+
+    def swapped(value, axis):
+        return lax.ppermute(value, axis, [(0, 1), (1, 0)])
+
+    near = lax.dynamic_slice_in_dim(
+        couplings.reshape(n_core, n_z, piece, row_width), core_index, 1, 0
+    )[0]
+    near_below = ring(near, 1)
+    near_above = ring(near, -1)
+    far = swapped(near, "xl")
+    far_below = ring(far, 1)
+    far_above = ring(far, -1)
+
     slot_ids = first_slot + jnp.arange(rep_dev, dtype=jnp.int32)
     mate_ids = lax.dynamic_slice_in_dim(partners, first_slot, rep_dev)
     all_ids = jnp.arange(partners.shape[0], dtype=jnp.int32)[None, :]
@@ -101,8 +102,10 @@
     beta_gap = picked(all_betas, slot_ids) - picked(all_betas, mate_ids)
     noise = picked(swap_noise, jnp.minimum(slot_ids, mate_ids))
     mate_rows_of = (mate_ids[:, None] == all_ids).astype(jnp.bfloat16)
-    terms, beta_gap, noise, mate_rows_of = lax.optimization_barrier(
-        (terms, beta_gap, noise, mate_rows_of)
+    terms, beta_gap, noise, mate_rows_of, near_below, near_above, far = (
+        lax.optimization_barrier(
+            (terms, beta_gap, noise, mate_rows_of, near_below, near_above, far)
+        )
     )
 
     def own_piece(value):
@@ -114,6 +117,9 @@
     own_spins = metropolis(own_spins, fields, limit, first_slot)
 
     rows = sent_to_all(own_spins.astype(jnp.bfloat16), ("xl", "z"))
+    near_across = ring(near_below, 1)
+    far_across = ring(far_above, -1)
+    rows, near_across, far_across = lax.optimization_barrier((rows, near_across, far_across))
     rows = rows.transpose(1, 0, 2).reshape(rep_dev, -1)
     partial = jnp.dot(rows, own_block, preferred_element_type=jnp.float32)
     partial = jnp.concatenate(
@@ -122,10 +128,37 @@
     partial = lax.all_to_all(
         partial.reshape(n_xl * n_y, share, row_width + 128), PLANE, 0, 0, tiled=True
     )
+    core_block = (n_z, n_y, piece, row_width)
+
+    def by_y(scalars):
+        here = scalars[0]
+        shifts = (0, n_y - 1, 1, 2)
+        return [
+            (side * n_y + n, pl.ds(0, n_z), 0, (side, pl.ds(0, n_z), (here + shift) % n_y))
+            for side in range(n_xl)
+            for n, shift in enumerate(shifts)
+        ]
+
+    (core_half,) = placed(
+        "by_y",
+        {"of": by_y, "count": n_xl * n_y, "scalars": y_index[None]},
+        [near, near_below, near_above, near_across, far, far_below, far_above, far_across],
+        [(n_xl, *core_block)],
+    )
+    other_half = swapped(core_half, "core")
+
+    is_left = xl_index == 0
+
+    def own_first(left, right):
+        return jnp.concatenate(
+            [jnp.where(is_left, left, right), jnp.where(is_left, right, left)], axis=-1
+        )
+
     fields = partial[:, :, :row_width].reshape(n_xl, n_y, share, row_width).sum(axis=1)
-    fields = fields.transpose(1, 0, 2).reshape(share, width)
+    fields = own_first(fields[0], fields[1])
     spins = partial[:, :, row_width : row_width + piece]
     spins = spins.transpose(1, 0, 2).reshape(share, width)
+    spins = own_first(spins[:, :row_width], spins[:, row_width:])
 
     steps = jnp.arange(1, SWEEPS, dtype=jnp.int32)[:, None, None]
 
@@ -135,11 +168,7 @@
         return jnp.where(colors[None, None, :] == steps % 2, noise, NEVER)
 
     kept = limits_of(xl_index)
-    other = lax.ppermute(limits_of(1 - xl_index), "xl", [(0, 1), (1, 0)])
-    is_left = xl_index == 0
-    limits = jnp.concatenate(
-        [jnp.where(is_left, kept, other), jnp.where(is_left, other, kept)], axis=2
-    )
+    limits = jnp.concatenate([kept, swapped(limits_of(1 - xl_index), "xl")], axis=2)
     own_slot = first_slot + lax.axis_index(PLANE) * share
 
     def layer_rows(spins):
@@ -151,13 +180,35 @@
         return jnp.concatenate(halves, axis=1)
 
     spins = metropolis(spins, fields, limits[0], own_slot)
-    rows, gathered = lax.optimization_barrier((layer_rows(spins), gathered))
-    layer_block = in_spin_order(
-        gathered.reshape(n_core, n_xl, n_y, n_z, piece, row_width)
-    )
+    rows, core_half, other_half = lax.optimization_barrier(
+        (layer_rows(spins), core_half, other_half)
+    )
+
+    def by_core(scalars):
+        mine = scalars[0]
+        return [
+            (source, side, side, (pl.ds(0, n_z), (mine + source) % n_core))
+            for source in range(n_core)
+            for side in range(n_xl)
+        ]
+
+    layer_block = placed(
+        "by_core",
+        {"of": by_core, "count": n_core * n_xl, "scalars": (core_index ^ xl_index)[None]},
+        [core_half, other_half],
+        [(n_z, n_core, *core_block[1:])] * n_xl,
+    )
+    layer_block = [half.reshape(N, row_width) for half in layer_block]
+
+    def final_blocks(spins):
+        left_right = own_first(spins[:, :row_width], spins[:, row_width:])
+        left_right = left_right.astype(jnp.bfloat16).reshape(share, n_xl, row_width)
+        return left_right.transpose(1, 0, 2)
+
     for limit in limits[1:]:
         spins = metropolis(spins, layer_fields(rows, layer_block), limit, own_slot)
-        spins = lax.optimization_barrier(spins)
+        final_spins = final_blocks(spins)
+        spins, final_spins = lax.optimization_barrier((spins, final_spins))
         rows = layer_rows(spins)
 
     layer_sum = jnp.sum(spins * layer_fields(rows, layer_block), axis=1, keepdims=True)
@@ -170,9 +221,8 @@
     terms = jnp.concatenate(
         [high[:, :1], middle[:, :1], low[:, :1], jnp.zeros((share, 125), jnp.float32)], axis=1
     )
-    blocks = spins.astype(jnp.bfloat16).reshape(share, n_xl, row_width).transpose(1, 0, 2)
     terms = jnp.broadcast_to(terms.astype(jnp.bfloat16)[None], (n_xl, share, 128))
-    blocks = jnp.concatenate([blocks, terms], axis=2)
+    blocks = jnp.concatenate([final_spins, terms], axis=2)
     blocks = jnp.broadcast_to(
         blocks[None, :, None], (lax.axis_size(GROUP), n_xl, n_y, *blocks.shape[1:])
     ).reshape(-1, *blocks.shape[1:])

time: 302 us -> 389 us (1.29)
  Pallas kernels: 3.51 us -> 68.2 us
  starting transfers between devices: 39.8 us -> 77.5 us
  between operations: 14.5 us -> 1.12 us
  waiting for transfers between devices: 62.7 us -> 51.6 us
    pallas_call x1 -> x2, Pallas kernels: 3.51 us -> 68.2 us  [placed(): pl.pallas_call(body, in_specs=[pl.BlockSpec(memory_space=pltpu.SMEM)] + [...]
    ppermute x1 -> x9, starting transfers between devices: 3.15 us -> 31.1 us  [the longest x6 19.2 us: ring(): lax.ppermute(value, 'y', [(i, (i + shift) % n_y) for i in range(n_y)])]
    all_to_all x1, waiting for transfers between devices: 19.2 us -> 0.01 us  [per_device(): terms = lax.all_to_all(terms, ('xl', 'z'), 0, 0, tiled=True)]
    ppermute x1 -> x9, waiting for transfers between devices: 0.01 us -> 17.6 us  [the longest x3 11.6 us: swapped(): return lax.ppermute(value, axis, [(0, 1), (1, 0)])]
    all_to_all x3, starting transfers between devices: 15.3 us -> 26.1 us  [sent_to_all(): lax.all_to_all(jnp.broadcast_to(value[None], (length, *value.shape)), axe...]
    all_to_all x3, waiting for transfers between devices: 38.2 us -> 33 us  [sent_to_all(): lax.all_to_all(jnp.broadcast_to(value[None], (length, *value.shape)), axe...]
    all_to_all x8, blocking collectives: 126 us -> 130 us  [sent_to_all(): lax.all_to_all(jnp.broadcast_to(value[None], (length, *value.shape)), axe...]
    all_to_all x1, waiting for transfers between devices: 5.25 us -> 0.89 us  [per_device(): lax.all_to_all(partial.reshape(n_xl * n_y, share, row_width + 128), PLANE...]
  transfers between devices with their start and end apart: 7 -> 14, of which waited for: 5 -> 7; matrix products, arithmetic and copies ran while one was open for 3% -> 4% of each run, Pallas kernels for 0% -> 0%
where the time goes in v4:
time: 389 us; the launch traced here: 388 us
  blocking collectives  156 us (40%)
  starting transfers between devices  77.5 us (20%)
  Pallas kernels  68.2 us (18%)
  waiting for transfers between devices  51.6 us (13%)
  matrix products  13.4 us (3%)
  local copies, waits for them, and re-layouts  12.3 us (3%)
  other arithmetic  7.98 us (2%)
    all_to_all x8, blocking collectives, sent_to_all(): lax.all_to_all(jnp.broadcast_to(value[None], (length, *value.shape)), axe...  130 us
    pallas_call x2, Pallas kernels, placed(): pl.pallas_call(body, in_specs=[pl.BlockSpec(memory_space=pltpu.SMEM)] + [...  68.2 us
    all_to_all x3, waiting for transfers between devices, sent_to_all(): lax.all_to_all(jnp.broadcast_to(value[None], (length, *value.shape)), axe...  33 us
    all_to_all x3, starting transfers between devices, sent_to_all(): lax.all_to_all(jnp.broadcast_to(value[None], (length, *value.shape)), axe...  26.1 us
    all_to_all x1, blocking collectives, per_device(): lax.all_to_all(blocks, LAYER, 0, 0, tiled=True).reshape(-1, row_width + 128)  25.4 us
    ppermute x6, starting transfers between devices, ring(): lax.ppermute(value, 'y', [(i, (i + shift) % n_y) for i in range(n_y)])  19.2 us
    all_to_all x1, starting transfers between devices, per_device(): terms = lax.all_to_all(terms, ('xl', 'z'), 0, 0, tiled=True)  16.9 us
    ppermute x3, starting transfers between devices, swapped(): return lax.ppermute(value, axis, [(0, 1), (1, 0)])  11.9 us
  transfers between devices with their start and end apart: 14, of which 7 were waited for; matrix products, arithmetic and copies ran while one was open for 4% of the time, Pallas kernels for 0%

profile of v4, /device:TPU:1, one launch (start us, length us, event | category | flops | bytes accessed | tf_op | source)
XLA Modules:
  0.0 387.8 jit_solution(8200594432012698953)
XLA Ops:
  0.7 1.2 copy-done
  1.9 1.2 convolution_convert_fusion
  3.9 1.1 reshape.301
  5.0 16.9 %all-to-all-start = ((bf16[32,2,2048]{2,1,0:T(2,128)(2,1)}), bf16[32,2,2048]{2,1,0:T(2,128)(2,1)S(1)}, u32[]{:S(2)}, u32[]{:S(2)}) async-start(bf16[32,2,2048]{2,1,0:T(2,128)(2,1)} %reshape.301), calls=%async_computation | async-start | bytes 524288 | tf_op jit(solution)/shard_map/all_to_all | solution.py:78
  22.0 3.2 collective-permute-start
  25.2 3.4 collective-permute-start.1
  28.6 3.1 collective-permute-start.2
  33.5 10.3 %collective-permute-done.2.refs_4_ = bf16[16,64,256]{2,1,0:T(8,128)(2,1)S(1)} collective-permute-done((bf16[16,64,256]{2,1,0:T(8,128)(2,1)S(1)}, bf16[16,64,256]{2,1,0:T(8,128)(2,1)S(1)}, u32[]{:S(2)}, u32[]{:S(2)}) %collective-permute-start.2) | collective-permute-done | bytes 524320 | tf_op jit(solution)/shard_map/ppermute | solution.py:84
  43.9 4.2 %collective-permute-start.4 = (bf16[16,64,256]{2,1,0:T(8,128)(2,1)S(1)}, bf16[16,64,256]{2,1,0:T(8,128)(2,1)}, u32[]{:S(2)}, u32[]{:S(2)}) collective-permute-start(bf16[16,64,256]{2,1,0:T(8,128)(2,1)S(1)} %collective-permute-done.2.refs_4_), channel_id=1, source_target_pairs={{0,3},{1,0},{2,1},{3,2},{4,7},{5,4},{6,5},{7,6},{8,11},{9,8},{10,9... | collective-permute-start | bytes 1572872 | tf_op jit(solution)/shard_map/ppermute | solution.py:81
  48.1 1.2 reshape.302
  49.3 1.2 convert_reduce_fusion
  50.5 0.8 fusion.54
  51.3 0.9 broadcast_in_dim.94
  52.2 2.1 reshape.303
  54.3 11.0 %all-to-all-start.1 = ((bf16[32,2,2048]{2,1,0:T(2,128)(2,1)}), bf16[32,2,2048]{2,1,0:T(2,128)(2,1)S(1)}, u32[]{:S(2)}, u32[]{:S(2)}) async-start(bf16[32,2,2048]{2,1,0:T(2,128)(2,1)} %reshape.303), calls=%async_computation.1 | async-start | bytes 524288 | tf_op jit(solution)/shard_map/all_to_all | solution.py:21
  65.4 1.9 collective-permute-start.3
  67.3 4.6 %collective-permute-start.5 = (bf16[16,64,256]{2,1,0:T(8,128)(2,1)}, bf16[16,64,256]{2,1,0:T(8,128)(2,1)}, u32[]{:S(2)}, u32[]{:S(2)}) collective-permute-start(bf16[16,64,256]{2,1,0:T(8,128)(2,1)} %collective-permute-done.4.refs_6_), channel_id=1, source_target_pairs={{0,3},{1,0},{2,1},{3,2},{4,7},{5,4},{6,5},{7,6},{8,11},{9,8},{10,9... | collective-permute-start | bytes 1572872 | tf_op jit(solution)/shard_map/ppermute | solution.py:81
  71.9 1.9 collective-permute-start.7
  73.8 9.6 %all-to-all-done.1 = bf16[32,2,2048]{2,1,0:T(2,128)(2,1)S(1)} async-done(((bf16[32,2,2048]{2,1,0:T(2,128)(2,1)}), bf16[32,2,2048]{2,1,0:T(2,128)(2,1)S(1)}, u32[]{:S(2)}, u32[]{:S(2)}) %all-to-all-start.1) | async-done | bytes 262176 | tf_op jit(solution)/shard_map/all_to_all | solution.py:21
  83.4 1.2 reshape.304
  84.7 6.0 %collective-permute-done.7.refs_5_ = bf16[16,64,256]{2,1,0:T(8,128)(2,1)} collective-permute-done((bf16[16,64,256]{2,1,0:T(8,128)(2,1)S(1)}, bf16[16,64,256]{2,1,0:T(8,128)(2,1)}, u32[]{:S(2)}, u32[]{:S(2)}) %collective-permute-start.7) | collective-permute-done | bytes 524320 | tf_op jit(solution)/shard_map/ppermute | solution.py:81
  90.6 64.7 %by_y.1.refs_0_ = bf16[2,16,4,64,256]{4,3,2,1,0:T(8,128)(2,1)} custom-call(s32[1]{0:T(128)} %bitcast.15.scalars, bf16[16,64,256]{2,1,0:T(8,128)(2,1)S(1)} %dynamic-slice_bitcast_fusion.refs_0_, bf16[16,64,256]{2,1,0:T(8,128)(2,1)S(1)} %collective-permute-done.refs_1_, bf16[16,64,256]{2,1,0:T(8,128)(2,1)S(1)} %collective-permute-done.1.refs_2_, ...), custom_call_target="tpu_custom_call" | custom-call | tf_op jit(solution)/shard_map/by_y/pallas_call | solution.py:38
  155.4 5.4 %collective-permute-start.8 = (bf16[2,16,4,64,256]{4,3,2,1,0:T(8,128)(2,1)}, bf16[2,16,4,64,256]{4,3,2,1,0:T(8,128)(2,1)}, u32[]{:S(2)}, u32[]{:S(2)}) collective-permute-start(bf16[2,16,4,64,256]{4,3,2,1,0:T(8,128)(2,1)} %by_y.1.refs_0_), channel_id=1, source_target_pairs={{0,128},{128,0},{1,129},{129,1},{2,130},{130,2},{3,131},{131,3},{4... | collective-permute-start | bytes 12582920 | tf_op jit(solution)/shard_map/ppermute | solution.py:84
  161.0 1.4 copy.15
  163.1 0.7 maximum_bitcast_fusion
  163.8 3.4 all-to-all-start.2
  167.2 1.0 dynamic-slice_select_fusion.1
  168.1 3.3 collective-permute-start.6
  171.5 0.9 all-to-all-done.2
  172.5 1.3 collective-permute-done.6
  173.9 0.7 broadcast_in_dim.99
  174.6 11.3 %all-to-all-start.3 = ((bf16[16,8,512]{2,1,0:T(8,128)(2,1)}), bf16[16,8,512]{2,1,0:T(8,128)(2,1)S(1)}, u32[]{:S(2)}, u32[]{:S(2)}) async-start(bf16[16,8,512]{2,1,0:T(8,128)(2,1)} %broadcast_in_dim.99), calls=%async_computation.3 | async-start | bytes 262144 | tf_op jit(solution)/shard_map/all_to_all | solution.py:21
  185.9 12.0 %all-to-all-done.3 = bf16[16,8,512]{2,1,0:T(8,128)(2,1)S(1)} async-done(((bf16[16,8,512]{2,1,0:T(8,128)(2,1)}), bf16[16,8,512]{2,1,0:T(8,128)(2,1)S(1)}, u32[]{:S(2)}, u32[]{:S(2)}) %all-to-all-start.3) | async-done | bytes 131104 | tf_op jit(solution)/shard_map/all_to_all | solution.py:21
  197.9 3.5 by_core.1
  201.4 0.6 fusion.57
  202.0 0.7 fusion.56
  202.8 17.4 %all_to_all.70 = bf16[16,8,512]{2,1,0:T(8,128)(2,1)S(1)} all-to-all(bf16[16,8,512]{2,1,0:T(8,128)(2,1)S(1)} %broadcast_in_dim.102), channel_id=1, replica_groups=mesh['xh'=2,'core'=2,'xl'=2,'z'=16,'y'=4] {'z'}, dimensions={0} | all-to-all | bytes 262144 | tf_op jit(solution)/shard_map/all_to_all | solution.py:21
  220.1 0.6 fusion.59
  220.8 0.7 fusion.58
  221.5 17.1 %all_to_all.71 = bf16[16,8,512]{2,1,0:T(8,128)(2,1)S(1)} all-to-all(bf16[16,8,512]{2,1,0:T(8,128)(2,1)S(1)} %broadcast_in_dim.182), channel_id=1, replica_groups=mesh['xh'=2,'core'=2,'xl'=2,'z'=16,'y'=4] {'z'}, dimensions={0} | all-to-all | bytes 262144 | tf_op jit(solution)/shard_map/all_to_all | solution.py:21
  238.6 0.6 fusion.61
  239.3 0.7 fusion.60
  240.0 16.9 %all_to_all.72 = bf16[16,8,512]{2,1,0:T(8,128)(2,1)S(1)} all-to-all(bf16[16,8,512]{2,1,0:T(8,128)(2,1)S(1)} %broadcast_in_dim.183), channel_id=1, replica_groups=mesh['xh'=2,'core'=2,'xl'=2,'z'=16,'y'=4] {'z'}, dimensions={0} | all-to-all | bytes 262144 | tf_op jit(solution)/shard_map/all_to_all | solution.py:21
  256.9 0.6 fusion.63
  257.5 0.7 fusion.62
  258.3 15.8 %all_to_all.73 = bf16[16,8,512]{2,1,0:T(8,128)(2,1)S(1)} all-to-all(bf16[16,8,512]{2,1,0:T(8,128)(2,1)S(1)} %broadcast_in_dim.184), channel_id=1, replica_groups=mesh['xh'=2,'core'=2,'xl'=2,'z'=16,'y'=4] {'z'}, dimensions={0} | all-to-all | bytes 262144 | tf_op jit(solution)/shard_map/all_to_all | solution.py:21
  274.1 0.6 fusion.65
  274.7 0.7 fusion.64
  275.5 15.8 %all_to_all.74 = bf16[16,8,512]{2,1,0:T(8,128)(2,1)S(1)} all-to-all(bf16[16,8,512]{2,1,0:T(8,128)(2,1)S(1)} %broadcast_in_dim.185), channel_id=1, replica_groups=mesh['xh'=2,'core'=2,'xl'=2,'z'=16,'y'=4] {'z'}, dimensions={0} | all-to-all | bytes 262144 | tf_op jit(solution)/shard_map/all_to_all | solution.py:21
  291.3 0.6 fusion.67
  291.9 0.7 fusion.66
  292.7 15.8 %all_to_all.75 = bf16[16,8,512]{2,1,0:T(8,128)(2,1)S(1)} all-to-all(bf16[16,8,512]{2,1,0:T(8,128)(2,1)S(1)} %broadcast_in_dim.186), channel_id=1, replica_groups=mesh['xh'=2,'core'=2,'xl'=2,'z'=16,'y'=4] {'z'}, dimensions={0} | all-to-all | bytes 262144 | tf_op jit(solution)/shard_map/all_to_all | solution.py:21
  308.5 0.6 fusion.69
  309.1 0.7 fusion.68
  309.9 15.8 %all_to_all.76 = bf16[16,8,512]{2,1,0:T(8,128)(2,1)S(1)} all-to-all(bf16[16,8,512]{2,1,0:T(8,128)(2,1)S(1)} %broadcast_in_dim.187), channel_id=1, replica_groups=mesh['xh'=2,'core'=2,'xl'=2,'z'=16,'y'=4] {'z'}, dimensions={0} | all-to-all | bytes 262144 | tf_op jit(solution)/shard_map/all_to_all | solution.py:21
  326.4 0.7 fusion.70
  327.1 15.8 %all_to_all.77 = bf16[16,8,512]{2,1,0:T(8,128)(2,1)S(1)} all-to-all(bf16[16,8,512]{2,1,0:T(8,128)(2,1)S(1)} %broadcast_in_dim.188), channel_id=1, replica_groups=mesh['xh'=2,'core'=2,'xl'=2,'z'=16,'y'=4] {'z'}, dimensions={0} | all-to-all | bytes 262144 | tf_op jit(solution)/shard_map/all_to_all | solution.py:21
  342.9 0.6 fusion.73
  343.6 0.7 fusion.72
  344.4 0.7 broadcast_in_dim_broadcast_in_dim_broadcast_in_dim.2
  345.1 3.8 all-to-all-start.12
  348.9 11.5 %all-to-all-done.12 = f32[16,8,128]{2,1,0:T(8,128)S(1)} async-done(((f32[16,8,128]{2,1,0:T(8,128)}), f32[16,8,128]{2,1,0:T(8,128)S(1)}, u32[]{:S(2)}, u32[]{:S(2)}) %all-to-all-start.12) | async-done | bytes 65568 | tf_op jit(solution)/shard_map/all_to_all | solution.py:21
  360.6 25.4 %all_to_all.78 = bf16[32,8,384]{2,1,0:T(8,128)(2,1)S(1)} all-to-all(bf16[32,8,384]{2,1,0:T(8,128)(2,1)S(1)} %bitcast.202), channel_id=1, replica_groups=mesh['xh'=2,'core'=2,'xl'=2,'z'=16,'y'=4] {'xh','core','xl','y'}, dimensions={0} | all-to-all | bytes 393216 | tf_op jit(solution)/shard_map/all_to_all | solution.py:229
  387.1 0.7 fusion
  (87 shorter events, 6.6 us)
Async XLA Ops:
  0.6 1.3 copy-start
  0.6 49.8 %slice-start = ((f32[10,64,256]{2,1,0:T(8,128)}), f32[1,64,256]{2,1,0:T(8,128)S(1)}, s32[]{:S(2)}) async-start(f32[10,64,256]{2,1,0:T(8,128)} %param.9), calls=%async_computation.14 | async-start | bytes 131072 | tf_op jit(solution)/shard_map/slice | solution.py:114
  0.7 31.1 %copy-start.1 = (s32[256]{0:T(256)S(1)}, s32[256]{0:T(256)}, u32[]{:S(2)}) copy-start(s32[256]{0:T(256)} %param.11) | copy-start | bytes 3076
  0.7 31.2 %copy-start.5 = (s32[256]{0:T(256)S(1)}, s32[256]{0:T(256)}, u32[]{:S(2)}) copy-start(s32[256]{0:T(256)} %param.12) | copy-start | bytes 3076
  0.7 32.0 %copy-start.3 = (s32[256]{0:T(256)S(1)}, s32[256]{0:T(256)}, u32[]{:S(2)}) copy-start(s32[256]{0:T(256)} %param.10) | copy-start | bytes 3076
  1.9 31.4 %copy-start.2 = (f32[256]{0:T(256)S(1)}, f32[256]{0:T(256)}, u32[]{:S(2)}) copy-start(f32[256]{0:T(256)} %param.13) | copy-start | bytes 3076
  5.0 43.1 %all-to-all-start = ((bf16[32,2,2048]{2,1,0:T(2,128)(2,1)}), bf16[32,2,2048]{2,1,0:T(2,128)(2,1)S(1)}, u32[]{:S(2)}, u32[]{:S(2)}) async-start(bf16[32,2,2048]{2,1,0:T(2,128)(2,1)} %reshape.301), calls=%async_computation | async-start | bytes 524288 | tf_op jit(solution)/shard_map/all_to_all | solution.py:78
  22.0 27.3 %collective-permute-start = (bf16[16,64,256]{2,1,0:T(8,128)(2,1)S(1)}, bf16[16,64,256]{2,1,0:T(8,128)(2,1)S(1)}, u32[]{:S(2)}, u32[]{:S(2)}) collective-permute-start(bf16[16,64,256]{2,1,0:T(8,128)(2,1)S(1)} %dynamic-slice_bitcast_fusion.refs_0_), channel_id=1, source_target_pairs={{0,1},{1,2},{2,3},{3,0},{4,5},{5,6},{6,7},{7,4},{8,9},{9,10},{10,1... | collective-permute-start | bytes 1572872 | tf_op jit(solution)/shard_map/ppermute | solution.py:81
  25.2 24.1 %collective-permute-start.1 = (bf16[16,64,256]{2,1,0:T(8,128)(2,1)S(1)}, bf16[16,64,256]{2,1,0:T(8,128)(2,1)S(1)}, u32[]{:S(2)}, u32[]{:S(2)}) collective-permute-start(bf16[16,64,256]{2,1,0:T(8,128)(2,1)S(1)} %dynamic-slice_bitcast_fusion.refs_0_), channel_id=1, source_target_pairs={{0,3},{1,0},{2,1},{3,2},{4,7},{5,4},{6,5},{7,6},{8,11},{9,8},{10,9... | collective-permute-start | bytes 1572872 | tf_op jit(solution)/shard_map/ppermute | solution.py:81
  28.6 15.3 %collective-permute-start.2 = (bf16[16,64,256]{2,1,0:T(8,128)(2,1)S(1)}, bf16[16,64,256]{2,1,0:T(8,128)(2,1)S(1)}, u32[]{:S(2)}, u32[]{:S(2)}) collective-permute-start(bf16[16,64,256]{2,1,0:T(8,128)(2,1)S(1)} %dynamic-slice_bitcast_fusion.refs_0_), channel_id=1, source_target_pairs={{0,64},{64,0},{1,65},{65,1},{2,66},{66,2},{3,67},{67,3},{4,68},{68... | collective-permute-start | bytes 1572872 | tf_op jit(solution)/shard_map/ppermute | solution.py:84
  43.9 23.4 %collective-permute-start.4 = (bf16[16,64,256]{2,1,0:T(8,128)(2,1)S(1)}, bf16[16,64,256]{2,1,0:T(8,128)(2,1)}, u32[]{:S(2)}, u32[]{:S(2)}) collective-permute-start(bf16[16,64,256]{2,1,0:T(8,128)(2,1)S(1)} %collective-permute-done.2.refs_4_), channel_id=1, source_target_pairs={{0,3},{1,0},{2,1},{3,2},{4,7},{5,4},{6,5},{7,6},{8,11},{9,8},{10,9... | collective-permute-start | bytes 1572872 | tf_op jit(solution)/shard_map/ppermute | solution.py:81
  54.3 29.1 %all-to-all-start.1 = ((bf16[32,2,2048]{2,1,0:T(2,128)(2,1)}), bf16[32,2,2048]{2,1,0:T(2,128)(2,1)S(1)}, u32[]{:S(2)}, u32[]{:S(2)}) async-start(bf16[32,2,2048]{2,1,0:T(2,128)(2,1)} %reshape.303), calls=%async_computation.1 | async-start | bytes 524288 | tf_op jit(solution)/shard_map/all_to_all | solution.py:21
  65.4 19.3 %collective-permute-start.3 = (bf16[16,64,256]{2,1,0:T(8,128)(2,1)S(1)}, bf16[16,64,256]{2,1,0:T(8,128)(2,1)}, u32[]{:S(2)}, u32[]{:S(2)}) collective-permute-start(bf16[16,64,256]{2,1,0:T(8,128)(2,1)S(1)} %collective-permute-done.refs_1_), channel_id=1, source_target_pairs={{0,1},{1,2},{2,3},{3,0},{4,5},{5,6},{6,7},{7,4},{8,9},{9,10},{10,1... | collective-permute-start | bytes 1572872 | tf_op jit(solution)/shard_map/ppermute | solution.py:81
  67.3 17.3 %collective-permute-start.5 = (bf16[16,64,256]{2,1,0:T(8,128)(2,1)}, bf16[16,64,256]{2,1,0:T(8,128)(2,1)}, u32[]{:S(2)}, u32[]{:S(2)}) collective-permute-start(bf16[16,64,256]{2,1,0:T(8,128)(2,1)} %collective-permute-done.4.refs_6_), channel_id=1, source_target_pairs={{0,3},{1,0},{2,1},{3,2},{4,7},{5,4},{6,5},{7,6},{8,11},{9,8},{10,9... | collective-permute-start | bytes 1572872 | tf_op jit(solution)/shard_map/ppermute | solution.py:81
  71.9 18.7 %collective-permute-start.7 = (bf16[16,64,256]{2,1,0:T(8,128)(2,1)S(1)}, bf16[16,64,256]{2,1,0:T(8,128)(2,1)}, u32[]{:S(2)}, u32[]{:S(2)}) collective-permute-start(bf16[16,64,256]{2,1,0:T(8,128)(2,1)S(1)} %collective-permute-done.2.refs_4_), channel_id=1, source_target_pairs={{0,1},{1,2},{2,3},{3,0},{4,5},{5,6},{6,7},{7,4},{8,9},{9,10},{10,1... | collective-permute-start | bytes 1572872 | tf_op jit(solution)/shard_map/ppermute | solution.py:81
  155.4 42.5 %collective-permute-start.8 = (bf16[2,16,4,64,256]{4,3,2,1,0:T(8,128)(2,1)}, bf16[2,16,4,64,256]{4,3,2,1,0:T(8,128)(2,1)}, u32[]{:S(2)}, u32[]{:S(2)}) collective-permute-start(bf16[2,16,4,64,256]{4,3,2,1,0:T(8,128)(2,1)} %by_y.1.refs_0_), channel_id=1, source_target_pairs={{0,128},{128,0},{1,129},{129,1},{2,130},{130,2},{3,131},{131,3},{4... | collective-permute-start | bytes 12582920 | tf_op jit(solution)/shard_map/ppermute | solution.py:84
  163.8 8.6 %all-to-all-start.2 = ((f32[8,8,384]{2,1,0:T(8,128)}), f32[8,8,384]{2,1,0:T(8,128)S(1)}, u32[]{:S(2)}, u32[]{:S(2)}) async-start(f32[8,8,384]{2,1,0:T(8,128)} %maximum_bitcast_fusion), calls=%async_computation.2 | async-start | bytes 196608 | tf_op jit(solution)/shard_map/all_to_all | solution.py:128
  168.1 5.7 %collective-permute-start.6 = (f32[9,8,256]{2,1,0:T(8,128)S(1)}, f32[9,8,256]{2,1,0:T(8,128)S(1)}, u32[]{:S(2)}, u32[]{:S(2)}) collective-permute-start(f32[9,8,256]{2,1,0:T(8,128)S(1)} %get-tuple-element.45), channel_id=1, source_target_pairs={{0,64},{64,0},{1,65},{65,1},{2,66},{66,2},{3,67},{67,3},{4,68},{68... | collective-permute-start | bytes 221192 | tf_op jit(solution)/shard_map/ppermute | solution.py:84
  174.6 23.3 %all-to-all-start.3 = ((bf16[16,8,512]{2,1,0:T(8,128)(2,1)}), bf16[16,8,512]{2,1,0:T(8,128)(2,1)S(1)}, u32[]{:S(2)}, u32[]{:S(2)}) async-start(bf16[16,8,512]{2,1,0:T(8,128)(2,1)} %broadcast_in_dim.99), calls=%async_computation.3 | async-start | bytes 262144 | tf_op jit(solution)/shard_map/all_to_all | solution.py:21
  342.9 43.6 %copy-start.4 = (f32[64]{0:T(128)S(1)}, f32[64]{0:T(128)}, u32[]{:S(2)}) copy-start(f32[64]{0:T(128)} %sub.16) | copy-start | bytes 772
  345.1 15.3 %all-to-all-start.12 = ((f32[16,8,128]{2,1,0:T(8,128)}), f32[16,8,128]{2,1,0:T(8,128)S(1)}, u32[]{:S(2)}, u32[]{:S(2)}) async-start(f32[16,8,128]{2,1,0:T(8,128)} %broadcast_in_dim_broadcast_in_dim_broadcast_in_dim.2), calls=%async_computation.12 | async-start | bytes 131072 | tf_op jit(solution)/shard_map/all_to_all | solution.py:21

commit v5 on v3

v5 whole, which is shorter than its diff:
```python
import math

import jax
import jax.numpy as jnp
from jax import lax
from jax.experimental import pallas as pl
from jax.experimental.pallas import tpu as pltpu
from jax.sharding import Mesh, PartitionSpec as P

N = 8192
SWEEPS = 10
NEVER = -3.0e38

GROUP = ("xh", "core")
PLANE = ("xl", "y")
LAYER = ("xh", "core", "xl", "y")


def sent_to_all(value, axes):
    length = lax.axis_size(axes)
    return lax.all_to_all(
        jnp.broadcast_to(value[None], (length, *value.shape)), axes, 0, 0, tiled=True
    )


def in_spin_order(gathered):
    n_core, n_xl, n_y, n_z, piece, width = gathered.shape
    shape = (n_z, n_core * n_y, piece, n_xl * width)

    def body(source, target, sems):
        copies = [
            pltpu.make_async_copy(
                source.at[core, xl, y],
                target.at[:, core * n_y + y, :, pl.ds(xl * width, width)],
                sems.at[core, xl, y],
            )
            for xl in range(n_xl)
            for core in range(n_core)
            for y in range(n_y)
        ]
        for copy in copies:
            copy.start()
        for copy in copies:
            copy.wait()

    ordered = pl.pallas_call(
        body,
        in_specs=[pl.BlockSpec(memory_space=pltpu.HBM)],
        out_specs=pl.BlockSpec(memory_space=pl.ANY),
        out_shape=jax.ShapeDtypeStruct(shape, gathered.dtype),
        scratch_shapes=[pltpu.SemaphoreType.DMA((n_core, n_xl, n_y))],
        compiler_params=pltpu.CompilerParams(vmem_limit_bytes=2 * 1024 * 1024),
        name="in_spin_order",
    )(pltpu.with_memory_space_constraint(gathered, pltpu.HBM))
    return ordered.reshape(-1, n_xl * width)


def left_lanes(shape):
    return lax.broadcasted_iota(jnp.int32, shape, len(shape) - 1) < shape[-1] // 2


def packed(value):
    half = value.shape[0] // 2
    return jnp.concatenate([value[:half], value[half:]], axis=1)


def first_terms(spins, blocks, core, count):
    n_core, rows, width = blocks.shape
    half = spins.shape[0] // 2
    lanes = 2 * (n_core * rows // count)
    pairs = count // 2 // n_core

    def body(core_ref, spins_ref, blocks_ref, out_ref, half_ref, held_ref, sems):
        arrive = [
            pltpu.make_async_copy(blocks_ref.at[n], held_ref.at[n], sems.at[n])
            for n in range(n_core)
        ]
        for copy in arrive:
            copy.start()
        for copy in arrive:
            copy.wait()
        leave = pltpu.make_async_copy(held_ref.at[core_ref[0]], half_ref, sems.at[n_core])
        leave.start()
        is_left = left_lanes((half, lanes))
        for n in range(n_core):
            terms = lax.dot_general(
                spins_ref[...],
                held_ref[n],
                (((1,), (1,)), ((), ())),
                preferred_element_type=jnp.float32,
            )
            for pair in range(pairs):
                both = terms[:, pair * lanes : (pair + 1) * lanes]
                top, bottom = both[:half], both[half:]
                even = jnp.where(is_left, top, pltpu.roll(bottom, lanes // 2, 1))
                odd = jnp.where(is_left, pltpu.roll(top, lanes // 2, 1), bottom)
                at = 2 * (n * pairs + pair)
                out_ref[at] = even.astype(jnp.bfloat16)
                out_ref[at + 1] = odd.astype(jnp.bfloat16)
        leave.wait()

    return pl.pallas_call(
        body,
        in_specs=[
            pl.BlockSpec(memory_space=pltpu.SMEM),
            pl.BlockSpec(memory_space=pltpu.VMEM),
            pl.BlockSpec(memory_space=pl.ANY),
        ],
        out_specs=[pl.BlockSpec(memory_space=pltpu.VMEM), pl.BlockSpec(memory_space=pl.ANY)],
        out_shape=[
            jax.ShapeDtypeStruct((count, half, lanes), jnp.bfloat16),
            jax.ShapeDtypeStruct((rows, width), jnp.bfloat16),
        ],
        scratch_shapes=[
            pltpu.VMEM((n_core, rows, width), jnp.bfloat16),
            pltpu.SemaphoreType.DMA((n_core + 1,)),
        ],
        compiler_params=pltpu.CompilerParams(vmem_limit_bytes=16 * 1024 * 1024),
        name="first_terms",
    )(core[None], spins, pltpu.with_memory_space_constraint(blocks, pltpu.HBM))


def second_terms(rows, own_spins, block, parts):
    count, half, lanes = rows.shape
    width = block.shape[1]
    share = 2 * half // parts

    def body(rows_ref, own_ref, block_ref, out_ref, all_ref, held_ref, sem):
        arrive = pltpu.make_async_copy(block_ref, held_ref, sem)
        arrive.start()
        is_left = left_lanes((half, lanes))
        for pair in range(count // 2):
            even = rows_ref[2 * pair].astype(jnp.float32)
            odd = rows_ref[2 * pair + 1].astype(jnp.float32)
            top = jnp.where(is_left, even, pltpu.roll(odd, lanes // 2, 1))
            bottom = jnp.where(is_left, pltpu.roll(even, lanes // 2, 1), odd)
            at = pl.ds(pair * lanes, lanes)
            all_ref[0:half, at] = top.astype(jnp.bfloat16)
            all_ref[half : 2 * half, at] = bottom.astype(jnp.bfloat16)
        arrive.wait()
        terms = jnp.dot(all_ref[...], held_ref[...], preferred_element_type=jnp.float32)
        out_ref[:, :, 0:width] = terms.reshape(parts, share, width)
        own = own_ref[...]
        beside = pl.ds(width, lanes)
        out_ref[0 : parts // 2, :, beside] = own.reshape(parts // 2, share, lanes)
        own = pltpu.roll(own, lanes // 2, 1)
        out_ref[parts // 2 : parts, :, beside] = own.reshape(parts // 2, share, lanes)

    return pl.pallas_call(
        body,
        out_shape=jax.ShapeDtypeStruct((parts, share, width + lanes), jnp.float32),
        in_specs=[
            pl.BlockSpec(memory_space=pltpu.VMEM),
            pl.BlockSpec(memory_space=pltpu.VMEM),
            pl.BlockSpec(memory_space=pl.ANY),
        ],
        scratch_shapes=[
            pltpu.VMEM((2 * half, block.shape[0]), jnp.bfloat16),
            pltpu.VMEM(block.shape, jnp.bfloat16),
            pltpu.SemaphoreType.DMA,
        ],
        compiler_params=pltpu.CompilerParams(vmem_limit_bytes=16 * 1024 * 1024),
        name="second_terms",
    )(rows, own_spins, pltpu.with_memory_space_constraint(block, pltpu.HBM))


def per_device(spin_init, couplings, flip_noise, colors, beta_steps, partners, swap_noise):
    rep_dev, row_width = spin_init.shape
    n_xl = lax.axis_size("xl")
    n_y = lax.axis_size("y")
    n_z = lax.axis_size("z")
    n_core = lax.axis_size("core")
    y_index = lax.axis_index("y")
    xl_index = lax.axis_index("xl")
    core_index = lax.axis_index("core")
    rep_index = lax.axis_index(GROUP)
    share = rep_dev // (n_xl * n_y)
    piece = row_width // n_y
    width = n_xl * row_width
    own_block = couplings.reshape(-1, row_width)

    first_slot = rep_index * rep_dev

    def metropolis(spins, fields, limit, scale):
        energy_cost = scale * (spins * fields)
        return jnp.where(energy_cost < limit, -spins, spins)

    terms, core_half = first_terms(
        spin_init, own_block.reshape(n_core, -1, row_width), core_index, n_xl * n_z
    )
    gathered = lax.all_gather(core_half, ("core", *PLANE))
    terms = lax.all_to_all(terms, ("xl", "z"), 0, 0, tiled=True)
    all_betas = beta_steps.astype(jnp.float32)
    all_scales = all_betas * (1.0 / 16384.0)

    def scales(first, length):
        return lax.dynamic_slice_in_dim(all_scales, first, length)[:, None]

    slot_ids = first_slot + jnp.arange(rep_dev, dtype=jnp.int32)
    mate_ids = lax.dynamic_slice_in_dim(partners, first_slot, rep_dev)
    all_ids = jnp.arange(partners.shape[0], dtype=jnp.int32)[None, :]

    def picked(values, ids):
        return jnp.sum(jnp.where(ids[:, None] == all_ids, values[None, :], 0.0), axis=1)

    beta_gap = picked(all_betas, slot_ids) - picked(all_betas, mate_ids)
    noise = picked(swap_noise, jnp.minimum(slot_ids, mate_ids))
    mate_rows_of = (mate_ids[:, None] == all_ids).astype(jnp.bfloat16)

    def own_piece(value):
        return lax.dynamic_slice_in_dim(value, y_index * piece, piece, value.ndim - 1)

    limit = jnp.where(own_piece(colors)[None, :] == 0, own_piece(flip_noise[0]), NEVER)
    fields = terms.astype(jnp.float32).sum(axis=0)
    own_spins = packed(own_piece(spin_init)).astype(jnp.float32)
    own_scales = packed(jnp.broadcast_to(scales(first_slot, rep_dev), (rep_dev, piece)))
    own_spins = metropolis(own_spins, fields, packed(limit), own_scales)
    own_spins, late_noise, late_colors = lax.optimization_barrier(
        (own_spins, flip_noise, colors)
    )

    rows = sent_to_all(own_spins.astype(jnp.bfloat16), ("xl", "z"))

    def limits_of(xl):
        first = (xl * n_y + y_index) * share
        noise = lax.dynamic_slice_in_dim(late_noise, first, share, 1)
        return [
            jnp.where(late_colors[None, :] == step % 2, noise[step], NEVER)
            for step in range(1, SWEEPS)
        ]

    is_left = xl_index == 0
    kept = limits_of(xl_index)
    other = lax.ppermute(jnp.stack(limits_of(1 - xl_index)), "xl", [(0, 1), (1, 0)])
    limits = [
        jnp.concatenate(
            [jnp.where(is_left, here, there), jnp.where(is_left, there, here)], axis=1
        )
        for here, there in zip(kept, other)
    ]
    scale = scales(first_slot + lax.axis_index(PLANE) * share, share)

    partial = second_terms(rows, own_spins, own_block, n_xl * n_y)
    partial, limits, scale, beta_gap, noise, mate_rows_of = lax.optimization_barrier(
        (partial, limits, scale, beta_gap, noise, mate_rows_of)
    )
    partial = lax.all_to_all(partial, PLANE, 0, 0, tiled=True)
    fields = partial[:, :, :row_width].reshape(n_xl, n_y, share, row_width).sum(axis=1)
    fields = fields.transpose(1, 0, 2).reshape(share, width)
    spins = partial[:, :, row_width : row_width + piece]
    spins = spins.transpose(1, 0, 2).reshape(share, width)

    def layer_rows(spins):
        return sent_to_all(spins.astype(jnp.bfloat16), "z")

    def layer_fields(rows, layer_block):
        rows = rows.transpose(1, 0, 2).reshape(share, N)
        return jnp.dot(rows, layer_block, preferred_element_type=jnp.float32)

    spins = metropolis(spins, fields, limits[0], scale)
    spins = lax.optimization_barrier(spins)
    rows, gathered = lax.optimization_barrier((layer_rows(spins), gathered))
    layer_block = in_spin_order(
        gathered.reshape(n_core, n_xl, n_y, n_z, piece, row_width)
    )
    for limit in limits[1:]:
        spins = metropolis(spins, layer_fields(rows, layer_block), limit, scale)
        spins = lax.optimization_barrier(spins)
        rows = layer_rows(spins)

    layer_sum = jnp.sum(spins * layer_fields(rows, layer_block), axis=1, keepdims=True)
    layer_sum = jnp.broadcast_to(layer_sum, (share, 128))
    energy = -0.5 * sent_to_all(layer_sum, "z").sum(axis=0)

    high = lax.reduce_precision(energy, 8, 7)
    middle = lax.reduce_precision(energy - high, 8, 7)
    low = (energy - high) - middle
    terms = jnp.concatenate([high[:, :1], middle[:, :1], low[:, :126]], axis=1)
    blocks = spins.astype(jnp.bfloat16).reshape(share, n_xl, row_width).transpose(1, 0, 2)
    terms = jnp.broadcast_to(terms.astype(jnp.bfloat16)[None], (n_xl, share, 128))
    blocks = jnp.concatenate([blocks, terms], axis=2)
    blocks = jnp.broadcast_to(
        blocks[None, :, None], (lax.axis_size(GROUP), n_xl, n_y, *blocks.shape[1:])
    ).reshape(-1, *blocks.shape[1:])
    table = lax.all_to_all(blocks, LAYER, 0, 0, tiled=True).reshape(-1, row_width + 128)

    own_rows = lax.dynamic_slice_in_dim(table, first_slot, rep_dev, 0)
    own_rows = own_rows.astype(jnp.float32)
    mate_rows = jnp.dot(mate_rows_of, table, preferred_element_type=jnp.float32)

    def energy_of(rows):
        return rows[:, row_width] + (rows[:, row_width + 1] + rows[:, row_width + 2])

    own_energy = energy_of(own_rows)
    mate_energy = energy_of(mate_rows)
    swap_gain = beta_gap * (own_energy - mate_energy) * (1.0 / (64.0 * N * math.sqrt(N)))
    accept = swap_gain + noise > 0.0
    spins_out = jnp.where(
        accept[:, None], mate_rows[:, :row_width], own_rows[:, :row_width]
    )
    energies = jnp.where(accept, mate_energy, own_energy) * (1.0 / (N * math.sqrt(N)))
    return (spins_out.astype(jnp.bfloat16), energies)


def solution(mesh):
    fine = Mesh(mesh.devices.reshape(2, 2, 2, 16, 4), ("xh", "core", "xl", "z", "y"))
    rep, row, col = ("xh", "core"), ("xl", "z"), "y"
    in_specs = (
        P(rep, row),
        P(None, col, None, row),
        P(None, rep, row),
        P(row),
        P(),
        P(),
        P(),
    )
    out_specs = (P(rep, row), P(rep))
    return jax.shard_map(
        per_device, mesh=fine, in_specs=in_specs, out_specs=out_specs, check_vma=False
    )
```

time: 302 us -> 305 us (level)
  blocking collectives: 154 us -> 195 us
  waiting for transfers between devices: 62.7 us -> 31.7 us
  starting transfers between devices: 39.8 us -> 25.1 us
  other arithmetic: 4.16 us -> 14.7 us
  local copies, waits for them, and re-layouts: 8.62 us -> 4.13 us
  Pallas kernels: 3.51 us -> 7.91 us
    all_to_all x8 -> x10, blocking collectives: 126 us -> 157 us  [sent_to_all(): lax.all_to_all(jnp.broadcast_to(value[None], (length, *value.shape)), axe...]
    all_to_all x3 -> x1, waiting for transfers between devices: 38.2 us -> 17.6 us  [sent_to_all(): lax.all_to_all(jnp.broadcast_to(value[None], (length, *value.shape)), axe...]
    all_to_all x0 -> x1, blocking collectives: none -> 9.73 us  [per_device(): partial = lax.all_to_all(partial, PLANE, 0, 0, tiled=True)]
    all_to_all x3 -> x1, starting transfers between devices: 15.3 us -> 5.81 us  [sent_to_all(): lax.all_to_all(jnp.broadcast_to(value[None], (length, *value.shape)), axe...]
    unnamed x0 -> x8, other arithmetic: none -> 5.62 us
    all_to_all x1 -> x0, waiting for transfers between devices: 5.25 us -> none  [per_device(): lax.all_to_all(partial.reshape(n_xl * n_y, share, row_width + 128), PLANE...]
    all_to_all x1, waiting for transfers between devices: 19.2 us -> 14.1 us  [per_device(): terms = lax.all_to_all(terms, ('xl', 'z'), 0, 0, tiled=True)]
    all_to_all x1 -> x0, starting transfers between devices: 4.4 us -> none  [per_device(): lax.all_to_all(partial.reshape(n_xl * n_y, share, row_width + 128), PLANE...]
  transfers between devices with their start and end apart: 7 -> 4, of which waited for: 5 -> 2; matrix products, arithmetic and copies ran while one was open for 3% -> 5% of each run, Pallas kernels for 0% -> 1%
where the time goes in v5:
time: 305 us; the launch traced here: 304 us
  blocking collectives  195 us (64%)
  waiting for transfers between devices  31.7 us (10%)
  starting transfers between devices  25.1 us (8%)
  other arithmetic  14.7 us (5%)
  between operations  14.3 us (5%)
  matrix products  10.7 us (4%)
  Pallas kernels  7.91 us (3%)
  local copies, waits for them, and re-layouts  4.13 us (1%)
    all_to_all x10, blocking collectives, sent_to_all(): lax.all_to_all(jnp.broadcast_to(value[None], (length, *value.shape)), axe...  157 us
    all_to_all x1, blocking collectives, per_device(): lax.all_to_all(blocks, LAYER, 0, 0, tiled=True).reshape(-1, row_width + 128)  28.4 us
    all_to_all x1, waiting for transfers between devices, sent_to_all(): lax.all_to_all(jnp.broadcast_to(value[None], (length, *value.shape)), axe...  17.6 us
    all_to_all x1, starting transfers between devices, per_device(): terms = lax.all_to_all(terms, ('xl', 'z'), 0, 0, tiled=True)  17 us
    all_to_all x1, waiting for transfers between devices, per_device(): terms = lax.all_to_all(terms, ('xl', 'z'), 0, 0, tiled=True)  14.1 us
    dot_general x9, matrix products, layer_fields(): return jnp.dot(rows, layer_block, preferred_element_type=jnp.float32)  10.5 us
    all_to_all x1, blocking collectives, per_device(): partial = lax.all_to_all(partial, PLANE, 0, 0, tiled=True)  9.73 us
  transfers between devices with their start and end apart: 4, of which 2 were waited for; matrix products, arithmetic and copies ran while one was open for 5% of the time, Pallas kernels for 1%

profile of v5, /device:TPU:1, one launch (start us, length us, event | category | flops | bytes accessed | tf_op | source)
XLA Modules:
  0.0 303.9 jit_solution(7477418297155770709)
XLA Ops:
  7.2 0.7 copy-done
  8.0 2.8 first_terms.1
  10.8 17.0 %all-to-all-start = ((bf16[32,32,128]{2,1,0:T(8,128)(2,1)}), bf16[32,32,128]{2,1,0:T(8,128)(2,1)S(1)}, u32[]{:S(2)}, u32[]{:S(2)}) async-start(bf16[32,32,128]{2,1,0:T(8,128)(2,1)} %get-tuple-element.23), calls=%async_computation | async-start | bytes 524288 | tf_op jit(solution)/shard_map/all_to_all | solution.py:192
  27.8 0.7 convert_element_type.54
  28.5 0.8 fusion.63
  29.2 0.8 constant_dynamic-slice_fusion
  30.0 0.2 select_reduce_fusion.1
  30.2 0.7 broadcast_multiply_fusion
  30.9 0.8 dynamic-slice_compare_fusion
  31.6 0.1 dynamic_slice.29
  31.7 0.8 slice.124
  32.6 0.9 select_reduce_fusion
  33.5 0.1 fusion.26
  33.6 0.1 bitcast_select_fusion
  33.7 14.1 %all-to-all-done = bf16[32,32,128]{2,1,0:T(8,128)(2,1)S(1)} async-done(((bf16[32,32,128]{2,1,0:T(8,128)(2,1)}), bf16[32,32,128]{2,1,0:T(8,128)(2,1)S(1)}, u32[]{:S(2)}, u32[]{:S(2)}) %all-to-all-start) | async-done | bytes 262176 | tf_op jit(solution)/shard_map/all_to_all | solution.py:192
  48.0 0.1 negate_select_fusion.1.own_ref
  48.1 0.7 broadcast_compare_fusion
  48.7 0.7 constant_dynamic-update-slice_fusion.8
  49.4 0.7 constant_dynamic-update-slice_fusion.7
  50.1 0.7 constant_dynamic-update-slice_fusion.6
  50.8 0.7 constant_dynamic-update-slice_fusion.5
  51.5 0.7 constant_dynamic-update-slice_fusion.4
  52.3 0.7 constant_dynamic-update-slice_fusion.3
  53.0 0.7 constant_dynamic-update-slice_fusion.2
  53.7 0.7 constant_dynamic-update-slice_fusion.1
  54.4 0.7 constant_dynamic-update-slice_fusion
  55.1 2.3 collective-permute-start
  57.4 0.1 dynamic-slice_bitcast_fusion.9
  57.5 0.8 broadcast_in_dim.250
  58.2 5.8 %all-to-all-start.1 = ((bf16[32,32,128]{2,1,0:T(8,128)(2,1)}), bf16[32,32,128]{2,1,0:T(8,128)(2,1)S(1)}, u32[]{:S(2)}, u32[]{:S(2)}) async-start(bf16[32,32,128]{2,1,0:T(8,128)(2,1)} %broadcast_in_dim.250), calls=%async_computation.1 | async-start | bytes 524288 | tf_op jit(solution)/shard_map/all_to_all | solution.py:21
  64.1 0.8 fusion.59
  64.9 0.8 fusion.57
  65.7 17.6 %all-to-all-done.1.rows_ref = bf16[32,32,128]{2,1,0:T(8,128)(2,1)S(1)} async-done(((bf16[32,32,128]{2,1,0:T(8,128)(2,1)}), bf16[32,32,128]{2,1,0:T(8,128)(2,1)S(1)}, u32[]{:S(2)}, u32[]{:S(2)}) %all-to-all-start.1) | async-done | bytes 262176 | tf_op jit(solution)/shard_map/all_to_all | solution.py:21
  83.2 1.6 second_terms.1
  84.8 9.7 %all_to_all.70 = f32[8,8,384]{2,1,0:T(8,128)S(1)} all-to-all(f32[8,8,384]{2,1,0:T(8,128)S(1)} %second_terms.1), channel_id=1, replica_groups=mesh['xh'=2,'core'=2,'xl'=2,'z'=16,'y'=4] {'xl','y'}, dimensions={0} | all-to-all | bytes 196608 | tf_op jit(solution)/shard_map/all_to_all | solution.py:247
  94.6 0.1 reshape.160
  94.7 0.1 negate_select_fusion
  94.8 16.6 %all_to_all.71 = bf16[16,8,512]{2,1,0:T(8,128)(2,1)S(1)} all-to-all(bf16[16,8,512]{2,1,0:T(8,128)(2,1)S(1)} %broadcast_in_dim.261), channel_id=1, replica_groups=mesh['xh'=2,'core'=2,'xl'=2,'z'=16,'y'=4] {'z'}, dimensions={0} | all-to-all | bytes 262144 | tf_op jit(solution)/shard_map/all_to_all | solution.py:21
  111.3 3.5 %in_spin_order.1 = bf16[16,8,64,512]{3,2,1,0:T(8,128)(2,1)S(1)} custom-call(bf16[2,2,4,16,64,256]{5,4,3,2,1,0:T(8,128)(2,1)} %bitcast.209), custom_call_target="tpu_custom_call" | custom-call | tf_op jit(solution)/shard_map/in_spin_order/pallas_call | solution.py:46
  114.9 1.2 fusion.9
  116.1 15.8 %all_to_all.72 = bf16[16,8,512]{2,1,0:T(8,128)(2,1)S(1)} all-to-all(bf16[16,8,512]{2,1,0:T(8,128)(2,1)S(1)} %broadcast_in_dim.262), channel_id=1, replica_groups=mesh['xh'=2,'core'=2,'xl'=2,'z'=16,'y'=4] {'z'}, dimensions={0} | all-to-all | bytes 262144 | tf_op jit(solution)/shard_map/all_to_all | solution.py:21
  131.9 1.1 fusion.11
  133.1 15.9 %all_to_all.73 = bf16[16,8,512]{2,1,0:T(8,128)(2,1)S(1)} all-to-all(bf16[16,8,512]{2,1,0:T(8,128)(2,1)S(1)} %broadcast_in_dim.263), channel_id=1, replica_groups=mesh['xh'=2,'core'=2,'xl'=2,'z'=16,'y'=4] {'z'}, dimensions={0} | all-to-all | bytes 262144 | tf_op jit(solution)/shard_map/all_to_all | solution.py:21
  149.0 1.1 fusion.13
  150.2 15.8 %all_to_all.74 = bf16[16,8,512]{2,1,0:T(8,128)(2,1)S(1)} all-to-all(bf16[16,8,512]{2,1,0:T(8,128)(2,1)S(1)} %broadcast_in_dim.264), channel_id=1, replica_groups=mesh['xh'=2,'core'=2,'xl'=2,'z'=16,'y'=4] {'z'}, dimensions={0} | all-to-all | bytes 262144 | tf_op jit(solution)/shard_map/all_to_all | solution.py:21
  166.0 1.1 fusion.15
  167.2 15.8 %all_to_all.75 = bf16[16,8,512]{2,1,0:T(8,128)(2,1)S(1)} all-to-all(bf16[16,8,512]{2,1,0:T(8,128)(2,1)S(1)} %broadcast_in_dim.265), channel_id=1, replica_groups=mesh['xh'=2,'core'=2,'xl'=2,'z'=16,'y'=4] {'z'}, dimensions={0} | all-to-all | bytes 262144 | tf_op jit(solution)/shard_map/all_to_all | solution.py:21
  183.0 1.1 fusion.17
  184.3 15.7 %all_to_all.76 = bf16[16,8,512]{2,1,0:T(8,128)(2,1)S(1)} all-to-all(bf16[16,8,512]{2,1,0:T(8,128)(2,1)S(1)} %broadcast_in_dim.266), channel_id=1, replica_groups=mesh['xh'=2,'core'=2,'xl'=2,'z'=16,'y'=4] {'z'}, dimensions={0} | all-to-all | bytes 262144 | tf_op jit(solution)/shard_map/all_to_all | solution.py:21
  200.0 1.1 fusion.19
  201.2 15.5 %all_to_all.77 = bf16[16,8,512]{2,1,0:T(8,128)(2,1)S(1)} all-to-all(bf16[16,8,512]{2,1,0:T(8,128)(2,1)S(1)} %broadcast_in_dim.267), channel_id=1, replica_groups=mesh['xh'=2,'core'=2,'xl'=2,'z'=16,'y'=4] {'z'}, dimensions={0} | all-to-all | bytes 262144 | tf_op jit(solution)/shard_map/all_to_all | solution.py:21
  216.7 1.1 fusion.21
  217.9 15.5 %all_to_all.78 = bf16[16,8,512]{2,1,0:T(8,128)(2,1)S(1)} all-to-all(bf16[16,8,512]{2,1,0:T(8,128)(2,1)S(1)} %broadcast_in_dim.268), channel_id=1, replica_groups=mesh['xh'=2,'core'=2,'xl'=2,'z'=16,'y'=4] {'z'}, dimensions={0} | all-to-all | bytes 262144 | tf_op jit(solution)/shard_map/all_to_all | solution.py:21
  233.4 1.1 fusion.23
  234.6 15.6 %all_to_all.79 = bf16[16,8,512]{2,1,0:T(8,128)(2,1)S(1)} all-to-all(bf16[16,8,512]{2,1,0:T(8,128)(2,1)S(1)} %broadcast_in_dim.269), channel_id=1, replica_groups=mesh['xh'=2,'core'=2,'xl'=2,'z'=16,'y'=4] {'z'}, dimensions={0} | all-to-all | bytes 262144 | tf_op jit(solution)/shard_map/all_to_all | solution.py:21
  250.2 1.3 fusion.24
  251.6 15.2 %all_to_all.80 = f32[16,8,128]{2,1,0:T(8,128)S(1)} all-to-all(f32[16,8,128]{2,1,0:T(8,128)S(1)} %broadcast_in_dim_broadcast_in_dim_broadcast_in_dim.2), channel_id=1, replica_groups=mesh['xh'=2,'core'=2,'xl'=2,'z'=16,'y'=4] {'z'}, dimensions={0} | all-to-all | bytes 131072 | tf_op jit(solution)/shard_map/all_to_all | solution.py:21
  266.8 0.1 pad_maximum_fusion.10
  266.9 28.4 %all_to_all.81 = bf16[32,8,384]{2,1,0:T(8,128)(2,1)S(1)} all-to-all(bf16[32,8,384]{2,1,0:T(8,128)(2,1)S(1)} %bitcast.221), channel_id=1, replica_groups=mesh['xh'=2,'core'=2,'xl'=2,'z'=16,'y'=4] {'xh','core','xl','y'}, dimensions={0} | all-to-all | bytes 393216 | tf_op jit(solution)/shard_map/all_to_all | solution.py:285
  295.3 0.2 fusion.61
  295.5 0.2 fusion.28
  295.7 0.2 fusion.30
  295.9 0.5 select_multiply_fusion
  296.4 0.7 fusion.25
  (45 shorter events, 1.0 us)
Async XLA Ops:
  7.2 104.2 %all-gather.3.cloned.1.call-start = ((), (), s32[]{:S(2)}) async-start(), calls=%async_computation.14 | async-start | bytes 8912896 | tf_op jit(solution)/shard_map/all_gather | solution.py:191
  7.2 0.8 copy-start
  10.8 37.0 %all-to-all-start = ((bf16[32,32,128]{2,1,0:T(8,128)(2,1)}), bf16[32,32,128]{2,1,0:T(8,128)(2,1)S(1)}, u32[]{:S(2)}, u32[]{:S(2)}) async-start(bf16[32,32,128]{2,1,0:T(8,128)(2,1)} %get-tuple-element.23), calls=%async_computation | async-start | bytes 524288 | tf_op jit(solution)/shard_map/all_to_all | solution.py:192
  55.1 9.0 %collective-permute-start = (f32[9,8,256]{2,1,0:T(8,128)S(1)}, f32[9,8,256]{2,1,0:T(8,128)S(1)}, u32[]{:S(2)}, u32[]{:S(2)}) collective-permute-start(f32[9,8,256]{2,1,0:T(8,128)S(1)} %constant_dynamic-update-slice_fusion), channel_id=1, source_target_pairs={{0,64},{64,0},{1,65},{65,1},{2,66},{66,2},{3,67},{67,3},{4,68},{68... | collective-permute-start | bytes 221192 | tf_op jit(solution)/shard_map/ppermute | solution.py:234
  58.2 25.0 %all-to-all-start.1 = ((bf16[32,32,128]{2,1,0:T(8,128)(2,1)}), bf16[32,32,128]{2,1,0:T(8,128)(2,1)S(1)}, u32[]{:S(2)}, u32[]{:S(2)}) async-start(bf16[32,32,128]{2,1,0:T(8,128)(2,1)} %broadcast_in_dim.250), calls=%async_computation.1 | async-start | bytes 524288 | tf_op jit(solution)/shard_map/all_to_all | solution.py:21
Sparse Core Ops, SparseCore 0:
  10.9 71.6 all-gather.2

commit v6 on v5

--- a/solution.py
+++ b/solution.py
@@ -215,29 +215,25 @@
     own_spins = packed(own_piece(spin_init)).astype(jnp.float32)
     own_scales = packed(jnp.broadcast_to(scales(first_slot, rep_dev), (rep_dev, piece)))
     own_spins = metropolis(own_spins, fields, packed(limit), own_scales)
-    own_spins, late_noise, late_colors = lax.optimization_barrier(
-        (own_spins, flip_noise, colors)
-    )
+    own_spins = lax.optimization_barrier(own_spins)
 
     rows = sent_to_all(own_spins.astype(jnp.bfloat16), ("xl", "z"))
+
+    steps = jnp.arange(1, SWEEPS, dtype=jnp.int32)[:, None, None]
 
     def limits_of(xl):
         first = (xl * n_y + y_index) * share
-        noise = lax.dynamic_slice_in_dim(late_noise, first, share, 1)
-        return [
-            jnp.where(late_colors[None, :] == step % 2, noise[step], NEVER)
-            for step in range(1, SWEEPS)
-        ]
+        noise = lax.dynamic_slice_in_dim(flip_noise, first, share, 1)[1:]
+        return jnp.where(colors[None, None, :] == steps % 2, noise, NEVER)
 
     is_left = xl_index == 0
     kept = limits_of(xl_index)
-    other = lax.ppermute(jnp.stack(limits_of(1 - xl_index)), "xl", [(0, 1), (1, 0)])
-    limits = [
-        jnp.concatenate(
-            [jnp.where(is_left, here, there), jnp.where(is_left, there, here)], axis=1
-        )
-        for here, there in zip(kept, other)
-    ]
+    other = limits_of(1 - xl_index)
+    other = lax.ppermute(other, "xl", [(0, 1), (1, 0)])
+    limits = jnp.concatenate(
+        [jnp.where(is_left, kept, other), jnp.where(is_left, other, kept)], axis=2
+    )
+    limits = [limits[step] for step in range(SWEEPS - 1)]
     scale = scales(first_slot + lax.axis_index(PLANE) * share, share)
 
     partial = second_terms(rows, own_spins, own_block, n_xl * n_y)

time: 305 us -> 299 us (0.980)
  other arithmetic: 14.7 us -> 8.67 us
    unnamed x8 -> x0, other arithmetic: 5.62 us -> none
  transfers between devices with their start and end apart: 4 -> 4, of which waited for: 2 -> 2; matrix products, arithmetic and copies ran while one was open for 5% -> 3% of each run, Pallas kernels for 1% -> 1%
where the time goes in v6:
time: 299 us; the launch traced here: 298 us
  blocking collectives  197 us (66%)
  waiting for transfers between devices  31.1 us (10%)
  starting transfers between devices  24.4 us (8%)
  between operations  14.3 us (5%)
  matrix products  10.7 us (4%)
  other arithmetic  8.67 us (3%)
  Pallas kernels  7.91 us (3%)
  local copies, waits for them, and re-layouts  4.13 us (1%)
    all_to_all x10, blocking collectives, sent_to_all(): lax.all_to_all(jnp.broadcast_to(value[None], (length, *value.shape)), axe...  159 us
    all_to_all x1, blocking collectives, per_device(): lax.all_to_all(blocks, LAYER, 0, 0, tiled=True).reshape(-1, row_width + 128)  28.7 us
    all_to_all x1, waiting for transfers between devices, per_device(): terms = lax.all_to_all(terms, ('xl', 'z'), 0, 0, tiled=True)  15.7 us
    all_to_all x1, waiting for transfers between devices, sent_to_all(): lax.all_to_all(jnp.broadcast_to(value[None], (length, *value.shape)), axe...  15.4 us
    all_to_all x1, starting transfers between devices, per_device(): terms = lax.all_to_all(terms, ('xl', 'z'), 0, 0, tiled=True)  15.2 us
    dot_general x9, matrix products, layer_fields(): return jnp.dot(rows, layer_block, preferred_element_type=jnp.float32)  10.5 us
    all_to_all x1, blocking collectives, per_device(): partial = lax.all_to_all(partial, PLANE, 0, 0, tiled=True)  9.53 us
  transfers between devices with their start and end apart: 4, of which 2 were waited for; matrix products, arithmetic and copies ran while one was open for 3% of the time, Pallas kernels for 1%

profile of v6, /device:TPU:1, one launch (start us, length us, event | category | flops | bytes accessed | tf_op | source)
XLA Modules:
  0.0 298.0 jit_solution(566687207251100231)
XLA Ops:
  7.2 0.7 copy-done
  8.0 2.8 first_terms.1
  10.8 0.8 broadcast_compare_fusion
  11.6 0.9 dynamic-slice_select_fusion
  12.5 3.9 %collective-permute-start = (f32[9,8,256]{2,1,0:T(8,128)S(1)}, f32[9,8,256]{2,1,0:T(8,128)S(1)}, u32[]{:S(2)}, u32[]{:S(2)}) collective-permute-start(f32[9,8,256]{2,1,0:T(8,128)S(1)} %dynamic-slice_select_fusion), channel_id=1, source_target_pairs={{0,64},{64,0},{1,65},{65,1},{2,66},{66,2},{3,67},{67,3},{4,68},{68... | collective-permute-start | bytes 221192 | tf_op jit(solution)/shard_map/ppermute | solution.py:232
  16.4 15.2 %all-to-all-start = ((bf16[32,32,128]{2,1,0:T(8,128)(2,1)}), bf16[32,32,128]{2,1,0:T(8,128)(2,1)S(1)}, u32[]{:S(2)}, u32[]{:S(2)}) async-start(bf16[32,32,128]{2,1,0:T(8,128)(2,1)} %get-tuple-element.20), calls=%async_computation | async-start | bytes 524288 | tf_op jit(solution)/shard_map/all_to_all | solution.py:192
  31.7 0.8 slice.103
  32.5 0.7 convert_element_type.54
  33.2 0.7 broadcast_multiply_fusion
  33.9 0.1 dynamic_slice.29
  34.0 0.8 dynamic-slice_compare_fusion
  34.7 0.8 constant_dynamic-slice_fusion
  35.5 0.1 fusion.58
  35.6 0.1 bitcast_select_fusion
  35.7 15.7 %all-to-all-done = bf16[32,32,128]{2,1,0:T(8,128)(2,1)S(1)} async-done(((bf16[32,32,128]{2,1,0:T(8,128)(2,1)}), bf16[32,32,128]{2,1,0:T(8,128)(2,1)S(1)}, u32[]{:S(2)}, u32[]{:S(2)}) %all-to-all-start) | async-done | bytes 262176 | tf_op jit(solution)/shard_map/all_to_all | solution.py:192
  51.5 0.1 broadcast_in_dim.87
  51.5 0.1 broadcast_in_dim.88
  51.6 0.1 negate_select_fusion.1.own_ref
  51.7 0.8 broadcast_in_dim.92
  52.5 5.2 %all-to-all-start.1 = ((bf16[32,32,128]{2,1,0:T(8,128)(2,1)}), bf16[32,32,128]{2,1,0:T(8,128)(2,1)S(1)}, u32[]{:S(2)}, u32[]{:S(2)}) async-start(bf16[32,32,128]{2,1,0:T(8,128)(2,1)} %broadcast_in_dim.92), calls=%async_computation.1 | async-start | bytes 524288 | tf_op jit(solution)/shard_map/all_to_all | solution.py:21
  57.7 0.8 fusion.56
  58.5 0.2 select_reduce_fusion.1
  58.7 0.9 select_reduce_fusion
  59.5 0.1 fusion.26
  59.6 0.1 dynamic-slice_bitcast_fusion
  59.7 0.9 fusion.27
  60.6 15.4 %all-to-all-done.1.rows_ref = bf16[32,32,128]{2,1,0:T(8,128)(2,1)S(1)} async-done(((bf16[32,32,128]{2,1,0:T(8,128)(2,1)}), bf16[32,32,128]{2,1,0:T(8,128)(2,1)S(1)}, u32[]{:S(2)}, u32[]{:S(2)}) %all-to-all-start.1) | async-done | bytes 262176 | tf_op jit(solution)/shard_map/all_to_all | solution.py:21
  76.0 1.6 second_terms.1
  77.6 9.5 %all_to_all.70 = f32[8,8,384]{2,1,0:T(8,128)S(1)} all-to-all(f32[8,8,384]{2,1,0:T(8,128)S(1)} %second_terms.1), channel_id=1, replica_groups=mesh['xh'=2,'core'=2,'xl'=2,'z'=16,'y'=4] {'xl','y'}, dimensions={0} | all-to-all | bytes 196608 | tf_op jit(solution)/shard_map/all_to_all | solution.py:243
  87.2 0.1 reshape.160
  87.2 0.1 negate_select_fusion
  87.3 17.8 %all_to_all.71 = bf16[16,8,512]{2,1,0:T(8,128)(2,1)S(1)} all-to-all(bf16[16,8,512]{2,1,0:T(8,128)(2,1)S(1)} %broadcast_in_dim.170), channel_id=1, replica_groups=mesh['xh'=2,'core'=2,'xl'=2,'z'=16,'y'=4] {'z'}, dimensions={0} | all-to-all | bytes 262144 | tf_op jit(solution)/shard_map/all_to_all | solution.py:21
  105.2 3.5 %in_spin_order.1 = bf16[16,8,64,512]{3,2,1,0:T(8,128)(2,1)S(1)} custom-call(bf16[2,2,4,16,64,256]{5,4,3,2,1,0:T(8,128)(2,1)} %bitcast.101), custom_call_target="tpu_custom_call" | custom-call | tf_op jit(solution)/shard_map/in_spin_order/pallas_call | solution.py:46
  108.7 1.2 fusion.9
  109.9 0.1 broadcast_in_dim.171
  109.9 15.8 %all_to_all.72 = bf16[16,8,512]{2,1,0:T(8,128)(2,1)S(1)} all-to-all(bf16[16,8,512]{2,1,0:T(8,128)(2,1)S(1)} %broadcast_in_dim.171), channel_id=1, replica_groups=mesh['xh'=2,'core'=2,'xl'=2,'z'=16,'y'=4] {'z'}, dimensions={0} | all-to-all | bytes 262144 | tf_op jit(solution)/shard_map/all_to_all | solution.py:21
  125.7 1.1 fusion.11
  126.9 15.8 %all_to_all.73 = bf16[16,8,512]{2,1,0:T(8,128)(2,1)S(1)} all-to-all(bf16[16,8,512]{2,1,0:T(8,128)(2,1)S(1)} %broadcast_in_dim.172), channel_id=1, replica_groups=mesh['xh'=2,'core'=2,'xl'=2,'z'=16,'y'=4] {'z'}, dimensions={0} | all-to-all | bytes 262144 | tf_op jit(solution)/shard_map/all_to_all | solution.py:21
  142.8 1.1 fusion.13
  143.9 0.1 broadcast_in_dim.173
  144.0 15.8 %all_to_all.74 = bf16[16,8,512]{2,1,0:T(8,128)(2,1)S(1)} all-to-all(bf16[16,8,512]{2,1,0:T(8,128)(2,1)S(1)} %broadcast_in_dim.173), channel_id=1, replica_groups=mesh['xh'=2,'core'=2,'xl'=2,'z'=16,'y'=4] {'z'}, dimensions={0} | all-to-all | bytes 262144 | tf_op jit(solution)/shard_map/all_to_all | solution.py:21
  159.9 1.1 fusion.15
  161.1 15.8 %all_to_all.75 = bf16[16,8,512]{2,1,0:T(8,128)(2,1)S(1)} all-to-all(bf16[16,8,512]{2,1,0:T(8,128)(2,1)S(1)} %broadcast_in_dim.174), channel_id=1, replica_groups=mesh['xh'=2,'core'=2,'xl'=2,'z'=16,'y'=4] {'z'}, dimensions={0} | all-to-all | bytes 262144 | tf_op jit(solution)/shard_map/all_to_all | solution.py:21
  176.9 1.1 fusion.17
  178.0 0.1 broadcast_in_dim.175
  178.1 15.7 %all_to_all.76 = bf16[16,8,512]{2,1,0:T(8,128)(2,1)S(1)} all-to-all(bf16[16,8,512]{2,1,0:T(8,128)(2,1)S(1)} %broadcast_in_dim.175), channel_id=1, replica_groups=mesh['xh'=2,'core'=2,'xl'=2,'z'=16,'y'=4] {'z'}, dimensions={0} | all-to-all | bytes 262144 | tf_op jit(solution)/shard_map/all_to_all | solution.py:21
  193.8 1.1 fusion.19
  195.0 0.1 broadcast_in_dim.176
  195.0 15.5 %all_to_all.77 = bf16[16,8,512]{2,1,0:T(8,128)(2,1)S(1)} all-to-all(bf16[16,8,512]{2,1,0:T(8,128)(2,1)S(1)} %broadcast_in_dim.176), channel_id=1, replica_groups=mesh['xh'=2,'core'=2,'xl'=2,'z'=16,'y'=4] {'z'}, dimensions={0} | all-to-all | bytes 262144 | tf_op jit(solution)/shard_map/all_to_all | solution.py:21
  210.5 1.1 fusion.21
  211.7 0.1 broadcast_in_dim.177
  211.8 15.5 %all_to_all.78 = bf16[16,8,512]{2,1,0:T(8,128)(2,1)S(1)} all-to-all(bf16[16,8,512]{2,1,0:T(8,128)(2,1)S(1)} %broadcast_in_dim.177), channel_id=1, replica_groups=mesh['xh'=2,'core'=2,'xl'=2,'z'=16,'y'=4] {'z'}, dimensions={0} | all-to-all | bytes 262144 | tf_op jit(solution)/shard_map/all_to_all | solution.py:21
  227.3 1.1 fusion.23
  228.5 15.6 %all_to_all.79 = bf16[16,8,512]{2,1,0:T(8,128)(2,1)S(1)} all-to-all(bf16[16,8,512]{2,1,0:T(8,128)(2,1)S(1)} %broadcast_in_dim.178), channel_id=1, replica_groups=mesh['xh'=2,'core'=2,'xl'=2,'z'=16,'y'=4] {'z'}, dimensions={0} | all-to-all | bytes 262144 | tf_op jit(solution)/shard_map/all_to_all | solution.py:21
  244.1 1.3 fusion.24
  245.4 0.1 broadcast_in_dim_broadcast_in_dim_broadcast_in_dim.2
  245.5 15.1 %all_to_all.80 = f32[16,8,128]{2,1,0:T(8,128)S(1)} all-to-all(f32[16,8,128]{2,1,0:T(8,128)S(1)} %broadcast_in_dim_broadcast_in_dim_broadcast_in_dim.2), channel_id=1, replica_groups=mesh['xh'=2,'core'=2,'xl'=2,'z'=16,'y'=4] {'z'}, dimensions={0} | all-to-all | bytes 131072 | tf_op jit(solution)/shard_map/all_to_all | solution.py:21
  260.6 0.1 pad_maximum_fusion.2
  260.7 28.7 %all_to_all.81 = bf16[32,8,384]{2,1,0:T(8,128)(2,1)S(1)} all-to-all(bf16[32,8,384]{2,1,0:T(8,128)(2,1)S(1)} %bitcast.113), channel_id=1, replica_groups=mesh['xh'=2,'core'=2,'xl'=2,'z'=16,'y'=4] {'xh','core','xl','y'}, dimensions={0} | all-to-all | bytes 393216 | tf_op jit(solution)/shard_map/all_to_all | solution.py:281
  289.4 0.2 fusion.54
  289.6 0.2 fusion.30
  289.8 0.2 fusion.32
  290.0 0.5 select_multiply_fusion
  290.5 0.7 fusion.25
  (33 shorter events, 0.5 us)
Async XLA Ops:
  7.2 98.0 %all-gather.3.cloned.1.call-start = ((), (), s32[]{:S(2)}) async-start(), calls=%async_computation.14 | async-start | bytes 8912896 | tf_op jit(solution)/shard_map/all_gather | solution.py:191
  7.2 0.8 copy-start
  12.5 47.2 %collective-permute-start = (f32[9,8,256]{2,1,0:T(8,128)S(1)}, f32[9,8,256]{2,1,0:T(8,128)S(1)}, u32[]{:S(2)}, u32[]{:S(2)}) collective-permute-start(f32[9,8,256]{2,1,0:T(8,128)S(1)} %dynamic-slice_select_fusion), channel_id=1, source_target_pairs={{0,64},{64,0},{1,65},{65,1},{2,66},{66,2},{3,67},{67,3},{4,68},{68... | collective-permute-start | bytes 221192 | tf_op jit(solution)/shard_map/ppermute | solution.py:232
  16.4 35.0 %all-to-all-start = ((bf16[32,32,128]{2,1,0:T(8,128)(2,1)}), bf16[32,32,128]{2,1,0:T(8,128)(2,1)S(1)}, u32[]{:S(2)}, u32[]{:S(2)}) async-start(bf16[32,32,128]{2,1,0:T(8,128)(2,1)} %get-tuple-element.20), calls=%async_computation | async-start | bytes 524288 | tf_op jit(solution)/shard_map/all_to_all | solution.py:192
  52.5 23.5 %all-to-all-start.1 = ((bf16[32,32,128]{2,1,0:T(8,128)(2,1)}), bf16[32,32,128]{2,1,0:T(8,128)(2,1)S(1)}, u32[]{:S(2)}, u32[]{:S(2)}) async-start(bf16[32,32,128]{2,1,0:T(8,128)(2,1)} %broadcast_in_dim.92), calls=%async_computation.1 | async-start | bytes 524288 | tf_op jit(solution)/shard_map/all_to_all | solution.py:21
Sparse Core Ops, SparseCore 0:
  10.9 70.7 all-gather.2
